TPU v7x, 128 devices: a whole 4x4x4 slice. The times are simulated.
128 devices in a mesh: sp: 4 (over x), fsdp: 32 (over z, y, core).
Axes of the slice: x: 4, y: 4, z: 4, core: 2. Of those that a mesh axis runs over, the one named last changes fastest.
Arguments:
- x: bfloat16 [32, 512, 4096], P('fsdp', 'sp')
- grad_y: bfloat16 [32, 512, 4096], P('fsdp', 'sp')
- w_q: bfloat16 [4096, 4096], P('fsdp')
- w_k: bfloat16 [4096, 4096], P('fsdp')
- w_v: bfloat16 [4096, 4096], P('fsdp')
- w_o: bfloat16 [4096, 4096], P('fsdp')
- q_norm_w: float32 [4096], P('fsdp')
- k_norm_w: float32 [4096], P('fsdp')
- post_norm_w: float32 [4096], P('fsdp')
Outputs:
- output 1: bfloat16 [32, 512, 4096], P('fsdp', 'sp')
- output 2: bfloat16 [32, 512, 4096], P('fsdp', 'sp')
- output 3: float32 [4096, 4096], P('fsdp')
- output 4: float32 [4096, 4096], P('fsdp')
- output 5: float32 [4096, 4096], P('fsdp')
- output 6: float32 [4096, 4096], P('fsdp')
- output 7: float32 [4096], P('fsdp')
- output 8: float32 [4096], P('fsdp')
- output 9: float32 [4096], P('fsdp')
All inputs are finite; a program needn't handle non-finite values.
Results may differ from a plain program's by a relative error of at most 0.02.
Values are sent between devices in bfloat16 or wider.
A program may use at most 1 GiB of HBM per device.

v0:
```python
import jax
import jax.numpy as jnp
from jax import lax
from jax.sharding import PartitionSpec as P, NamedSharding

HEAD_DIM = 128
RMS_EPSILON = 1e-6
ROPE_THETA = 500000.0


def rope_angles(positions):
    half_dim = HEAD_DIM // 2
    inv_freq = ROPE_THETA ** (-jnp.arange(half_dim, dtype=jnp.float32) * (2.0 / HEAD_DIM))
    angles = positions.astype(jnp.float32)[:, None] * inv_freq[None, :]
    return jnp.cos(angles)[:, None, :], jnp.sin(angles)[:, None, :]


def rope_apply(heads_in, cos_tab, sin_tab):
    half_dim = HEAD_DIM // 2
    first_half = heads_in[..., :half_dim]
    second_half = heads_in[..., half_dim:]
    return jnp.concatenate([first_half * cos_tab - second_half * sin_tab, second_half * cos_tab + first_half * sin_tab], axis=-1)


def causal_attention(q_rot, k_rot, v_heads):
    seq_len = q_rot.shape[1]
    scores = jnp.einsum('bqhd,bkhd->bhqk', q_rot, k_rot, preferred_element_type=jnp.float32) * (HEAD_DIM ** -0.5)
    causal = jnp.arange(seq_len)[:, None] >= jnp.arange(seq_len)[None, :]
    attn_probs = jax.nn.softmax(jnp.where(causal, scores, -1e30), axis=-1).astype(jnp.bfloat16)
    return jnp.einsum('bhqk,bkhd->bqhd', attn_probs, v_heads, preferred_element_type=jnp.float32).astype(jnp.bfloat16)


def rms_forward(values, gain_vec):
    inv_rms = lax.rsqrt(jnp.mean(values * values, axis=-1, keepdims=True) + RMS_EPSILON)
    normed = values * inv_rms
    return normed * gain_vec, normed, inv_rms


def rms_backward(grad_out, normed, inv_rms, gain_vec):
    grad_hat = grad_out * gain_vec
    grad_in = inv_rms * (grad_hat - normed * jnp.mean(grad_hat * normed, axis=-1, keepdims=True))
    gain_grad = jnp.sum(grad_out * normed, axis=(0, 1))
    return grad_in, gain_grad


def solution(mesh):
    sp_size = mesh.shape['sp']
    tok_spec = P('fsdp', 'sp', None)
    row_spec = P('fsdp', None)
    vec_spec = P('fsdp')

    def local_step(x, grad_y, wq_rows, wk_rows, wv_rows, wo_rows, gq_rows, gk_rows, gpost_rows):
        n_batch, tok_len, model_width = x.shape
        n_heads = model_width // HEAD_DIM
        local_heads = n_heads // sp_size
        local_width = local_heads * HEAD_DIM
        seq_len = tok_len * sp_size
        head_start = lax.axis_index('sp') * local_width

        def to_heads(blocks):
            return lax.all_to_all(blocks.reshape(n_batch, tok_len, n_heads, HEAD_DIM), 'sp', 2, 1, tiled=True)

        def to_tokens(blocks):
            return lax.all_to_all(blocks, 'sp', 1, 2, tiled=True).reshape(n_batch, tok_len, model_width)

        def reduce_rows(grad_part):
            return lax.psum(lax.psum_scatter(grad_part, 'fsdp', scatter_dimension=0, tiled=True), 'sp')

        w_q = lax.all_gather(wq_rows, 'fsdp', axis=0, tiled=True)
        w_k = lax.all_gather(wk_rows, 'fsdp', axis=0, tiled=True)
        w_v = lax.all_gather(wv_rows, 'fsdp', axis=0, tiled=True)
        w_o = lax.all_gather(wo_rows, 'fsdp', axis=0, tiled=True)
        gain_q = lax.all_gather(gq_rows, 'fsdp', axis=0, tiled=True)
        gain_k = lax.all_gather(gk_rows, 'fsdp', axis=0, tiled=True)
        gain_post = lax.all_gather(gpost_rows, 'fsdp', axis=0, tiled=True)
        gain_q_local = lax.dynamic_slice_in_dim(gain_q, head_start, local_width).reshape(local_heads, HEAD_DIM)
        gain_k_local = lax.dynamic_slice_in_dim(gain_k, head_start, local_width).reshape(local_heads, HEAD_DIM)

        q_heads = to_heads(jnp.dot(x, w_q, preferred_element_type=jnp.float32).astype(jnp.bfloat16)).astype(jnp.float32)
        k_heads = to_heads(jnp.dot(x, w_k, preferred_element_type=jnp.float32).astype(jnp.bfloat16)).astype(jnp.float32)
        v_heads = to_heads(jnp.dot(x, w_v, preferred_element_type=jnp.float32).astype(jnp.bfloat16))
        q_sumsq, k_sumsq = lax.psum((jnp.sum(q_heads * q_heads, axis=(2, 3)), jnp.sum(k_heads * k_heads, axis=(2, 3))), 'sp')
        q_inv = lax.rsqrt(q_sumsq / model_width + RMS_EPSILON)[:, :, None, None]
        k_inv = lax.rsqrt(k_sumsq / model_width + RMS_EPSILON)[:, :, None, None]
        q_hat = q_heads * q_inv
        k_hat = k_heads * k_inv
        cos_tab, sin_tab = rope_angles(jnp.arange(seq_len))
        q_rot = rope_apply(q_hat * gain_q_local, cos_tab, sin_tab).astype(jnp.bfloat16)
        k_rot = rope_apply(k_hat * gain_k_local, cos_tab, sin_tab).astype(jnp.bfloat16)
        attn_heads, attn_pull = jax.vjp(causal_attention, q_rot, k_rot, v_heads)
        attn_tok = to_tokens(attn_heads)
        a_lin = jnp.dot(attn_tok, w_o, preferred_element_type=jnp.float32).astype(jnp.bfloat16)
        post_out, a_hat, a_inv = rms_forward(a_lin.astype(jnp.float32), gain_post)
        y = (x.astype(jnp.float32) + post_out).astype(jnp.bfloat16)

        grad_y_float = grad_y.astype(jnp.float32)
        grad_a, post_part = rms_backward(grad_y_float, a_hat, a_inv, gain_post)
        grad_a = grad_a.astype(jnp.bfloat16)
        wo_part = jnp.einsum('btd,bte->de', attn_tok, grad_a, preferred_element_type=jnp.float32)
        grad_attn = jnp.einsum('bte,de->btd', grad_a, w_o, preferred_element_type=jnp.float32).astype(jnp.bfloat16)
        grad_q_rot, grad_k_rot, grad_v_heads = attn_pull(to_heads(grad_attn))
        grad_q_norm = rope_apply(grad_q_rot.astype(jnp.float32), cos_tab, -sin_tab)
        grad_k_norm = rope_apply(grad_k_rot.astype(jnp.float32), cos_tab, -sin_tab)
        gain_q_part = jnp.sum(grad_q_norm * q_hat, axis=(0, 1)).reshape(local_width)
        gain_k_part = jnp.sum(grad_k_norm * k_hat, axis=(0, 1)).reshape(local_width)
        grad_q_hat = grad_q_norm * gain_q_local
        grad_k_hat = grad_k_norm * gain_k_local
        q_proj, k_proj = lax.psum((jnp.sum(grad_q_hat * q_hat, axis=(2, 3)), jnp.sum(grad_k_hat * k_hat, axis=(2, 3))), 'sp')
        grad_q_lin = (q_inv * (grad_q_hat - q_hat * (q_proj / model_width)[:, :, None, None])).astype(jnp.bfloat16)
        grad_k_lin = (k_inv * (grad_k_hat - k_hat * (k_proj / model_width)[:, :, None, None])).astype(jnp.bfloat16)
        grad_q_tok = to_tokens(grad_q_lin)
        grad_k_tok = to_tokens(grad_k_lin)
        grad_v_tok = to_tokens(grad_v_heads)
        grad_x = (grad_y_float
                  + jnp.einsum('bte,de->btd', grad_q_tok, w_q, preferred_element_type=jnp.float32)
                  + jnp.einsum('bte,de->btd', grad_k_tok, w_k, preferred_element_type=jnp.float32)
                  + jnp.einsum('bte,de->btd', grad_v_tok, w_v, preferred_element_type=jnp.float32)).astype(jnp.bfloat16)
        wq_part = jnp.einsum('btd,bte->de', x, grad_q_tok, preferred_element_type=jnp.float32)
        wk_part = jnp.einsum('btd,bte->de', x, grad_k_tok, preferred_element_type=jnp.float32)
        wv_part = jnp.einsum('btd,bte->de', x, grad_v_tok, preferred_element_type=jnp.float32)
        gain_q_full = lax.all_gather(gain_q_part, 'sp', axis=0, tiled=True)
        gain_k_full = lax.all_gather(gain_k_part, 'sp', axis=0, tiled=True)
        return (y, grad_x, reduce_rows(wq_part), reduce_rows(wk_part), reduce_rows(wv_part), reduce_rows(wo_part),
                lax.psum_scatter(gain_q_full, 'fsdp', scatter_dimension=0, tiled=True),
                lax.psum_scatter(gain_k_full, 'fsdp', scatter_dimension=0, tiled=True),
                reduce_rows(post_part))

    return jax.shard_map(local_step, mesh=mesh,
                         in_specs=(tok_spec, tok_spec, row_spec, row_spec, row_spec, row_spec, vec_spec, vec_spec, vec_spec),
                         out_specs=(tok_spec, tok_spec, row_spec, row_spec, row_spec, row_spec, vec_spec, vec_spec, vec_spec),
                         check_vma=False)
```

profile of v0, /device:TPU:1, one launch (start us, length us, event | category | flops | bytes accessed | tf_op | source)
XLA Modules:
  0.0 1870.6 jit_solution(4532238743336086794)
XLA Ops:
  10.0 27.2 %all-gather = f32[32,1,128]{2,1,0:T(1,128)S(1)} all-gather(f32[1,1,128]{2,1,0:T(1,128)S(1)} %bitcast.260), channel_id=1, replica_groups=mesh['sp'=4,'fsdp'=32] {'fsdp'}, dimensions={0}, use_global_device_ids=true | all-gather | bytes 16896 | tf_op jit(solution)/shard_map/all_gather | solution.py:73
  37.2 23.8 %all-gather.1 = f32[32,1,128]{2,1,0:T(1,128)S(1)} all-gather(f32[1,1,128]{2,1,0:T(1,128)S(1)} %bitcast.261), channel_id=1, replica_groups=mesh['sp'=4,'fsdp'=32] {'fsdp'}, dimensions={0}, use_global_device_ids=true | all-gather | bytes 16896 | tf_op jit(solution)/shard_map/all_gather | solution.py:74
  61.0 66.6 %all-gather.8.cloned.1.call-done = bf16[4096,4096]{1,0:T(8,128)(2,1)} async-done(((bf16[128,4096]{1,0:T(8,128)(2,1)}), bf16[4096,4096]{1,0:T(8,128)(2,1)}) %all-gather.8.cloned.1.call-update) | async-done | bytes 33554448 | tf_op jit(solution)/shard_map/all_gather | solution.py:71
  127.5 13.0 fusion.37
  146.2 96.3 %all-gather.10.cloned.1.call-done = bf16[4096,4096]{1,0:T(8,128)(2,1)} async-done(((bf16[128,4096]{1,0:T(8,128)(2,1)}), bf16[4096,4096]{1,0:T(8,128)(2,1)}) %all-gather.10.cloned.1.call-update) | async-done | bytes 33554448 | tf_op jit(solution)/shard_map/all_gather | solution.py:69
  242.5 13.0 fusion.38
  262.1 95.3 %all-gather.12.cloned.1.call-done = bf16[4096,4096]{1,0:T(8,128)(2,1)} async-done(((bf16[128,4096]{1,0:T(8,128)(2,1)}), bf16[4096,4096]{1,0:T(8,128)(2,1)}) %all-gather.12.cloned.1.call-update) | async-done | bytes 33554448 | tf_op jit(solution)/shard_map/all_gather | solution.py:70
  357.4 13.0 fusion.39
  405.8 9.6 fusion.61
  427.9 28.0 %all-gather.2 = f32[32,1,128]{2,1,0:T(1,128)S(1)} all-gather(f32[1,1,128]{2,1,0:T(1,128)S(1)} %bitcast.262), channel_id=1, replica_groups=mesh['sp'=4,'fsdp'=32] {'fsdp'}, dimensions={0}, use_global_device_ids=true | all-gather | bytes 16896 | tf_op jit(solution)/shard_map/all_gather | solution.py:75
  456.7 15.8 all-gather.14.cloned.1.call-done
  472.5 13.1 multiply_reduce_fusion.4
  488.3 23.9 %fusion.62 = f32[4096,4096]{1,0:T(8,128)} fusion(bf16[128,4096]{0,1:T(8,128)(2,1)S(1)} %bitcast.225, bf16[128,4096]{1,0:T(8,128)(2,1)S(1)} %get-tuple-element.71), kind=kOutput, calls=%fused_computation.124 | convolution fusion | flops 4294967296 | bytes 69206016 | tf_op jit(solution)/shard_map/btd,bte->de/dot_general | solution.py:99
  512.2 16.0 fusion.40
  535.3 13.0 all-to-all-done.4
  573.6 9.1 all_gather.34
  583.6 8.9 all_gather.35
  592.5 127.4 %all-reduce.3 = (f32[4096]{0:T(1024)S(1)}, f32[4096]{0:T(1024)S(1)}, f32[4096]{0:T(1024)S(1)}) all-reduce(f32[4096]{0:T(1024)S(1)} %all_gather.34, f32[4096]{0:T(1024)S(1)} %all_gather.35, f32[4096]{0:T(1024)S(1)} %get-tuple-element.49), channel_id=6, replica_groups=mesh['sp'=4,'fsdp'=32] {'fsdp'}, use_global_device_ids=true, to_apply=%region_22.23.clone | all-reduce | flops 12288 | bytes 98304
  720.1 8.6 all-reduce.4
  732.3 12.2 all_to_all.111
  745.3 23.9 %convolution_bitcast_fusion.2 = f32[4096,4096]{0,1:T(8,128)} fusion(bf16[128,4096]{0,1:T(8,128)(2,1)S(1)} %bitcast.222, bf16[1,128,4096]{2,1,0:T(8,128)(2,1)S(1)} %copy-done), kind=kOutput, calls=%fused_computation.3 | convolution fusion | flops 4294967296 | bytes 69206016 | tf_op jit(solution)/shard_map/btd,bte->de/dot_general | solution.py:118
  774.5 12.2 all_to_all.112
  787.4 23.9 %convolution_bitcast_fusion.1 = f32[4096,4096]{0,1:T(8,128)} fusion(bf16[128,4096]{0,1:T(8,128)(2,1)S(1)} %bitcast.226, bf16[1,128,4096]{2,1,0:T(8,128)(2,1)S(1)} %copy-done), kind=kOutput, calls=%fused_computation.2 | convolution fusion | flops 4294967296 | bytes 69206016 | tf_op jit(solution)/shard_map/btd,bte->de/dot_general | solution.py:119
  818.9 13.0 all_to_all.113
  833.7 23.9 %convolution_bitcast_fusion = f32[4096,4096]{0,1:T(8,128)} fusion(bf16[128,4096]{0,1:T(8,128)(2,1)S(1)} %bitcast.228, bf16[1,128,4096]{2,1,0:T(8,128)(2,1)S(1)} %copy-done), kind=kOutput, calls=%fused_computation.1 | convolution fusion | flops 4294967296 | bytes 69206016 | tf_op jit(solution)/shard_map/btd,bte->de/dot_general | solution.py:120
  857.7 242.4 %reduce-scatter.5.cloned.1.call-done = f32[128,4096]{0,1:T(8,128)} async-done(((f32[4096,4096]{0,1:T(8,128)}), f32[128,4096]{0,1:T(8,128)}) %reduce-scatter.5.cloned.1.call-update) | async-done | bytes 2097168 | tf_op jit(solution)/shard_map/reduce_scatter | solution.py:67
  1100.2 296.1 %reduce-scatter.7.cloned.1.call-done = f32[128,4096]{0,1:T(8,128)} async-done(((f32[4096,4096]{0,1:T(8,128)}), f32[128,4096]{0,1:T(8,128)}) %reduce-scatter.7.cloned.1.call-update) | async-done | bytes 2097168 | tf_op jit(solution)/shard_map/reduce_scatter | solution.py:67
  1396.2 296.0 %reduce-scatter.9.cloned.1.call-done = f32[128,4096]{0,1:T(8,128)} async-done(((f32[4096,4096]{0,1:T(8,128)}), f32[128,4096]{0,1:T(8,128)}) %reduce-scatter.9.cloned.1.call-update) | async-done | bytes 2097168 | tf_op jit(solution)/shard_map/reduce_scatter | solution.py:67
  1693.5 17.3 convolution_bitcast_fusion.3
  1710.7 17.4 convolution_bitcast_fusion.4
  1728.2 18.5 fusion.11
  1746.7 107.7 %all-reduce.9.cloned.1.call-done = (f32[128,4096]{0,1:T(8,128)}, f32[128,4096]{0,1:T(8,128)}, f32[128,4096]{0,1:T(8,128)}, f32[128,4096]{1,0:T(8,128)}) async-done(((f32[128,4096]{0,1:T(8,128)}, f32[128,4096]{0,1:T(8,128)}, f32[128,4096]{0,1:T(8,128)}, f32[128,4096]{1,0:T(8,128)}), (f32[128,4096]{0,1:T(8,128)}, f32[128,4096]{0,1:T(8,128)}, f32[128,4096]{0,1:T(8,128)}, ...) | async-done | bytes 8388624 | tf_op jit(solution)/shard_map/psum | solution.py:67
  (171 shorter events, 128.8 us)
Async XLA Ops:
  7.2 30.0 %copy-start.35 = (f32[128]{0:T(128)S(1)}, f32[128]{0:T(128)}, u32[]{:S(2)}) copy-start(f32[128]{0:T(128)} %param.16) | copy-start | bytes 1540
  7.2 120.3 %copy-start = (bf16[1,128,4096]{2,1,0:T(8,128)(2,1)S(1)}, bf16[1,128,4096]{2,1,0:T(8,128)(2,1)}, u32[]{:S(2)}) copy-start(bf16[1,128,4096]{2,1,0:T(8,128)(2,1)} %param.9) | copy-start | bytes 3145732
  7.2 120.3 %all-gather.8.cloned.1.call-start = ((), (), s32[]{:S(2)}) async-start(), calls=%async_computation.12 | async-start | bytes 34603008 | tf_op jit(solution)/shard_map/all_gather | solution.py:71
  7.9 234.5 %all-gather.10.cloned.1.call-start = ((), (), s32[]{:S(2)}) async-start(), calls=%async_computation.13 | async-start | bytes 34603008 | tf_op jit(solution)/shard_map/all_gather | solution.py:69
  8.7 348.7 %all-gather.12.cloned.1.call-start = ((), (), s32[]{:S(2)}) async-start(), calls=%async_computation.14 | async-start | bytes 34603008 | tf_op jit(solution)/shard_map/all_gather | solution.py:70
  9.4 463.0 %all-gather.14.cloned.1.call-start = ((), (), s32[]{:S(2)}) async-start(), calls=%async_computation.15 | async-start | bytes 34603008 | tf_op jit(solution)/shard_map/all_gather | solution.py:72
  142.2 114.9 %all-to-all-start = ((bf16[1,128,32,128]{3,1,0,2:T(8,128)(2,1)}), bf16[1,128,32,128]{3,1,0,2:T(8,128)(2,1)S(1)}, u32[]{:S(2)}, u32[]{:S(2)}) async-start(bf16[1,128,32,128]{3,1,0,2:T(8,128)(2,1)} %copy.78), calls=%async_computation | async-start | bytes 2097152 | tf_op jit(solution)/shard_map/all_to_all | solution.py:61
  258.1 114.0 %all-to-all-start.1 = ((bf16[1,128,32,128]{3,1,0,2:T(8,128)(2,1)}), bf16[1,128,32,128]{3,1,0,2:T(8,128)(2,1)S(1)}, u32[]{:S(2)}, u32[]{:S(2)}) async-start(bf16[1,128,32,128]{3,1,0,2:T(8,128)(2,1)} %copy.80), calls=%async_computation.1 | async-start | bytes 2097152 | tf_op jit(solution)/shard_map/all_to_all | solution.py:61
  372.1 11.5 copy-start.9
  372.1 18.6 all-to-all-start.2
  393.3 9.7 copy-start.2
  405.8 9.6 copy-start.27
  405.8 9.6 copy-start.29
  424.3 31.6 %all-to-all-start.3 = ((bf16[1,512,8,128]{3,2,0,1:T(8,128)(2,1)}), bf16[1,512,8,128]{3,2,0,1:T(8,128)(2,1)S(1)}, u32[]{:S(2)}, u32[]{:S(2)}) async-start(bf16[1,512,8,128]{3,2,0,1:T(8,128)(2,1)} %copy.85), calls=%async_computation.3 | async-start | bytes 2097152 | tf_op jit(solution)/shard_map/all_to_all | solution.py:64
  427.8 429.9 %reduce-scatter.11.cloned.1.call-start = ((), (), s32[]{:S(2)}) async-start(), calls=%async_computation.19 | async-start | bytes 69206016 | tf_op jit(solution)/shard_map/reduce_scatter | solution.py:67
  472.5 13.1 copy-start.21
  529.9 18.4 all-to-all-start.4
  533.9 566.3 %reduce-scatter.5.cloned.1.call-start = ((), (), s32[]{:S(2)}) async-start(), calls=%async_computation.16 | async-start | bytes 69206016 | tf_op jit(solution)/shard_map/reduce_scatter | solution.py:67
  551.2 7.2 copy-start.19
  551.2 13.8 slice-start
  572.5 10.1 copy-start.5
  572.5 10.1 copy-start.6
  572.6 11.0 copy-start.7
  572.6 11.0 copy-start.8
  572.6 10.0 copy-start.14
  582.6 146.0 %copy-start.4 = (f32[1,128,4,8,128]{4,1,2,3,0:T(8,128)S(1)}, f32[1,128,4,8,128]{4,1,2,3,0:T(8,128)}, u32[]{:S(2)}) copy-start(f32[1,128,4,8,128]{4,1,2,3,0:T(8,128)} %copy.81) | copy-start | bytes 6291460
  745.3 23.9 %copy-start.15 = (bf16[1,128,4,8,128]{1,4,3,2,0:T(8,128)(2,1)}, bf16[1,128,4,8,128]{1,4,3,2,0:T(8,128)(2,1)S(1)}, u32[]{:S(2)}) copy-start(bf16[1,128,4,8,128]{1,4,3,2,0:T(8,128)(2,1)S(1)} %copy.94) | copy-start | bytes 3145732
  769.2 627.0 %reduce-scatter.7.cloned.1.call-start = ((), (), s32[]{:S(2)}) async-start(), calls=%async_computation.17 | async-start | bytes 69206016 | tf_op jit(solution)/shard_map/reduce_scatter | solution.py:67
  811.4 880.9 %reduce-scatter.9.cloned.1.call-start = ((), (), s32[]{:S(2)}) async-start(), calls=%async_computation.18 | async-start | bytes 69206016 | tf_op jit(solution)/shard_map/reduce_scatter | solution.py:67
  857.7 996.8 %all-reduce.9.cloned.1.call-start = ((), (), s32[]{:S(2)}) async-start(), calls=%async_computation.20 | async-start | bytes 16777216 | tf_op jit(solution)/shard_map/psum | solution.py:67
  1710.7 17.4 copy-start.16
  1710.7 17.4 copy-start.22
  (22 other events, 83.4 us)
Sparse Core Ops, SparseCore 0:
  10.3 117.2 all-gather.7
  129.8 112.6 all-gather.9
  244.7 112.6 all-gather.11
  359.6 112.8 all-gather.13
  512.4 291.8 reduce-scatter.10
  808.2 291.9 reduce-scatter.4
  1104.2 291.9 reduce-scatter.6
  1400.2 291.9 reduce-scatter.8
  1694.9 159.4 all-reduce.8
where the time goes:
time: 1880 us; the launch traced here: 1870 us
  waiting for transfers between devices  1240 us (66%)
  blocking collectives  277 us (15%)
  matrix products  251 us (13%)
  local copies, waits for them, and re-layouts  43.6 us (2%)
  other arithmetic  25.5 us (1%)
  starting transfers between devices  20.1 us (1%)
    reduce_scatter x4, waiting for transfers between devices, reduce_rows(): lax.psum_scatter(grad_part, 'fsdp', scatter_dimension=0, tiled=True)  835 us
    unnamed x1, blocking collectives  127 us
    psum x1, waiting for transfers between devices, reduce_rows(): lax.psum(lax.psum_scatter(grad_part, 'fsdp', scatter_dimension=0, tiled=T...  108 us
    all_gather x1, waiting for transfers between devices, local_step(): w_q = lax.all_gather(wq_rows, 'fsdp', axis=0, tiled=True)  96.3 us
    all_gather x1, waiting for transfers between devices, local_step(): w_k = lax.all_gather(wk_rows, 'fsdp', axis=0, tiled=True)  95.3 us
    all_gather x1, waiting for transfers between devices, local_step(): w_v = lax.all_gather(wv_rows, 'fsdp', axis=0, tiled=True)  66.6 us
  transfers between devices with their start and end apart: 14, of which 10 were waited for; matrix products, arithmetic and copies ran while one was open for 14% of the time, Pallas kernels for 0%

commit v1 on v0

v1 whole, which is shorter than its diff:
```python
import jax
import jax.numpy as jnp
from jax import lax
from jax.experimental import pallas as pl
from jax.experimental.pallas import tpu as pltpu
from jax.sharding import Mesh, PartitionSpec as P

HEAD_DIM = 128
RMS_EPSILON = 1e-6
ROPE_THETA = 500000.0
FS = ('z', 'y', 'c')
F32 = jnp.float32
BF16 = jnp.bfloat16
MESH_ID = pl.DeviceIdType.MESH
HBM = pl.ANY
SEG = 256
NM = 4


def grads_kernel(*refs):
    parts = refs[:NM]
    gx_part, gy = refs[NM:NM + 2]
    outs = refs[NM + 2:2 * NM + 2]
    gx_out = refs[2 * NM + 2]
    (r1, r2, loc, rg, gloc, s1s, s1r, s2s, s2r, ags, agr, d2s, d2r, fws, fwr, lws, lsem, gs, gr, gsem) = refs[2 * NM + 3:]
    x, z, y, c = (lax.axis_index(n) for n in ('sp', 'z', 'y', 'c'))

    def mod4(v):
        return lax.rem(v + 8, 4)

    p1 = (1 - c) * y + c * z
    p2 = (1 - c) * z + c * y
    dirs = (1, -1)

    def axis1(d):
        return (x, mod4(z + d * c), mod4(y + d * (1 - c)), c)

    def axis2(d):
        return (x, mod4(z + d * (1 - c)), mod4(y + d * c), c)

    def xdev(d, core):
        return (mod4(x + d), z, y, core)

    partner = (x, z, y, 1 - c)
    peers = [axis1(1), axis1(-1), axis2(1), axis2(-1), xdev(1, c), xdev(-1, c), xdev(1, 1 - c), xdev(-1, 1 - c), partner]
    barrier = pltpu.get_barrier_semaphore()
    for peer in peers:
        pl.semaphore_signal(barrier, inc=1, device_id=peer, device_id_type=MESH_ID)
    pl.semaphore_wait(barrier, len(peers))

    def seg_rows(b, j):
        zz = (1 - c) * j + c * b
        yy = (1 - c) * b + c * j
        return pl.ds(pl.multiple_of(zz * 1024 + yy * SEG, SEG), SEG)

    def remote(src, dst, ss, rs, dev):
        return pltpu.make_async_remote_copy(src_ref=src, dst_ref=dst, send_sem=ss, recv_sem=rs, device_id=dev, device_id_type=MESH_ID)

    def send1(m, t, kk, jj):
        d = dirs[kk]
        if t == 0:
            rows = seg_rows(mod4(p1 - d), mod4(p2 - d * (1 + jj)))
            src = parts[m].at[rows, pl.ds(kk * SEG, SEG)]
        else:
            src = r1.at[m, kk, t - 1, jj]
        return remote(src, r1.at[m, kk, t, jj], s1s.at[m, kk, t, jj], s1r.at[m, kk, t, jj], axis1(d))

    def load(m, t, kk, jj):
        d = dirs[kk]
        par = (3 * m + t) % 2
        rows = seg_rows(mod4(p1 - d * (2 + t)), mod4(p2 - d * (1 + jj)))
        return pltpu.make_async_copy(parts[m].at[rows, pl.ds(kk * SEG, SEG)], loc.at[par, kk, jj], lsem.at[par, kk, jj])

    def send2(m, u, kk):
        return remote(r1.at[m, kk, 2, u], r2.at[m, kk, u], s2s.at[m, kk, u], s2r.at[m, kk, u], axis2(dirs[kk]))

    def out_cols(k, xs):
        return pl.ds(pl.multiple_of(k * 1024 + xs * SEG, SEG), SEG)

    def ag_send(m, kk, di, h):
        k = 2 * c + kk
        return remote(r1.at[m, kk, 2, 3, pl.ds(h * 128, 128)], outs[m].at[:, out_cols(k, x)], ags.at[m, kk, di, h], agr.at[m, di, k], xdev(dirs[di], h))

    def ag_recv(m, di, k):
        cols = out_cols(k, mod4(x - dirs[di]))
        return remote(outs[m].at[:, cols], outs[m].at[:, cols], ags.at[m, 0, di, 0], agr.at[m, di, k], xdev(dirs[di], c))

    def pair_send(m, kk):
        k = 2 * c + kk
        rows = pl.ds(pl.multiple_of((1 - c) * 128, 128), 128)
        return remote(r1.at[m, kk, 2, 3, rows], outs[m].at[:, out_cols(k, x)], d2s.at[m, kk], d2r.at[m, kk], partner)

    def own_store(m, kk):
        k = 2 * c + kk
        rows = pl.ds(pl.multiple_of(c * 128, 128), 128)
        return pltpu.make_async_copy(r1.at[m, kk, 2, 3, rows], outs[m].at[:, out_cols(k, x)], lws.at[m, kk])

    def forward(m, k):
        di = k % 2
        cols = out_cols(k, mod4(x - dirs[di]))
        return remote(outs[m].at[:, cols], outs[m].at[:, cols], fws.at[m, k], fwr.at[m, k], xdev(dirs[di], c))

    def gcols(kk, jj):
        return pl.ds(pl.multiple_of(kk * 2048 + jj * 512, 512), 512)

    def gsend(t, kk, jj):
        d = dirs[kk]
        if t == 0:
            src = gx_part.at[pl.ds(pl.multiple_of(mod4(x - d) * 128, 128), 128), gcols(kk, jj)]
        else:
            src = rg.at[kk, t - 1, jj]
        return remote(src, rg.at[kk, t, jj], gs.at[kk, t, jj], gr.at[kk, t, jj], xdev(d, c))

    def gload(t, kk, jj):
        rows = pl.ds(pl.multiple_of(mod4(x - dirs[kk] * (2 + t)) * 128, 128), 128)
        return pltpu.make_async_copy(gx_part.at[rows, gcols(kk, jj)], gloc.at[t % 2, kk, jj], gsem.at[t % 2, kk, jj])

    def each(fn):
        def step(jj, carry):
            for kk in range(2):
                fn(kk, jj)
            return carry
        lax.fori_loop(0, 4, step, 0)

    each(lambda kk, jj: send1(0, 0, kk, jj).start())
    each(lambda kk, jj: load(0, 0, kk, jj).start())
    each(lambda kk, jj: gsend(0, kk, jj).start())
    each(lambda kk, jj: gload(0, kk, jj).start())

    def phase2(m, u):
        for kk in range(2):
            send2(m, u - 1, kk).wait_recv()
            r1[m, kk, 2, u] = r1[m, kk, 2, u] + r2[m, kk, u - 1]
            if u < 3:
                send2(m, u, kk).start()
            else:
                own_store(m, kk).start()
                for di in range(2):
                    for h in range(2):
                        ag_send(m, kk, di, h).start()
                pair_send(m, kk).start()

    def do_forward(m):
        for k in range(4):
            ag_recv(m, k % 2, k).wait_recv()
            forward(m, k).start()

    def gx_step(t):
        if t < 2:
            each(lambda kk, jj: gload(t + 1, kk, jj).start())

        def item(kk, jj):
            gsend(t, kk, jj).wait_recv()
            gload(t, kk, jj).wait()
            total = rg[kk, t, jj] + gloc[t % 2, kk, jj]
            if t < 2:
                rg[kk, t, jj] = total
                gsend(t + 1, kk, jj).start()
            else:
                gx_out[:, gcols(kk, jj)] = (total + gy[:, gcols(kk, jj)].astype(F32)).astype(BF16)
        each(item)

    last = 3 * NM
    for r in range(last):
        m, t = divmod(r, 3)
        if r + 1 < last:
            mn, tn = divmod(r + 1, 3)
            each(lambda kk, jj: load(mn, tn, kk, jj).start())

        def item(kk, jj):
            send1(m, t, kk, jj).wait_recv()
            load(m, t, kk, jj).wait()
            r1[m, kk, t, jj] = r1[m, kk, t, jj] + loc[r % 2, kk, jj]
            if t < 2:
                send1(m, t + 1, kk, jj).start()
            elif m + 1 < NM:
                send1(m + 1, 0, kk, jj).start()

        each(item)
        if t == 2:
            for kk in range(2):
                send2(m, 0, kk).start()
        if m > 0 and t == 0:
            phase2(m - 1, 1)
        if m > 0 and t == 1:
            phase2(m - 1, 2)
        if m > 0 and t == 2:
            phase2(m - 1, 3)
        if m > 1 and t == 0:
            do_forward(m - 2)
        if r in (2, 4, 6):
            gx_step((r - 2) // 2)
    for u in (1, 2, 3):
        phase2(NM - 1, u)
    if NM > 1:
        do_forward(NM - 2)
    do_forward(NM - 1)

    for m in range(NM):
        for t in range(3):
            each(lambda kk, jj: send1(m, t, kk, jj).wait_send())
        for kk in range(2):
            for u in range(3):
                send2(m, u, kk).wait_send()
            for di in range(2):
                for h in range(2):
                    ag_send(m, kk, di, h).wait_send()
            pair_send(m, kk).wait()
            own_store(m, kk).wait()
        for k in range(4):
            ag_recv(m, 1 - k % 2, k).wait_recv()
            forward(m, k).wait()
    for t in range(3):
        each(lambda kk, jj: gsend(t, kk, jj).wait_send())


def reduce_grads(parts, gx_part, gy):
    nm = len(parts)
    dma = pltpu.SemaphoreType.DMA
    vmem = pl.BlockSpec(memory_space=pltpu.VMEM)
    hbm = pl.BlockSpec(memory_space=HBM)
    return pl.pallas_call(
        grads_kernel,
        out_shape=[jax.ShapeDtypeStruct((128, 4096), F32)] * nm + [jax.ShapeDtypeStruct((128, 4096), BF16)],
        in_specs=[hbm] * (nm + 1) + [vmem],
        out_specs=[hbm] * nm + [vmem],
        scratch_shapes=[
            pltpu.VMEM((nm, 2, 3, 4, SEG, SEG), F32),
            pltpu.VMEM((nm, 2, 3, SEG, SEG), F32),
            pltpu.VMEM((2, 2, 4, SEG, SEG), F32),
            pltpu.VMEM((2, 3, 4, 128, 512), F32),
            pltpu.VMEM((2, 2, 4, 128, 512), F32),
            dma((nm, 2, 3, 4)), dma((nm, 2, 3, 4)),
            dma((nm, 2, 3)), dma((nm, 2, 3)),
            dma((nm, 2, 2, 2)), dma((nm, 2, 4)),
            dma((nm, 2)), dma((nm, 2)),
            dma((nm, 4)), dma((nm, 4)),
            dma((nm, 2)), dma((2, 2, 4)),
            dma((2, 3, 4)), dma((2, 3, 4)), dma((2, 2, 4)),
        ],
        compiler_params=pltpu.CompilerParams(collective_id=4, has_side_effects=True, vmem_limit_bytes=60 * 1024 * 1024),
        cost_estimate=pl.CostEstimate(flops=10 ** 11, bytes_accessed=10 ** 8, transcendentals=0),
        name='reduce_grads',
    )(*parts, gx_part, gy)


def gather_kernel(*refs):
    nw = 3
    w_in = refs[:nw]
    x_in, gy_in = refs[nw:nw + 2]
    w_out = refs[nw + 2:2 * nw + 2]
    qkv = refs[2 * nw + 2:3 * nw + 2]
    x_full, gy_cols, stats = refs[3 * nw + 2:3 * nw + 5]
    (w, sq, st, ld, d0s, d0r, a1s, a1r, a2s, a2r, f3s, f3r, xls, xs, xr, xfs, xfr, gls, gs, gr, sts, strv, wos) = refs[3 * nw + 5:]
    x, z, y, c = (lax.axis_index(n) for n in ('sp', 'z', 'y', 'c'))

    def mod4(v):
        return lax.rem(v + 8, 4)

    p1 = (1 - c) * y + c * z
    p2 = (1 - c) * z + c * y
    dirs = (1, -1)

    def axis1(d):
        return (x, mod4(z + d * c), mod4(y + d * (1 - c)), c)

    def axis2(d):
        return (x, mod4(z + d * (1 - c)), mod4(y + d * c), c)

    def xdev(d):
        return (mod4(x + d), z, y, c)

    partner = (x, z, y, 1 - c)
    peers = [axis1(1), axis1(-1), axis2(1), axis2(-1), xdev(1), xdev(-1), xdev(2), partner]
    barrier = pltpu.get_barrier_semaphore()
    for peer in peers:
        pl.semaphore_signal(barrier, inc=1, device_id=peer, device_id_type=MESH_ID)

    def seg_rows(b, j):
        zz = (1 - c) * j + c * b
        yy = (1 - c) * b + c * j
        return pl.ds(pl.multiple_of(zz * 1024 + yy * SEG, SEG), SEG)

    def remote(src, dst, ss, rs, dev):
        return pltpu.make_async_remote_copy(src_ref=src, dst_ref=dst, send_sem=ss, recv_sem=rs, device_id=dev, device_id_type=MESH_ID)

    def each(fn, n=4):
        def step(jj, carry):
            for kk in range(2):
                fn(kk, jj)
            return carry
        lax.fori_loop(0, n, step, 0)

    my_rows = pl.ds(pl.multiple_of(z * 1024 + y * SEG + c * 128, 128), 128)

    def load(m, k):
        src = w_in[m].at[:, pl.ds(pl.multiple_of(k * 1024 + x * SEG, SEG), SEG)]
        return pltpu.make_async_copy(src, w.at[m, my_rows, pl.ds(k * SEG, SEG)], ld.at[m, k])

    def pair_send(m):
        return remote(w.at[m, my_rows], w.at[m, my_rows], d0s.at[m], d0r.at[m], partner)

    def color(kk):
        return pl.ds(pl.multiple_of((2 * c + kk) * SEG, SEG), SEG)

    def same(m, kk, rows, ss, rs, dev):
        ref = w.at[m, rows, color(kk)]
        return remote(ref, ref, ss, rs, dev)

    def send1(m, u, kk):
        d = dirs[kk]
        return same(m, kk, seg_rows(p1, mod4(p2 - d * u)), a1s.at[m, kk, u], a1r.at[m, kk, u], axis2(d))

    def fwd1(m, u, kk):
        rows = seg_rows(p1, mod4(p2 - dirs[kk] * (u + 1)))
        return same(m, kk, rows, f3s.at[m, kk, u], f3r.at[m, kk, u], partner)

    def send2(m, t, kk, jj):
        d = dirs[kk]
        rows = seg_rows(mod4(p1 - d * t), mod4(p2 - d * jj))
        return same(m, kk, rows, a2s.at[m, kk, t, jj], a2r.at[m, kk, t, jj], axis1(d))

    def fwd2(m, t, kk, jj):
        d = dirs[kk]
        rows = seg_rows(mod4(p1 - d * (t + 1)), mod4(p2 - d * jj))
        idx = 3 + t * 4 + jj
        return same(m, kk, rows, f3s.at[m, kk, idx], f3r.at[m, kk, idx], partner)

    def xseg(ref, b, g):
        rows = pl.ds(pl.multiple_of(b * 128, 128), 128)
        return ref.at[rows, pl.ds(g * 1024, 1024)]

    x_own = pltpu.make_async_copy(x_in, x_full.at[pl.ds(pl.multiple_of(x * 128, 128), 128)], xls)

    def xsend(di, g):
        ref = xseg(x_full, x, g)
        return remote(ref, ref, xs.at[di, g], xr.at[di, g], xdev(dirs[di]))

    def xfwd(g):
        d = dirs[g // 2]
        ref = xseg(x_full, mod4(x - d), g)
        return remote(ref, ref, xfs.at[g], xfr.at[g], xdev(d))

    gy_rows = pl.ds(pl.multiple_of(x * 128, 128), 128)
    gy_own = pltpu.make_async_copy(gy_in.at[x], gy_cols.at[gy_rows], gls)

    def gy_send(i):
        d = (1, -1, 2)[i]
        return remote(gy_in.at[mod4(x + d)], gy_cols.at[gy_rows], gs.at[i], gr.at[i], xdev(d))

    def st_send(i):
        d = (1, -1, 2)[i]
        return remote(st.at[0], st.at[1 + i], sts.at[i], strv.at[i], xdev(d))

    def w_store(m):
        return pltpu.make_async_copy(w.at[m], w_out[m], wos.at[m])

    st[0] = jnp.zeros((8, 512), F32)
    x_own.start()
    for m in range(nw):
        for k in range(4):
            load(m, k).start()
    gy_own.start()
    pl.semaphore_wait(barrier, len(peers))
    x_own.wait()
    for m in range(nw):
        for k in range(4):
            load(m, k).wait()
        pair_send(m).start()
        if m == 0:
            for g in range(4):
                for di in range(2):
                    xsend(di, (g + 2 * di) % 4).start()

    def stage1_first(m):
        pair_send(m).wait_recv()
        for kk in range(2):
            send1(m, 0, kk).start()
            send2(m, 0, kk, 0).start()

    def stage1_next(m, u):
        for kk in range(2):
            send1(m, u, kk).wait_recv()
            if u < 2:
                send1(m, u + 1, kk).start()
            send2(m, 0, kk, u + 1).start()
            fwd1(m, u, kk).start()

    def pair_done(m):
        def step(i, carry):
            for kk in range(2):
                ref = w.at[m, pl.ds(0, SEG), pl.ds(0, SEG)]
                remote(ref, ref, f3s.at[m, kk, i], f3r.at[m, kk, i], partner).wait_recv()
            return carry
        lax.fori_loop(0, 15, step, 0)

    def chunks(m, theirs):
        def step(i, carry):
            base = (1 - c) if theirs else c
            k = 2 * base + i
            cols = pl.ds(pl.multiple_of(k * SEG, SEG), SEG)
            acc = jnp.dot(x_full[...], w[m, :, cols], preferred_element_type=F32).astype(BF16)
            qkv[m][:, cols] = acc
            if m < 2:
                sqv = acc.astype(F32)
                sqv = sqv * sqv
                sqv = sqv[:, :128] + sqv[:, 128:]
                if theirs:
                    sq[m] = sq[m] + sqv
                else:
                    @pl.when(i == 0)
                    def _():
                        sq[m] = sqv

                    @pl.when(i == 1)
                    def _():
                        sq[m] = sq[m] + sqv
            return carry
        lax.fori_loop(0, 2, step, 0)

    def x_wait():
        for g in range(4):
            xsend(1 - g // 2, g).wait_recv()
            xfwd(g).wait_recv()

    stage1_first(0)
    for u in range(3):
        stage1_next(0, u)
    for m in range(nw):
        for t in range(3):
            def item(kk, jj):
                send2(m, t, kk, jj).wait_recv()
                if t < 2:
                    send2(m, t + 1, kk, jj).start()
                fwd2(m, t, kk, jj).start()
            each(item)
            if m + 1 < nw:
                if t == 0:
                    stage1_first(m + 1)
                    stage1_next(m + 1, 0)
                elif t == 1:
                    stage1_next(m + 1, 1)
                else:
                    stage1_next(m + 1, 2)
            if (m, t) == (0, 1):
                for g in range(4):
                    xsend(g // 2, g).wait_recv()
                    xfwd(g).start()
                for i in range(3):
                    gy_send(i).start()
            if (m, t) == (1, 1):
                x_wait()
                chunks(0, False)
            if (m, t) == (1, 2):
                pair_done(0)
                w_store(0).start()
                chunks(0, True)
            if (m, t) == (2, 0):
                chunks(1, False)
            if (m, t) == (2, 1):
                pair_done(1)
                w_store(1).start()
                chunks(1, True)
                for i in range(2):
                    st[0, i:i + 1] = jnp.sum(sq[i].T, axis=0, keepdims=True)
                for i in range(3):
                    st_send(i).start()
    chunks(2, False)
    pair_done(2)
    w_store(2).start()
    chunks(2, True)
    for i in range(3):
        st_send(i).wait()
    stats[...] = (st[0] + st[1]) + (st[2] + st[3])

    gy_own.wait()
    for i in range(3):
        gy_send(i).wait()
    for g in range(4):
        xsend(0, g).wait_send()
        xsend(1, g).wait_send()
        xfwd(g).wait_send()
    for m in range(nw):
        pair_send(m).wait_send()
        for kk in range(2):
            for u in range(3):
                send1(m, u, kk).wait_send()
                fwd1(m, u, kk).wait_send()
        for t in range(3):
            each(lambda kk, jj: send2(m, t, kk, jj).wait_send())
            each(lambda kk, jj: fwd2(m, t, kk, jj).wait_send())
        w_store(m).wait()


def gather_project(weights, x_tok, gy_split):
    nw = len(weights)
    dma = pltpu.SemaphoreType.DMA
    vmem = pl.BlockSpec(memory_space=pltpu.VMEM)
    hbm = pl.BlockSpec(memory_space=HBM)
    sds = jax.ShapeDtypeStruct
    return pl.pallas_call(
        gather_kernel,
        out_shape=[sds((4096, 1024), BF16)] * nw + [sds((512, 1024), BF16)] * nw
        + [sds((512, 4096), BF16), sds((512, 1024), BF16), sds((8, 512), F32)],
        in_specs=[hbm] * (nw + 2),
        out_specs=[hbm] * nw + [vmem] * (nw + 3),
        scratch_shapes=[
            pltpu.VMEM((nw, 4096, 1024), BF16),
            pltpu.VMEM((2, 512, 128), F32),
            pltpu.VMEM((4, 8, 512), F32),
            dma((nw, 4)), dma((nw,)), dma((nw,)),
            dma((nw, 2, 3)), dma((nw, 2, 3)),
            dma((nw, 2, 3, 4)), dma((nw, 2, 3, 4)),
            dma((nw, 2, 15)), dma((nw, 2, 15)),
            dma(()), dma((2, 4)), dma((2, 4)), dma((4,)), dma((4,)),
            dma(()), dma((3,)), dma((3,)), dma((3,)), dma((3,)), dma((nw,)),
        ],
        compiler_params=pltpu.CompilerParams(collective_id=5, has_side_effects=True, vmem_limit_bytes=60 * 1024 * 1024),
        cost_estimate=pl.CostEstimate(flops=10 ** 11, bytes_accessed=10 ** 8, transcendentals=0),
        name='gather_project',
    )(*weights, x_tok, gy_split)


def rope_angles(positions):
    half_dim = HEAD_DIM // 2
    inv_freq = ROPE_THETA ** (-jnp.arange(half_dim, dtype=jnp.float32) * (2.0 / HEAD_DIM))
    angles = positions.astype(jnp.float32)[:, None] * inv_freq[None, :]
    return jnp.cos(angles)[:, None, :], jnp.sin(angles)[:, None, :]


def rope_apply(heads_in, cos_tab, sin_tab):
    half_dim = HEAD_DIM // 2
    first_half = heads_in[..., :half_dim]
    second_half = heads_in[..., half_dim:]
    return jnp.concatenate([first_half * cos_tab - second_half * sin_tab, second_half * cos_tab + first_half * sin_tab], axis=-1)


def causal_attention(q_rot, k_rot, v_heads):
    seq_len = q_rot.shape[0]
    scores = jnp.einsum('qhd,khd->hqk', q_rot, k_rot, preferred_element_type=F32) * (HEAD_DIM ** -0.5)
    causal = jnp.arange(seq_len)[:, None] >= jnp.arange(seq_len)[None, :]
    attn_probs = jax.nn.softmax(jnp.where(causal, scores, -1e30), axis=-1).astype(BF16)
    return jnp.einsum('hqk,khd->qhd', attn_probs, v_heads, preferred_element_type=F32).astype(BF16)


def solution(mesh):
    sp_size = mesh.shape['sp']
    mesh4 = Mesh(mesh.devices.reshape(4, 4, 4, 2), ('sp', 'z', 'y', 'c'))
    tok_spec = P(FS, 'sp', None)
    row_spec = P(FS, None)
    vec_spec = P(FS)

    def local_step(x, grad_y, wq_rows, wk_rows, wv_rows, wo_rows, gq_rows, gk_rows, gpost_rows):
        _, tok_len, width = x.shape
        rows = wq_rows.shape[0]
        seq_len = tok_len * sp_size
        lw = width // sp_size
        heads = lw // HEAD_DIM
        s = lax.axis_index('sp')

        def my_cols(w):
            return lax.dynamic_index_in_dim(w.reshape(w.shape[0], 4, 4, lw // 4), s, 2, False).reshape(w.shape[0], lw)

        def gather_cols(w):
            return lax.all_gather(my_cols(w), FS, axis=0, tiled=True)

        def gather_sp(v):
            n = v.shape[0]
            return lax.all_gather(v.reshape(n, 4, 1, lw // 4), 'sp', axis=2, tiled=True).reshape(n, width)

        def to_cols(v):
            n = v.shape[0]
            return lax.all_to_all(v.reshape(n, 4, 4, lw // 4), 'sp', 2, 0, tiled=True).reshape(n * 4, lw)

        def to_tokens(v):
            n = v.shape[0]
            return lax.all_to_all(v.reshape(n, 4, 1, lw // 4), 'sp', 0, 2, tiled=True).reshape(n // 4, width)

        x_tok, gy_tok = x[0], grad_y[0]
        gy_split = gy_tok.reshape(tok_len, 4, 4, lw // 4).transpose(2, 0, 1, 3).reshape(4, tok_len, lw)
        w_q, w_k, w_v, q_lin, k_lin, v_lin, x_full, gy_cols, qk_ss = gather_project([wq_rows, wk_rows, wv_rows], x_tok, gy_split)
        w_o = gather_cols(wo_rows)
        wo_x = lax.all_to_all(wo_rows.reshape(rows, 4, lw), 'y', 1, 0, tiled=False)
        wo_mine = lax.dynamic_index_in_dim(wo_x, s, 0, False)
        wo_gath = lax.all_gather(wo_mine, FS, axis=0, tiled=False)
        wo_head = wo_gath.reshape(4, 4, 2, rows, lw).transpose(0, 2, 3, 1, 4).reshape(lw, width)

        gains = jnp.concatenate([jnp.stack([gq_rows, gk_rows, gpost_rows]), jnp.zeros((61, HEAD_DIM), F32)], axis=0)
        gains = lax.all_gather(gains, FS, axis=0, tiled=False)[:, :3]
        gains = my_cols(gains.transpose(1, 0, 2).reshape(3, width))
        gain_q, gain_k, gain_post = gains[0], gains[1], gains[2]

        q_lin, k_lin = q_lin.astype(F32), k_lin.astype(F32)
        qk_inv = lax.rsqrt(qk_ss / width + RMS_EPSILON)
        q_inv, k_inv = qk_inv[0][:, None], qk_inv[1][:, None]
        q_hat = q_lin * q_inv
        k_hat = k_lin * k_inv
        cos_tab, sin_tab = rope_angles(jnp.arange(seq_len))
        hs = (seq_len, heads, HEAD_DIM)
        q_rot = rope_apply((q_hat * gain_q).reshape(hs), cos_tab, sin_tab).astype(BF16)
        k_rot = rope_apply((k_hat * gain_k).reshape(hs), cos_tab, sin_tab).astype(BF16)
        attn, attn_pull = jax.vjp(causal_attention, q_rot, k_rot, v_lin.reshape(hs))
        o_full = gather_sp(attn.reshape(seq_len, lw))
        a_lin = jnp.dot(o_full, w_o, preferred_element_type=F32).astype(BF16).astype(F32)
        gy_cols = gy_cols.astype(F32)
        grad_hat = gy_cols * gain_post
        a_st = lax.psum(jnp.stack([jnp.sum(a_lin * a_lin, axis=1), jnp.sum(grad_hat * a_lin, axis=1)]), 'sp')
        a_inv = lax.rsqrt(a_st[0] / width + RMS_EPSILON)[:, None]
        a_mean = a_st[1][:, None] * a_inv / width
        a_hat = a_lin * a_inv
        y_cols = (my_cols(x_full).astype(F32) + a_hat * gain_post).astype(BF16)
        y = to_tokens(y_cols)
        grad_a = (a_inv * (grad_hat - a_hat * a_mean)).astype(BF16)
        post_part = jnp.sum(gy_cols * a_hat, axis=0)
        ga_full = gather_sp(grad_a)
        grad_o = lax.dot_general(ga_full, wo_head, (((1,), (1,)), ((), ())), preferred_element_type=F32).astype(BF16)

        cidx = lax.axis_index('c')

        def swap(v):
            return lax.ppermute(v, 'c', [(0, 1), (1, 0)])

        def halves(v):
            h = v.reshape(seq_len, 2, lw // 2)
            mine = lax.dynamic_index_in_dim(h, cidx, 1, False)
            theirs = swap(lax.dynamic_index_in_dim(h, 1 - cidx, 1, False))
            return jnp.concatenate([mine, theirs], axis=0)

        x_two = jnp.concatenate([x_full, swap(x_full)], axis=0)
        o_two = jnp.concatenate([o_full, swap(o_full)], axis=0)

        def weight_part(left, right):
            return lax.dot_general(left, halves(right), (((0,), (0,)), ((), ())), preferred_element_type=F32)

        po = weight_part(o_two, grad_a)
        grad_q_rot, grad_k_rot, grad_v = attn_pull(grad_o.reshape(hs))
        grad_v = grad_v.reshape(seq_len, lw)
        pv = weight_part(x_two, grad_v)
        grad_qn = rope_apply(grad_q_rot.astype(F32), cos_tab, -sin_tab).reshape(seq_len, lw)
        grad_kn = rope_apply(grad_k_rot.astype(F32), cos_tab, -sin_tab).reshape(seq_len, lw)
        gain_q_part = jnp.sum(grad_qn * q_hat, axis=0)
        gain_k_part = jnp.sum(grad_kn * k_hat, axis=0)
        grad_qh = grad_qn * gain_q
        grad_kh = grad_kn * gain_k
        pr = lax.psum(jnp.stack([jnp.sum(grad_qh * q_hat, axis=1), jnp.sum(grad_kh * k_hat, axis=1)]), 'sp') / width
        grad_q = (q_inv * (grad_qh - q_hat * pr[0][:, None])).astype(BF16)
        grad_k = (k_inv * (grad_kh - k_hat * pr[1][:, None])).astype(BF16)
        pk = weight_part(x_two, grad_k)
        pq = weight_part(x_two, grad_q)

        def back(g, w):
            return lax.dot_general(g, w, (((1,), (1,)), ((), ())), preferred_element_type=F32)

        gx_part = back(grad_q, w_q) + back(grad_k, w_k) + back(grad_v, w_v)
        dwo, dwv, dwk, dwq, grad_x = reduce_grads([po, pv, pk, pq], gx_part, gy_tok)

        parts = jnp.stack([gain_q_part, gain_k_part, post_part])
        every = lax.all_gather(parts, ('sp',) + FS, axis=0, tiled=False).reshape(4, 32, 3, 4, 2, HEAD_DIM)
        zi, yi = lax.axis_index('z'), lax.axis_index('y')
        every = lax.dynamic_slice(every, (yi, 0, 0, zi, cidx, 0), (1, 32, 3, 1, 1, HEAD_DIM))
        gn = jnp.sum(every, axis=(0, 1, 3, 4))
        return y[None], grad_x[None], dwq, dwk, dwv, dwo, gn[0], gn[1], gn[2]

    return jax.shard_map(local_step, mesh=mesh4,
                         in_specs=(tok_spec, tok_spec, row_spec, row_spec, row_spec, row_spec, vec_spec, vec_spec, vec_spec),
                         out_specs=(tok_spec, tok_spec, row_spec, row_spec, row_spec, row_spec, vec_spec, vec_spec, vec_spec),
                         check_vma=False)
```

time: 1880 us -> 732 us (0.39)
  waiting for transfers between devices: 1240 us -> 94.4 us
  Pallas kernels: 0 us -> 310 us
  blocking collectives: 277 us -> 30.9 us
  matrix products: 251 us -> 132 us
  local copies, waits for them, and re-layouts: 43.6 us -> 99.2 us
    reduce_scatter x4 -> x0, waiting for transfers between devices: 835 us -> none  [reduce_rows(): lax.psum_scatter(grad_part, 'fsdp', scatter_dimension=0, tiled=True)]
    pallas_call x0 -> x2, Pallas kernels: none -> 310 us  [the longest x1 210 us: reduce_grads(): pl.pallas_call(grads_kernel, out_shape=[jax.ShapeDtypeStruct((128, 4096),...]
    all_gather x4 -> x6, waiting for transfers between devices: 274 us -> 94.2 us  [the longest x1 61.6 us: gather_cols(): return lax.all_gather(my_cols(w), FS, axis=0, tiled=True)]
    unnamed x1 -> x0, blocking collectives: 127 us -> none
    dot_general x17 -> x14, matrix products: 242 us -> 122 us  [the longest x4 42.4 us: weight_part(): lax.dot_general(left, halves(right), (((0,), (0,)), ((), ())), preferred_...]
    psum x1 -> x0, waiting for transfers between devices: 108 us -> none  [reduce_rows(): lax.psum(lax.psum_scatter(grad_part, 'fsdp', scatter_dimension=0, tiled=T...]
    all_gather x5 -> x0, blocking collectives: 97 us -> none  [the longest x1 28 us: local_step(): gain_post = lax.all_gather(gpost_rows, 'fsdp', axis=0, tiled=True)]
    all_to_all x3 -> x1, blocking collectives: 37.4 us -> 15.3 us  [local_step(): wo_x = lax.all_to_all(wo_rows.reshape(rows, 4, lw), 'y', 1, 0, tiled=False)]
  transfers between devices with their start and end apart: 14 -> 13, of which waited for: 10 -> 3; matrix products, arithmetic and copies ran while one was open for 14% -> 25% of each run, Pallas kernels for 0% -> 43%
where the time goes in v1:
time: 732 us; the launch traced here: 721 us
  Pallas kernels  310 us (42%)
  matrix products  132 us (18%)
  local copies, waits for them, and re-layouts  99.2 us (14%)
  waiting for transfers between devices  94.4 us (13%)
  blocking collectives  30.9 us (4%)
  other arithmetic  30.3 us (4%)
  between operations  15.3 us (2%)
  starting transfers between devices  10 us (1%)
    pallas_call x1, Pallas kernels, reduce_grads(): pl.pallas_call(grads_kernel, out_shape=[jax.ShapeDtypeStruct((128, 4096),...  210 us
    pallas_call x1, Pallas kernels, gather_project(): pl.pallas_call(gather_kernel, out_shape=[sds((4096, 1024), BF16)] * nw +...  100 us
    all_gather x1, waiting for transfers between devices, gather_cols(): return lax.all_gather(my_cols(w), FS, axis=0, tiled=True)  61.6 us
    dot_general x4, matrix products, weight_part(): lax.dot_general(left, halves(right), (((0,), (0,)), ((), ())), preferred_...  42.4 us
    unnamed x97, local copies, waits for them, and re-layouts  36.7 us
    dot_general x3, matrix products, back(): lax.dot_general(g, w, (((1,), (1,)), ((), ())), preferred_element_type=F32)  35 us
    all_gather x2, waiting for transfers between devices, gather_sp(): lax.all_gather(v.reshape(n, 4, 1, lw // 4), 'sp', axis=2, tiled=True)  32.6 us
    all_to_all x1, blocking collectives, local_step(): wo_x = lax.all_to_all(wo_rows.reshape(rows, 4, lw), 'y', 1, 0, tiled=False)  15.3 us
  transfers between devices with their start and end apart: 13, of which 3 were waited for; matrix products, arithmetic and copies ran while one was open for 25% of the time, Pallas kernels for 43%

profile of v1, /device:TPU:1, one launch (start us, length us, event | category | flops | bytes accessed | tf_op | source)
XLA Modules:
  0.0 721.4 jit_solution(3674365236590718443)
XLA Ops:
  12.6 100.0 %gather_project.1 = (bf16[4096,1024]{1,0:T(8,128)(2,1)}, bf16[4096,1024]{1,0:T(8,128)(2,1)}, bf16[4096,1024]{1,0:T(8,128)(2,1)}, bf16[512,1024]{1,0:T(8,128)(2,1...) custom-call(bf16[128,4096]{1,0:T(8,128)(2,1)} %refs_0_.1, ...), custom_call_target="tpu_custom_call" | custom-call | flops 99999997952 | bytes 100000000 | tf_op jit(solution)/shard_map/gather_project/pallas_call | solution.py:501
  123.8 9.5 %fusion.65 = (f32[8,512]{1,0:T(8,128)S(1)}, f32[8,512,512]{1,2,0:T(8,128)}) fusion(pred[512,512]{0,1:T(8,128)(4,1)} %iota_compare_fusion, bf16[512,8,64]{2,0,1:T(8,128)(2,1)S(1)} %get-tuple-element.68, bf16[512,8,64]{2,0,1:T(8,128)(2,1)S(1)} %get-tuple-element.69, bf16[512,8,64]{2,0,1:T(8,128)(2,1)} %get-tuple-element.44, ...), kind=kOutput, calls=%fused_computation.148 | convolution fusion | flops 549454336 | bytes 10764288 | tf_op jit(solution)/shard_map/jvp()/sub | solution.py:542
  133.3 4.7 divide_convert_fusion
  141.8 15.3 %all_to_all.24 = bf16[1,128,4,1024]{1,3,0,2:T(8,128)(2,1)S(1)} all-to-all(bf16[1,128,4,1024]{1,3,0,2:T(8,128)(2,1)S(1)} %bitcast.174), channel_id=1, replica_groups=mesh['sp'=4,'z'=4,'y'=4,'c'=2] {'y'}, dimensions={2} | all-to-all | bytes 2097152 | tf_op jit(solution)/shard_map/all_to_all | solution.py:583
  158.1 8.3 %reshape.223 = bf16[512,4,4,256]{3,2,1,0:T(4,128)(2,1)} reshape(bf16[512,4096]{1,0:T(8,128)(2,1)} %get-tuple-element.23) | data formatting | bytes 8388608 | tf_op jit(solution)/shard_map/reshape | solution.py:562
  166.3 4.3 constant_dynamic-slice_fusion.11
  173.0 14.9 %all-gather.11.cloned.1.call-done = bf16[512,4,4,256]{0,3,2,1:T(8,128)(2,1)} async-done(((bf16[512,4,1,256]{0,3,2,1:T(8,128)(2,1)}), bf16[512,4,4,256]{0,3,2,1:T(8,128)(2,1)}) %all-gather.11.cloned.1.call-update) | async-done | bytes 4194320 | tf_op jit(solution)/shard_map/all_gather | solution.py:569
  188.0 61.6 %all-gather.13.cloned.1.call-done = bf16[4096,1024]{0,1:T(8,128)(2,1)} async-done(((bf16[128,1024]{0,1:T(8,128)(2,1)}), bf16[4096,1024]{0,1:T(8,128)(2,1)}) %all-gather.13.cloned.1.call-update) | async-done | bytes 8388624 | tf_op jit(solution)/shard_map/all_gather | solution.py:565
  249.6 10.3 %fusion.24 = (f32[512]{0:T(512)S(1)}, f32[512]{0:T(512)S(1)}, bf16[512,1024]{1,0:T(8,128)(2,1)}) fusion(f32[1024]{0:T(1024)S(1)} %bitcast.207, bf16[512,1024]{1,0:T(8,128)(2,1)S(1)} %copy-done.32, bf16[512,4096]{0,1:T(8,128)(2,1)} %bitcast.220, bf16[4096,1024]{0,1:T(8,128)(2,1)} %all-gather.13.cloned.1.call-done), kind=kOutput, calls=%fused_computation.35 | convolution fusion | flops 4299160576 | bytes 14688256 | tf_op jit(solution)/shard_map/dot_general | solution.py:604
  259.9 8.8 %psum.14 = f32[2,512]{1,0:T(2,128)S(1)} all-reduce(f32[2,512]{1,0:T(2,128)S(1)} %pad_maximum_fusion.2), channel_id=1, replica_groups=mesh['sp'=4,'z'=4,'y'=4,'c'=2] {'sp'}, use_global_device_ids=true, to_apply=%region_4.5 | all-reduce | flops 1024 | bytes 8192 | tf_op jit(solution)/shard_map/psum | solution.py:607
  268.7 3.9 fusion.23
  276.0 4.7 constant_dynamic-update-slice_fusion.1
  285.2 4.7 constant_dynamic-update-slice_fusion
  292.8 3.5 all-to-all-start
  296.4 11.2 %fusion.7.refs_0_ = f32[4096,512]{1,0:T(8,128)} fusion(bf16[512,4096]{0,1:T(8,128)(2,1)} %collective-permute-done, bf16[512,4096]{0,1:T(8,128)(2,1)} %bitcast.222, bf16[512,512]{1,0:T(8,128)(2,1)} %collective-permute-done.1, bf16[512,512]{1,0:T(8,128)(2,1)S(1)} %bitcast.187), kind=kOutput, calls=%fused_computation.9 | convolution fusion | flops 4313841664 | bytes 17825792 | tf_op jit(solution)/shard_map/dot_general | solution.py:633
  307.7 12.4 %copy.119 = bf16[4,2,128,4,1024]{4,3,2,1,0:T(4,128)(2,1)} copy(bf16[4,2,128,4,1024]{4,2,1,3,0:T(8,128)(2,1)} %bitcast.169) | data formatting | bytes 16777216 | tf_op jit(solution)/shard_map/transpose | solution.py:586
  320.1 12.1 %copy.169 = bf16[128,8,4,1024]{3,1,2,0:T(8,128)(2,1)} copy(bf16[128,8,4,1024]{3,2,1,0:T(4,128)(2,1)} %bitcast.164) | data formatting | bytes 16777216
  335.2 17.7 %all-gather.15.cloned.1.call-done = bf16[512,4,4,256]{0,3,2,1:T(8,128)(2,1)} async-done(((bf16[512,4,1,256]{0,3,2,1:T(8,128)(2,1)}), bf16[512,4,4,256]{0,3,2,1:T(8,128)(2,1)}) %all-gather.15.cloned.1.call-update) | async-done | bytes 4194320 | tf_op jit(solution)/shard_map/all_gather | solution.py:569
  352.8 10.2 %convolution_convert_fusion.3 = bf16[512,1024]{1,0:T(8,128)(2,1)} fusion(bf16[512,4096]{0,1:T(8,128)(2,1)} %bitcast.223, bf16[1024,4096]{1,0:T(8,128)(2,1)} %bitcast.170), kind=kOutput, calls=%fused_computation.65 | convolution fusion | flops 4295491584 | bytes 13631488 | tf_op jit(solution)/shard_map/dot_general | solution.py:616
  365.1 4.8 fusion.6
  371.9 7.6 %convert_bitcast_fusion.1 = f32[512,8,128]{2,0,1:T(8,128)} fusion(bf16[512,8,64]{2,0,1:T(8,128)(2,1)S(1)} %copy-done.28, bf16[512,8,64]{2,0,1:T(8,128)(2,1)S(1)} %copy-done.27, f32[8,512,512]{1,2,0:T(8,128)} %get-tuple-element.86, bf16[8,512,512]{1,2,0:T(8,128)(2,1)S(1)} %get-tuple-element.89, f32[8,512]{1,0:T(8,128)S(1)} %neg.59, ...), kind=kOutput, calls=%fused_computation.46 | convolution fusion | flops 552599552 | bytes 16023552 | tf_op jit(solution)/shard_map/transpose(jvp(qhd,khd->hqk))/dot_general | solution.py:540
  379.5 7.4 %convert_bitcast_fusion = f32[512,8,128]{2,0,1:T(8,128)} fusion(bf16[512,8,64]{2,0,1:T(8,128)(2,1)S(1)} %copy-done.25, bf16[512,8,64]{2,0,1:T(8,128)(2,1)} %copy-done.26, f32[8,512,512]{1,2,0:T(8,128)S(1)} %bitcast.163, bf16[8,512,512]{1,2,0:T(8,128)(2,1)} %copy-done.14, f32[8,512]{1,0:T(8,128)S(1)} %neg.59, f32[8,512]{1,0:T(8,128)S(1)} %get-tuple-element.85, ...), kind=kOutput, calls=%fused_computation.45 | convolution fusion | flops 552599552 | bytes 16023552 | tf_op jit(solution)/shard_map/transpose(jvp(qhd,khd->hqk))/dot_general | solution.py:540
  394.7 6.8 psum.15
  401.6 4.6 multiply_convert_fusion.1
  408.1 11.6 %fusion.67 = f32[512,4096]{1,0:T(8,128)} fusion(bf16[512,1024]{1,0:T(8,128)(2,1)} %multiply_convert_fusion.1, bf16[4096,1024]{1,0:T(8,128)(2,1)} %get-tuple-element.30), kind=kOutput, calls=%fused_computation.150 | convolution fusion | flops 4294967296 | bytes 17825792 | tf_op jit(solution)/shard_map/dot_general | solution.py:652
  423.8 10.2 %fusion.66 = f32[512,4096]{1,0:T(8,128)} fusion(bf16[512,1024]{1,0:T(8,128)(2,1)S(1)} %copy-done.16, bf16[4096,1024]{1,0:T(8,128)(2,1)} %get-tuple-element.29), kind=kOutput, calls=%fused_computation.149 | convolution fusion | flops 4294967296 | bytes 17825792 | tf_op jit(solution)/shard_map/dot_general | solution.py:652
  444.2 13.2 %add_add_fusion.refs_4_ = f32[512,4096]{1,0:T(8,128)} fusion(f32[512,4096]{1,0:T(8,128)} %fusion.66, f32[512,4096]{1,0:T(8,128)} %fusion.67, bf16[512,1024]{0,1:T(8,128)(2,1)S(1)} %bitcast.180, bf16[4096,1024]{1,0:T(8,128)(2,1)} %get-tuple-element.31), kind=kOutput, calls=%fused_computation.13 | convolution fusion | flops 4299161600 | bytes 34603008 | tf_op jit(solution)/shard_map/dot_general | solution.py:652
  457.7 11.5 %fusion.41.refs_3_ = f32[4096,512]{1,0:T(8,128)} fusion(bf16[1024,4096]{1,0:T(8,128)(2,1)} %constant_dynamic-update-slice_fusion, bf16[512,512]{1,0:T(8,128)(2,1)} %collective-permute-done.5, bf16[512,512]{1,0:T(8,128)(2,1)S(1)} %bitcast.189), kind=kOutput, calls=%fused_computation.84 | convolution fusion | flops 4297064448 | bytes 17825792 | tf_op jit(solution)/shard_map/dot_general | solution.py:633
  469.2 11.4 %fusion.37.refs_2_ = f32[4096,512]{1,0:T(8,128)} fusion(bf16[1024,4096]{1,0:T(8,128)(2,1)} %constant_dynamic-update-slice_fusion, bf16[512,512]{1,0:T(8,128)(2,1)} %collective-permute-done.4, bf16[512,512]{1,0:T(8,128)(2,1)S(1)} %bitcast.188), kind=kOutput, calls=%fused_computation.80 | convolution fusion | flops 4297064448 | bytes 17825792 | tf_op jit(solution)/shard_map/dot_general | solution.py:633
  480.6 8.3 %fusion.33.refs_1_ = f32[4096,512]{1,0:T(8,128)} fusion(bf16[1024,4096]{1,0:T(8,128)(2,1)S(1)} %bitcast.182, bf16[512,512]{0,1:T(8,128)(2,1)} %collective-permute-done.3, bf16[512,512]{0,1:T(8,128)(2,1)S(1)} %copy-done.34), kind=kOutput, calls=%fused_computation.76 | convolution fusion | flops 4297064448 | bytes 17825792 | tf_op jit(solution)/shard_map/dot_general | solution.py:633
  488.9 209.8 %reduce_grads.1 = (f32[128,4096]{1,0:T(8,128)}, f32[128,4096]{1,0:T(8,128)}, f32[128,4096]{1,0:T(8,128)}, f32[128,4096]{1,0:T(8,128)}, bf16[128,4096]{1,0:T(8,128)(2,1)}) custom-call(f32[4096,512]{1,0:T(8,128)} %fusion.7.refs_0_, f32[4096,512]{1,0:T(8,128)} %fusion.33.refs_1_, f32[4096,512]{1,0:T(8,128)} %fusion.37.refs_2_, f32[4096,512]{1,0:T(8,128)} %fusion.41.refs_3_, ...), custom_call_target="tpu_custom_call" | custom-call | flops 99999997952 | bytes 100000000 | tf_op jit(solution)/shard_map/reduce_grads/pallas_call | solution.py:222
  698.8 4.4 reshape.252
  (178 shorter events, 76.3 us)
Async XLA Ops:
  7.2 109.0 %all-gather.17.cloned.1.call-start = ((), (), s32[]{:S(2)}) async-start(), calls=%async_computation.5 | async-start | bytes 1081344 | tf_op jit(solution)/shard_map/all_gather | solution.py:589
  8.7 179.2 %all-gather.11.cloned.1.call-start = ((), (), s32[]{:S(2)}) async-start(), calls=%async_computation.2 | async-start | bytes 5242880 | tf_op jit(solution)/shard_map/all_gather | solution.py:569
  123.8 9.5 %copy-start.24 = (bf16[512,8,64]{2,0,1:T(8,128)(2,1)}, bf16[512,8,64]{2,0,1:T(8,128)(2,1)S(1)}, u32[]{:S(2)}) copy-start(bf16[512,8,64]{2,0,1:T(8,128)(2,1)S(1)} %get-tuple-element.68) | copy-start | bytes 1572868
  123.8 9.5 %copy-start.26 = (bf16[512,8,64]{2,0,1:T(8,128)(2,1)}, bf16[512,8,64]{2,0,1:T(8,128)(2,1)S(1)}, u32[]{:S(2)}) copy-start(bf16[512,8,64]{2,0,1:T(8,128)(2,1)S(1)} %get-tuple-element.69) | copy-start | bytes 1572868
  140.3 109.3 %all-gather.13.cloned.1.call-start = ((), (), s32[]{:S(2)}) async-start(), calls=%async_computation.3 | async-start | bytes 8650752 | tf_op jit(solution)/shard_map/all_gather | solution.py:565
  141.8 165.9 %all-gather.19.cloned.1.call-start = ((), (), s32[]{:S(2)}) async-start(), calls=%async_computation.6 | async-start | bytes 8650752 | tf_op jit(solution)/shard_map/all_gather | solution.py:585
  158.0 194.8 %all-gather.15.cloned.1.call-start = ((), (), s32[]{:S(2)}) async-start(), calls=%async_computation.4 | async-start | bytes 5242880 | tf_op jit(solution)/shard_map/all_gather | solution.py:569
  171.2 78.3 %copy-start.32 = (bf16[512,1024]{1,0:T(8,128)(2,1)S(1)}, bf16[512,1024]{1,0:T(8,128)(2,1)}, u32[]{:S(2)}) copy-start(bf16[512,1024]{1,0:T(8,128)(2,1)} %get-tuple-element.28) | copy-start | bytes 3145732
  273.9 11.3 %collective-permute-start.2 = (bf16[512,4096]{1,0:T(8,128)(2,1)}, bf16[512,4096]{1,0:T(8,128)(2,1)}, u32[]{:S(2)}, u32[]{:S(2)}) collective-permute-start(bf16[512,4096]{1,0:T(8,128)(2,1)} %get-tuple-element.23), channel_id=1, source_target_pairs={{0,1},{1,0},{2,3},{3,2},{4,5},{5,4},{6,7},{7,6},{8,9},{9,8},{10,11... | collective-permute-start | bytes 12582920 | tf_op jit(solution)/shard_map/ppermute | solution.py:621
  275.9 20.6 %collective-permute-start = (bf16[512,4096]{0,1:T(8,128)(2,1)}, bf16[512,4096]{0,1:T(8,128)(2,1)}, u32[]{:S(2)}, u32[]{:S(2)}) collective-permute-start(bf16[512,4096]{0,1:T(8,128)(2,1)} %bitcast.221), channel_id=1, source_target_pairs={{0,1},{1,0},{2,3},{3,2},{4,5},{5,4},{6,7},{7,6},{8,9},{9,8},{10,11... | collective-permute-start | bytes 12582920 | tf_op jit(solution)/shard_map/ppermute | solution.py:621
  284.8 11.7 %collective-permute-start.1 = (bf16[512,512]{1,0:T(8,128)(2,1)}, bf16[512,512]{1,0:T(8,128)(2,1)}, u32[]{:S(2)}, u32[]{:S(2)}) collective-permute-start(bf16[512,512]{1,0:T(8,128)(2,1)} %bitcast.160), channel_id=1, source_target_pairs={{0,1},{1,0},{2,3},{3,2},{4,5},{5,4},{6,7},{7,6},{8,9},{9,8},{10,11... | collective-permute-start | bytes 1572872 | tf_op jit(solution)/shard_map/ppermute | solution.py:621
  291.3 5.2 copy-start.33
  292.8 39.4 %all-to-all-start = ((bf16[512,4,1,256]{3,1,2,0:T(4,128)(2,1)}), bf16[512,4,1,256]{3,1,2,0:T(4,128)(2,1)S(1)}, u32[]{:S(2)}, u32[]{:S(2)}) async-start(bf16[512,4,1,256]{3,1,2,0:T(4,128)(2,1)} %bitcast.21), calls=%async_computation | async-start | bytes 2097152 | tf_op jit(solution)/shard_map/all_to_all | solution.py:577
  296.4 402.5 %all-gather.21.cloned.1.call-start = ((), (), s32[]{:S(2)}) async-start(), calls=%async_computation.7 | async-start | bytes 2113536 | tf_op jit(solution)/shard_map/all_gather | solution.py:658
  365.1 6.8 copy-start.27
  365.1 6.8 copy-start.28
  365.1 6.8 copy-start.35
  365.1 14.4 %slice-start = ((s8[8388608]{0:T(1024)(128)(4,1)}), s8[4194304]{0:T(1024)(128)(4,1)S(1)}, s32[]{:S(2)}) async-start(s8[8388608]{0:T(1024)(128)(4,1)} %bitcast.162), calls=%async_computation.8 | async-start | bytes 8388608
  371.8 7.7 %slice-start.1 = ((s8[8388608]{0:T(1024)(128)(4,1)}), s8[4194304]{0:T(1024)(128)(4,1)S(1)}, s32[]{:S(2)}) async-start(s8[8388608]{0:T(1024)(128)(4,1)} %bitcast.162), calls=%async_computation.9 | async-start | bytes 8388608
  371.9 7.7 %copy-start.25 = (bf16[512,8,64]{2,0,1:T(8,128)(2,1)S(1)}, bf16[512,8,64]{2,0,1:T(8,128)(2,1)}, u32[]{:S(2)}) copy-start(bf16[512,8,64]{2,0,1:T(8,128)(2,1)} %copy-done.24) | copy-start | bytes 1572868
  379.5 7.4 %copy-start.1 = (bf16[8,512,512]{1,2,0:T(8,128)(2,1)S(1)}, bf16[8,512,512]{1,2,0:T(8,128)(2,1)}, u32[]{:S(2)}) copy-start(bf16[8,512,512]{1,2,0:T(8,128)(2,1)} %copy-done) | copy-start | bytes 12582916
  408.0 11.7 %copy-start.3 = (f32[512,8,64]{2,0,1:T(8,128)S(1)}, f32[512,8,64]{2,0,1:T(8,128)}, u32[]{:S(2)}) copy-start(f32[512,8,64]{2,0,1:T(8,128)} %copy-done.2) | copy-start | bytes 3145732
  408.0 11.6 %copy-start.7 = (bf16[512,1024]{1,0:T(8,128)(2,1)S(1)}, bf16[512,1024]{1,0:T(8,128)(2,1)}, u32[]{:S(2)}) copy-start(bf16[512,1024]{1,0:T(8,128)(2,1)} %get-tuple-element.25) | copy-start | bytes 3145732
  436.3 6.4 copy-start.17
  436.3 21.4 %collective-permute-start.5 = (bf16[512,512]{1,0:T(8,128)(2,1)S(1)}, bf16[512,512]{1,0:T(8,128)(2,1)}, u32[]{:S(2)}, u32[]{:S(2)}) collective-permute-start(bf16[512,512]{1,0:T(8,128)(2,1)S(1)} %bitcast.186), channel_id=1, source_target_pairs={{0,1},{1,0},{2,3},{3,2},{4,5},{5,4},{6,7},{7,6},{8,9},{9,8},{10,11... | collective-permute-start | bytes 1572872 | tf_op jit(solution)/shard_map/ppermute | solution.py:621
  442.7 26.5 %collective-permute-start.4 = (bf16[512,512]{1,0:T(8,128)(2,1)}, bf16[512,512]{1,0:T(8,128)(2,1)}, u32[]{:S(2)}, u32[]{:S(2)}) collective-permute-start(bf16[512,512]{1,0:T(8,128)(2,1)} %bitcast.158), channel_id=1, source_target_pairs={{0,1},{1,0},{2,3},{3,2},{4,5},{5,4},{6,7},{7,6},{8,9},{9,8},{10,11... | collective-permute-start | bytes 1572872 | tf_op jit(solution)/shard_map/ppermute | solution.py:621
  443.8 36.9 %collective-permute-start.3 = (bf16[512,512]{0,1:T(8,128)(2,1)}, bf16[512,512]{0,1:T(8,128)(2,1)}, u32[]{:S(2)}, u32[]{:S(2)}) collective-permute-start(bf16[512,512]{0,1:T(8,128)(2,1)} %get-tuple-element.63), channel_id=1, source_target_pairs={{0,1},{1,0},{2,3},{3,2},{4,5},{5,4},{6,7},{7,6},{8,9},{9,8},{10,11... | collective-permute-start | bytes 1572872 | tf_op jit(solution)/shard_map/ppermute | solution.py:621
  457.7 22.9 %slice-start.2 = ((s8[8388608]{0:T(1024)(128)(4,1)}), s8[4194304]{0:T(1024)(128)(4,1)S(1)}, s32[]{:S(2)}) async-start(s8[8388608]{0:T(1024)(128)(4,1)} %bitcast.181), calls=%async_computation.10 | async-start | bytes 8388608
  469.2 11.5 %slice-start.3 = ((s8[8388608]{0:T(1024)(128)(4,1)}), s8[4194304]{0:T(1024)(128)(4,1)S(1)}, s32[]{:S(2)}) async-start(s8[8388608]{0:T(1024)(128)(4,1)} %bitcast.181), calls=%async_computation.11 | async-start | bytes 8388608
  469.2 11.5 %copy-start.34 = (bf16[512,512]{0,1:T(8,128)(2,1)S(1)}, bf16[512,512]{0,1:T(8,128)(2,1)}, u32[]{:S(2)}) copy-start(bf16[512,512]{0,1:T(8,128)(2,1)} %get-tuple-element.62) | copy-start | bytes 1572868
  698.8 6.0 copy-start.30
  698.8 6.9 copy-start.22
  (21 other events, 50.0 us)
Sparse Core Ops, SparseCore 0:
  10.8 47.4 all-gather.16
  140.4 47.4 all-gather.10
  190.1 59.3 all-gather.12
  251.7 52.1 all-gather.18
  306.0 46.7 all-gather.14
  394.8 66.4 all-gather.20

commit v2 on v0

v2 whole, which is shorter than its diff:
```python
import jax
import jax.numpy as jnp
from jax import lax
from jax.experimental import pallas as pl
from jax.experimental.pallas import tpu as pltpu
from jax.sharding import Mesh, PartitionSpec as P

HEAD_DIM = 128
RMS_EPSILON = 1e-6
ROPE_THETA = 500000.0
FS = ('z', 'y', 'c')
F32 = jnp.float32
BF16 = jnp.bfloat16
MESH_ID = pl.DeviceIdType.MESH
HBM = pl.ANY
SEG = 256
NM = 4


def rope_tables(seq_len):
    half_dim = HEAD_DIM // 2
    inv_freq = ROPE_THETA ** (-jnp.arange(half_dim, dtype=F32) * (2.0 / HEAD_DIM))
    angles = jnp.arange(seq_len).astype(F32)[:, None] * inv_freq[None, :]
    cos_half, sin_half = jnp.cos(angles), jnp.sin(angles)
    return jnp.concatenate([cos_half, cos_half], axis=1), jnp.concatenate([-sin_half, sin_half], axis=1)


def coords():
    return tuple(lax.axis_index(n) for n in ('sp', 'z', 'y', 'c'))


def mod4(v):
    return lax.rem(v + 8, 4)


def remote(src, dst, ss, rs, dev):
    return pltpu.make_async_remote_copy(src_ref=src, dst_ref=dst, send_sem=ss, recv_sem=rs, device_id=dev, device_id_type=MESH_ID)


def at256(v):
    return pl.ds(pl.multiple_of(v, SEG), SEG)


def at128(v):
    return pl.ds(pl.multiple_of(v, 128), 128)


def each(fn, n=4):
    def step(jj, carry):
        for kk in range(2):
            fn(kk, jj)
        return carry
    lax.fori_loop(0, n, step, 0)


def greet(peers):
    barrier = pltpu.get_barrier_semaphore()
    for peer in peers:
        pl.semaphore_signal(barrier, inc=1, device_id=peer, device_id_type=MESH_ID)
    return lambda: pl.semaphore_wait(barrier, len(peers))


class Torus:
    def __init__(self):
        self.x, self.z, self.y, self.c = x, z, y, c = coords()
        self.p1 = (1 - c) * y + c * z
        self.p2 = (1 - c) * z + c * y
        self.partner = (x, z, y, 1 - c)

    def axis1(self, d):
        return (self.x, mod4(self.z + d * self.c), mod4(self.y + d * (1 - self.c)), self.c)

    def axis2(self, d):
        return (self.x, mod4(self.z + d * (1 - self.c)), mod4(self.y + d * self.c), self.c)

    def xdev(self, d, core=None):
        return (mod4(self.x + d), self.z, self.y, self.c if core is None else core)

    def seg_rows(self, b, j):
        zz = (1 - self.c) * j + self.c * b
        yy = (1 - self.c) * b + self.c * j
        return at256(zz * 1024 + yy * SEG)


DIRS = (1, -1)
RING_SEMS = 8


def ring_sems(nw):
    dma = pltpu.SemaphoreType.DMA
    return [dma((nw,)), dma((nw,)), dma((nw, 2, 3)), dma((nw, 2, 3)), dma((nw, 2, 3, 4)), dma((nw, 2, 3, 4)), dma((nw, 2, 15)), dma((nw, 2, 15))]


class WeightRings:
    def __init__(self, g, w, sems):
        self.g, self.w = g, w
        self.d0s, self.d0r, self.a1s, self.a1r, self.a2s, self.a2r, self.f3s, self.f3r = sems
        self.my_rows = at128(g.z * 1024 + g.y * SEG + g.c * 128)

    def pair_send(self, m):
        ref = self.w.at[m, self.my_rows]
        return remote(ref, ref, self.d0s.at[m], self.d0r.at[m], self.g.partner)

    def same(self, m, kk, rows, ss, rs, dev):
        ref = self.w.at[m, rows, at256((2 * self.g.c + kk) * SEG)]
        return remote(ref, ref, ss, rs, dev)

    def send1(self, m, u, kk):
        g, d = self.g, DIRS[kk]
        return self.same(m, kk, g.seg_rows(g.p1, mod4(g.p2 - d * u)), self.a1s.at[m, kk, u], self.a1r.at[m, kk, u], g.axis2(d))

    def fwd1(self, m, u, kk):
        g = self.g
        rows = g.seg_rows(g.p1, mod4(g.p2 - DIRS[kk] * (u + 1)))
        return self.same(m, kk, rows, self.f3s.at[m, kk, u], self.f3r.at[m, kk, u], g.partner)

    def send2(self, m, t, kk, jj):
        g, d = self.g, DIRS[kk]
        rows = g.seg_rows(mod4(g.p1 - d * t), mod4(g.p2 - d * jj))
        return self.same(m, kk, rows, self.a2s.at[m, kk, t, jj], self.a2r.at[m, kk, t, jj], g.axis1(d))

    def fwd2(self, m, t, kk, jj):
        g, d = self.g, DIRS[kk]
        rows = g.seg_rows(mod4(g.p1 - d * (t + 1)), mod4(g.p2 - d * jj))
        idx = 3 + t * 4 + jj
        return self.same(m, kk, rows, self.f3s.at[m, kk, idx], self.f3r.at[m, kk, idx], g.partner)

    def first(self, m):
        self.pair_send(m).wait_recv()
        for kk in range(2):
            self.send1(m, 0, kk).start()
            self.send2(m, 0, kk, 0).start()

    def second(self, m, u):
        for kk in range(2):
            self.send1(m, u, kk).wait_recv()
            if u < 2:
                self.send1(m, u + 1, kk).start()
            self.send2(m, 0, kk, u + 1).start()
            self.fwd1(m, u, kk).start()

    def item(self, m, t, jj):
        for kk in range(2):
            self.send2(m, t, kk, jj).wait_recv()
            if isinstance(t, int):
                if t < 2:
                    self.send2(m, t + 1, kk, jj).start()
            else:
                pl.when(t < 2)(lambda kk=kk: self.send2(m, t + 1, kk, jj).start())
            self.fwd2(m, t, kk, jj).start()

    def round(self, m, t):
        def step(jj, carry):
            self.item(m, t, jj)
            return carry
        lax.fori_loop(0, 4, step, 0)

    def pair_done(self, m):
        def step(i, carry):
            for kk in range(2):
                ref = self.w.at[m, pl.ds(0, SEG), pl.ds(0, SEG)]
                remote(ref, ref, self.f3s.at[m, kk, i], self.f3r.at[m, kk, i], self.g.partner).wait_recv()
            return carry
        lax.fori_loop(0, 15, step, 0)

    def drain(self, m):
        self.pair_send(m).wait_send()
        for kk in range(2):
            for u in range(3):
                self.send1(m, u, kk).wait_send()
                self.fwd1(m, u, kk).wait_send()
        for t in range(3):
            each(lambda kk, jj: self.send2(m, t, kk, jj).wait_send())
            each(lambda kk, jj: self.fwd2(m, t, kk, jj).wait_send())


class StatExchange:
    def __init__(self, g, st, ss, rs):
        self.g, self.st, self.ss, self.rs = g, st, ss, rs

    def copy(self, i):
        return remote(self.st.at[0], self.st.at[1 + i], self.ss.at[i], self.rs.at[i], self.g.xdev((1, -1, 2)[i]))

    def put(self, i, lanes):
        self.st[0, i:i + 1] = jnp.sum(lanes.T, axis=0, keepdims=True)

    def start(self):
        for i in range(3):
            self.copy(i).start()

    def total(self):
        for i in range(3):
            self.copy(i).wait()
        return (self.st[0] + self.st[1]) + (self.st[2] + self.st[3])


def params(cid, vmem_mib=60):
    return pltpu.CompilerParams(collective_id=cid, has_side_effects=True, vmem_limit_bytes=vmem_mib * 1024 * 1024)


COST = pl.CostEstimate(flops=10 ** 11, bytes_accessed=10 ** 8, transcendentals=0)
DMA = pltpu.SemaphoreType.DMA
IN_VMEM = pl.BlockSpec(memory_space=pltpu.VMEM)
IN_HBM = pl.BlockSpec(memory_space=pl.ANY)
SDS = jax.ShapeDtypeStruct


def gather_kernel(wq_in, wk_in, wv_in, x_in, gy_in, wq_out, wk_out, wv_out, x_two, q_out, k_out, v_out, gy_cols, stats,
                  w, x_full, sq, st, ld, xls, xs, xr, xfs, xfr, gls, gs, gr, sts, strv, wos, xps, xpr, xst, *ring):
    w_in, w_out, qkv = (wq_in, wk_in, wv_in), (wq_out, wk_out, wv_out), (q_out, k_out, v_out)
    nw = 3
    g = Torus()
    x, c = g.x, g.c
    rings = WeightRings(g, w, ring)
    ready = greet([g.axis1(1), g.axis1(-1), g.axis2(1), g.axis2(-1), g.xdev(1), g.xdev(-1), g.xdev(2), g.partner])

    def load(m, k):
        src = w_in[m].at[:, at256(k * 1024 + x * SEG)]
        return pltpu.make_async_copy(src, w.at[m, rings.my_rows, pl.ds(k * SEG, SEG)], ld.at[m, k])

    def xseg(b, s):
        return x_full.at[at128(b * 128), pl.ds(s * 1024, 1024)]

    x_own = pltpu.make_async_copy(x_in, x_full.at[at128(x * 128)], xls)

    def xsend(di, s):
        ref = xseg(x, s)
        return remote(ref, ref, xs.at[di, s], xr.at[di, s], g.xdev(DIRS[di]))

    def xfwd(s):
        d = DIRS[s // 2]
        ref = xseg(mod4(x - d), s)
        return remote(ref, ref, xfs.at[s], xfr.at[s], g.xdev(d))

    gy_rows = at128(x * 128)
    gy_own = pltpu.make_async_copy(gy_in.at[x], gy_cols.at[gy_rows], gls)

    def gy_send(i):
        d = (1, -1, 2)[i]
        return remote(gy_in.at[mod4(x + d)], gy_cols.at[gy_rows], gs.at[i], gr.at[i], g.xdev(d))

    stat = StatExchange(g, st, sts, strv)
    x_pair = remote(x_full, x_two.at[pl.ds(512, 512)], xps, xpr, g.partner)
    x_store = pltpu.make_async_copy(x_full, x_two.at[pl.ds(0, 512)], xst)

    def w_store(m):
        return pltpu.make_async_copy(w.at[m], w_out[m], wos.at[m])

    st[0] = jnp.zeros((8, 512), F32)
    x_own.start()
    for m in range(nw):
        for k in range(4):
            load(m, k).start()
    gy_own.start()
    ready()
    x_own.wait()
    for m in range(nw):
        for k in range(4):
            load(m, k).wait()
        rings.pair_send(m).start()
        if m == 0:
            for s in range(4):
                for di in range(2):
                    xsend(di, (s + 2 * di) % 4).start()

    def chunks(m, theirs):
        def step(i, carry):
            k = 2 * ((1 - c) if theirs else c) + i
            cols = at256(k * SEG)
            acc = jnp.dot(x_full[...], w[m, :, cols], preferred_element_type=F32).astype(BF16)
            qkv[m][:, cols] = acc
            if m < 2:
                sqv = acc.astype(F32)
                sqv = sqv * sqv
                sqv = sqv[:, :128] + sqv[:, 128:]
                if theirs:
                    sq[m] = sq[m] + sqv
                else:
                    @pl.when(i == 0)
                    def _():
                        sq[m] = sqv

                    @pl.when(i == 1)
                    def _():
                        sq[m] = sq[m] + sqv
            return carry
        lax.fori_loop(0, 2, step, 0)

    rings.first(0)
    for u in range(3):
        rings.second(0, u)
    for m in range(nw):
        for t in range(3):
            rings.round(m, t)
            if m + 1 < nw:
                if t == 0:
                    rings.first(m + 1)
                rings.second(m + 1, t)
            if (m, t) == (0, 1):
                for s in range(4):
                    xsend(s // 2, s).wait_recv()
                    xfwd(s).start()
                for i in range(3):
                    gy_send(i).start()
            if (m, t) == (1, 1):
                for s in range(4):
                    xsend(1 - s // 2, s).wait_recv()
                    xfwd(s).wait_recv()
                x_pair.start()
                x_store.start()
                chunks(0, False)
            if (m, t) == (1, 2):
                rings.pair_done(0)
                w_store(0).start()
                chunks(0, True)
            if (m, t) == (2, 0):
                chunks(1, False)
            if (m, t) == (2, 1):
                rings.pair_done(1)
                w_store(1).start()
                chunks(1, True)
                for i in range(2):
                    stat.put(i, sq[i])
                stat.start()
    chunks(2, False)
    rings.pair_done(2)
    w_store(2).start()
    chunks(2, True)
    stats[...] = stat.total()

    gy_own.wait()
    for i in range(3):
        gy_send(i).wait()
    for s in range(4):
        xsend(0, s).wait_send()
        xsend(1, s).wait_send()
        xfwd(s).wait_send()
    x_pair.wait()
    x_store.wait()
    for m in range(nw):
        rings.drain(m)
        w_store(m).wait()


def gather_project(w_q, w_k, w_v, x_tok, gy_split):
    return pl.pallas_call(
        gather_kernel,
        out_shape=[SDS((4096, 1024), BF16)] * 3 + [SDS((1024, 4096), BF16)] + [SDS((512, 1024), BF16)] * 4 + [SDS((8, 512), F32)],
        in_specs=[IN_HBM] * 5,
        out_specs=[IN_HBM] * 4 + [IN_VMEM] * 5,
        scratch_shapes=[
            pltpu.VMEM((3, 4096, 1024), BF16),
            pltpu.VMEM((512, 4096), BF16),
            pltpu.VMEM((2, 512, 128), F32),
            pltpu.VMEM((4, 8, 512), F32),
            DMA((3, 4)), DMA(()), DMA((2, 4)), DMA((2, 4)), DMA((4,)), DMA((4,)),
            DMA(()), DMA((3,)), DMA((3,)), DMA((3,)), DMA((3,)), DMA((3,)), DMA(()), DMA(()), DMA(()),
        ] + ring_sems(3),
        compiler_params=params(5), cost_estimate=COST, name='gather_project',
    )(w_q, w_k, w_v, x_tok, gy_split)


SCALE = HEAD_DIM ** -0.5


def rope_turn(u, cos_tab, sin_tab):
    return u * cos_tab + pltpu.roll(u, 64, 1) * sin_tab


def causal_scores(q_blk, keys, i, n):
    s = lax.dot_general(q_blk, keys, (((1,), (1,)), ((), ())), preferred_element_type=F32) * SCALE
    rows = lax.broadcasted_iota(jnp.int32, (128, n), 0) + i * 128
    return jnp.where(rows >= lax.broadcasted_iota(jnp.int32, (128, n), 1), s, -1e30)


def inv_column(total, i):
    return lax.rsqrt(total.T[:, i:i + 1] / 4096.0 + RMS_EPSILON)


def forward_kernel(q0, k0, v0, stats, gains, cos_tab, sin_tab, gy, x_two, wo_in,
                   y_out, q_rot, k_rot, o_two, ga_two, grad_o, post,
                   w, o_full, a_acc, xc, ga_all, y_cols, sa, st,
                   ld, scs, scr, xcs, osd, orv, ofs, ofr, ops, opr, ost, gsd, grv, gfs, gfr, gps, gpr, gst, ysd, yrv, yst, sts, strv, *ring):
    g = Torus()
    x, z, y, c = g.x, g.z, g.y, g.c
    rings = WeightRings(g, w, ring)
    ready = greet([g.axis1(1), g.axis1(-1), g.axis2(1), g.axis2(-1), g.xdev(1), g.xdev(-1), g.xdev(2), g.partner]
                  + [(x, z, mod4(y + d), c) for d in (1, 2, 3)])

    def load(k):
        return pltpu.make_async_copy(wo_in.at[:, at256(k * 1024 + x * SEG)], w.at[0, rings.my_rows, pl.ds(k * SEG, SEG)], ld.at[k])

    def scatter(d):
        to = mod4(y + d)
        dst = w.at[1, at128(z * 1024 + to * SEG + c * 128)]
        return remote(wo_in.at[:, pl.ds(pl.multiple_of(to * 1024, 1024), 1024)], dst, scs.at[d], scr, (x, z, to, c))

    own_rows = pltpu.make_async_copy(wo_in.at[:, pl.ds(pl.multiple_of(y * 1024, 1024), 1024)], w.at[1, rings.my_rows], scs.at[0])

    def xc_load(k):
        return pltpu.make_async_copy(x_two.at[pl.ds(0, 512), at256(k * 1024 + x * SEG)], xc.at[:, pl.ds(k * SEG, SEG)], xcs.at[k])

    for k in range(4):
        load(k).start()
        xc_load(k).start()
    pl.when(y == x)(lambda: own_rows.start())

    inv_q = inv_column(stats[...], 0)
    inv_k = inv_column(stats[...], 1)

    def heads_prep(lo, n):
        def step(h, carry):
            cols = at128(h * 128)
            for src, inv, row, dst in ((q0, inv_q, 0, q_rot), (k0, inv_k, 1, k_rot)):
                u = src[:, cols].astype(F32) * inv * gains[row:row + 1, cols]
                dst[:, cols] = rope_turn(u, cos_tab[...], sin_tab[...]).astype(BF16)
            return carry
        lax.fori_loop(lo, lo + n, step, 0)

    def oblk(k, s):
        return o_full.at[:, at256(k * 1024 + s * SEG)]

    def osend(di, k):
        ref = oblk(k, x)
        return remote(ref, ref, osd.at[di, k], orv.at[di, k], g.xdev(DIRS[di]))

    def ofwd(k):
        d = DIRS[k % 2]
        ref = oblk(k, mod4(x - d))
        return remote(ref, ref, ofs.at[k], ofr.at[k], g.xdev(d))

    o_pair = remote(o_full, o_two.at[pl.ds(512, 512)], ops, opr, g.partner)
    o_store = pltpu.make_async_copy(o_full, o_two.at[pl.ds(0, 512)], ost)

    def gblk(k, s):
        return ga_all.at[s, :, pl.ds(k * SEG, SEG)]

    def gsend(di, k):
        ref = gblk(k, x)
        return remote(ref, ref, gsd.at[di, k], grv.at[di, k], g.xdev(DIRS[di]))

    def gfwd(k):
        d = DIRS[k % 2]
        ref = gblk(k, mod4(x - d))
        return remote(ref, ref, gfs.at[k], gfr.at[k], g.xdev(d))

    half = pl.ds(pl.multiple_of((1 - c) * 512, 512), 512)
    mine = pl.ds(pl.multiple_of(c * 512, 512), 512)
    ga_pair = remote(ga_all.at[x, :, half], ga_two.at[pl.ds(512, 512)], gps, gpr, g.partner)
    ga_store = pltpu.make_async_copy(ga_all.at[x, :, mine], ga_two.at[pl.ds(0, 512)], gst)

    def ysend(i, k):
        d = (1, -1, 2)[i]
        src = y_cols.at[at128(mod4(x + d) * 128), pl.ds(k * SEG, SEG)]
        return remote(src, y_out.at[:, at256(k * 1024 + x * SEG)], ysd.at[i, k], yrv.at[i, k], g.xdev(d))

    def y_store(k):
        return pltpu.make_async_copy(y_cols.at[at128(x * 128), pl.ds(k * SEG, SEG)], y_out.at[:, at256(k * 1024 + x * SEG)], yst.at[k])

    stat = StatExchange(g, st, sts, strv)

    ready()

    @pl.when(y == x)
    def _():
        for d in (1, 3, 2):
            scatter(d).start()
    for k in range(4):
        load(k).wait()
    rings.pair_send(0).start()
    st[0] = jnp.zeros((8, 512), F32)
    heads_prep(0, 1)
    rings.first(0)
    heads_prep(1, 2)
    rings.second(0, 0)
    heads_prep(3, 2)
    rings.second(0, 1)
    heads_prep(5, 2)
    rings.second(0, 2)
    heads_prep(7, 1)

    def head_group(hb, carry):
        for ch in range(2):
            cols = at128(hb * SEG + ch * 128)
            qh, kh, vh = q_rot[:, cols], k_rot[:, cols], v0[:, cols]
            for i in range(4):
                n = (i + 1) * 128
                s = causal_scores(qh[i * 128:n], kh[:n], i, n)
                e = jnp.exp(s - jnp.max(s, axis=-1, keepdims=True))
                p = (e / jnp.sum(e, axis=-1, keepdims=True)).astype(BF16)
                o = jnp.dot(p, vh[:n], preferred_element_type=F32).astype(BF16)
                o_full[pl.ds(i * 128, 128), at128(hb * 1024 + x * SEG + ch * 128)] = o
        for di in range(2):
            osend(di, hb).start()
        for r in range(3):
            it = 3 * hb + r
            rings.item(0, it // 4, lax.rem(it, 4))
        return carry
    lax.fori_loop(0, 4, head_group, 0)

    @pl.when(y == x)
    def _():
        own_rows.wait()

    @pl.when(y != x)
    def _():
        ref = w.at[1, rings.my_rows]
        remote(ref, ref, scs.at[1], scr, g.partner).wait_recv()
    rings.pair_send(1).start()
    rings.pair_done(0)
    rings.first(1)

    def a_part(s, init=False):
        def step(i, carry):
            cols = pl.ds(pl.multiple_of(i * 512, 512), 512)
            acc = None
            for k in range(4):
                dot = jnp.dot(o_full[:, at256(k * 1024 + s * SEG)], w[0, at256(k * 1024 + s * SEG), cols], preferred_element_type=F32)
                acc = dot if acc is None else acc + dot
            a_acc[:, cols] = acc if init else a_acc[:, cols] + acc
            return carry
        lax.fori_loop(0, 2, step, 0)

    a_part(x, True)
    rings.second(1, 0)
    for k in range(4):
        osend(k % 2, k).wait_recv()
        ofwd(k).start()
    rings.second(1, 1)
    rings.second(1, 2)
    rings.round(1, 0)
    for k in range(4):
        osend(1 - k % 2, k).wait_recv()
    a_part(mod4(x - 1))
    rings.round(1, 1)
    a_part(mod4(x + 1))
    for k in range(4):
        ofwd(k).wait_recv()
    a_part(mod4(x + 2))
    o_pair.start()
    o_store.start()
    for k in range(4):
        xc_load(k).wait()

    gpost = gains[2:3, :]

    def a_stats(h, carry):
        cols = at128(h * 128)
        a = a_acc[:, cols].astype(BF16).astype(F32)
        gh = gy[:, cols].astype(F32) * gains[2:3, cols]
        first = h == 0
        for i, v in ((0, a * a), (1, gh * a)):
            sa[i] = jnp.where(first, v, sa[i] + v)
        return carry
    sa[...] = jnp.zeros((2, 512, 128), F32)
    lax.fori_loop(0, 8, a_stats, 0)
    for i in range(2):
        stat.put(i, sa[i])
    stat.start()
    rings.round(1, 2)
    total = stat.total()
    inv_a = inv_column(total, 0)
    mean_a = total.T[:, 1:2] * inv_a / 4096.0

    for k in range(4):
        cols = pl.ds(k * SEG, SEG)
        a_hat = a_acc[:, cols].astype(BF16).astype(F32) * inv_a
        gyv = gy[:, cols].astype(F32)
        ga_all[x, :, cols] = (inv_a * (gyv * gpost[:, k * SEG:(k + 1) * SEG] - a_hat * mean_a)).astype(BF16)
        for di in range(2):
            gsend(di, k).start()
    ga_pair.start()
    ga_store.start()
    rings.pair_done(1)

    def go_part(s, init=False):
        def step(zi, carry):
            cols = at256(zi * SEG)
            acc = None
            for k in range(4):
                dot = lax.dot_general(ga_all[s, :, k * SEG:(k + 1) * SEG], w[1, at256(zi * 1024 + k * SEG), at256(s * SEG)],
                                      (((1,), (1,)), ((), ())), preferred_element_type=F32)
                acc = dot if acc is None else acc + dot
            a_acc[:, cols] = acc if init else a_acc[:, cols] + acc
            return carry
        lax.fori_loop(0, 4, step, 0)

    for k in range(4):
        cols = pl.ds(k * SEG, SEG)
        a_hat = a_acc[:, cols].astype(BF16).astype(F32) * inv_a
        y_cols[:, cols] = (xc[:, cols].astype(F32) + a_hat * gpost[:, k * SEG:(k + 1) * SEG]).astype(BF16)
        post[0:1, cols] = jnp.sum(gy[:, cols].astype(F32) * a_hat, axis=0, keepdims=True)
    go_part(x, True)
    for k in range(4):
        gsend(k % 2, k).wait_recv()
        gfwd(k).start()
    for i in range(3):
        for k in range(4):
            ysend(i, k).start()
    for k in range(4):
        y_store(k).start()
    for k in range(4):
        gsend(1 - k % 2, k).wait_recv()
    go_part(mod4(x - 1))
    go_part(mod4(x + 1))
    for k in range(4):
        gfwd(k).wait_recv()
    go_part(mod4(x + 2))
    grad_o[...] = a_acc[...].astype(BF16)

    @pl.when(y == x)
    def _():
        for d in (1, 2, 3):
            scatter(d).wait_send()
    for k in range(4):
        for di in range(2):
            osend(di, k).wait_send()
            gsend(di, k).wait_send()
        ofwd(k).wait_send()
        gfwd(k).wait_send()
        for i in range(3):
            ysend(i, k).wait()
        y_store(k).wait()
    o_pair.wait()
    o_store.wait()
    ga_pair.wait()
    ga_store.wait()
    for m in range(2):
        rings.drain(m)


def attention_forward(q0, k0, v0, stats, gains, cos_tab, sin_tab, gy_cols, x_two, wo_rows):
    act = SDS((512, 1024), BF16)
    return pl.pallas_call(
        forward_kernel,
        out_shape=[SDS((128, 4096), BF16), act, act, SDS((1024, 4096), BF16), SDS((1024, 512), BF16), act, SDS((1, 1024), F32)],
        in_specs=[IN_VMEM] * 8 + [IN_HBM] * 2,
        out_specs=[IN_HBM, IN_VMEM, IN_VMEM, IN_HBM, IN_HBM, IN_VMEM, IN_VMEM],
        scratch_shapes=[
            pltpu.VMEM((2, 4096, 1024), BF16),
            pltpu.VMEM((512, 4096), BF16),
            pltpu.VMEM((512, 1024), F32),
            pltpu.VMEM((512, 1024), BF16),
            pltpu.VMEM((4, 512, 1024), BF16),
            pltpu.VMEM((512, 1024), BF16),
            pltpu.VMEM((2, 512, 128), F32),
            pltpu.VMEM((4, 8, 512), F32),
            DMA((4,)), DMA((4,)), DMA(()), DMA((4,)), DMA((2, 4)), DMA((2, 4)), DMA((4,)), DMA((4,)), DMA(()), DMA(()), DMA(()),
            DMA((2, 4)), DMA((2, 4)), DMA((4,)), DMA((4,)), DMA(()), DMA(()), DMA(()),
            DMA((3, 4)), DMA((3, 4)), DMA((4,)), DMA((3,)), DMA((3,)),
        ] + ring_sems(2),
        compiler_params=params(6), cost_estimate=COST, name='attention_forward',
    )(q0, k0, v0, stats, gains, cos_tab, sin_tab, gy_cols, x_two, wo_rows)


def backward_kernel(q0, k0, v0, q_rot, k_rot, stats, gains, cos_tab, sin_tab, grad_o,
                    dq_out, dk_out, dv_out, d_two, gain_parts,
                    ghs, dkv, lanes, st, sts, strv, dps, dpr, dst):
    g = Torus()
    c = g.c
    ready = greet([g.xdev(1), g.xdev(-1), g.xdev(2), g.partner])
    stat = StatExchange(g, st, sts, strv)
    outs = (dv_out, dk_out, dq_out)
    half = pl.ds(pl.multiple_of((1 - c) * 512, 512), 512)
    mine = pl.ds(pl.multiple_of(c * 512, 512), 512)

    def pair(m):
        return remote(outs[m].at[:, half], d_two.at[m, pl.ds(512, 512)], dps.at[m], dpr.at[m], g.partner)

    def store(m):
        return pltpu.make_async_copy(outs[m].at[:, mine], d_two.at[m, pl.ds(0, 512)], dst.at[m])

    inv_q = inv_column(stats[...], 0)
    inv_k = inv_column(stats[...], 1)
    lanes[...] = jnp.zeros((2, 512, 128), F32)
    st[0] = jnp.zeros((8, 512), F32)
    tn = (((0,), (0,)), ((), ()))
    nt = (((1,), (1,)), ((), ()))

    def head(h, carry):
        cols = at128(h * 128)
        qh, kh, vh, do = q_rot[:, cols], k_rot[:, cols], v0[:, cols], grad_o[:, cols]
        dkv[...] = jnp.zeros((3, 512, 128), F32)
        for i in range(4):
            n = (i + 1) * 128
            s = causal_scores(qh[i * 128:n], kh[:n], i, n)
            e = jnp.exp(s - jnp.max(s, axis=-1, keepdims=True))
            p = e / jnp.sum(e, axis=-1, keepdims=True)
            do_i = do[i * 128:n]
            dp = lax.dot_general(do_i, vh[:n], nt, preferred_element_type=F32)
            ds = (p * (dp - jnp.sum(p * dp, axis=-1, keepdims=True)) * SCALE).astype(BF16)
            dkv[0, pl.ds(i * 128, 128)] = jnp.dot(ds, kh[:n], preferred_element_type=F32)
            dkv[1, pl.ds(0, n)] = dkv[1, pl.ds(0, n)] + lax.dot_general(ds, qh[i * 128:n], tn, preferred_element_type=F32)
            dkv[2, pl.ds(0, n)] = dkv[2, pl.ds(0, n)] + lax.dot_general(p.astype(BF16), do_i, tn, preferred_element_type=F32)
        dv_out[:, cols] = dkv[2].astype(BF16)
        for i, src, inv in ((0, q0, inv_q), (1, k0, inv_k)):
            gn = rope_turn(dkv[i], cos_tab[...], -sin_tab[...])
            hat = src[:, cols].astype(F32) * inv
            prod = gn * hat
            gain_parts[i:i + 1, cols] = jnp.sum(prod, axis=0, keepdims=True)
            gain = gains[i:i + 1, cols]
            ghs[i, :, cols] = gn * gain
            lanes[i] = lanes[i] + prod * gain
        return carry
    lax.fori_loop(0, 8, head, 0)
    for i in range(2):
        stat.put(i, lanes[i])
    ready()
    stat.start()
    pair(0).start()
    store(0).start()
    total = stat.total().T / 4096.0
    for i, m, src, inv in ((1, 1, k0, inv_k), (0, 2, q0, inv_q)):
        proj = total[:, i:i + 1]

        def finish(h, carry):
            cols = at128(h * 128)
            hat = src[:, cols].astype(F32) * inv
            outs[m][:, cols] = (inv * (ghs[i, :, cols] - hat * proj)).astype(BF16)
            return carry
        lax.fori_loop(0, 8, finish, 0)
        pair(m).start()
        store(m).start()
    for m in range(3):
        pair(m).wait()
        store(m).wait()


def attention_backward(q0, k0, v0, q_rot, k_rot, stats, gains, cos_tab, sin_tab, grad_o):
    act = SDS((512, 1024), BF16)
    return pl.pallas_call(
        backward_kernel,
        out_shape=[act, act, act, SDS((3, 1024, 512), BF16), SDS((2, 1024), F32)],
        in_specs=[IN_VMEM] * 10,
        out_specs=[IN_VMEM, IN_VMEM, IN_VMEM, IN_HBM, IN_VMEM],
        scratch_shapes=[
            pltpu.VMEM((2, 512, 1024), F32),
            pltpu.VMEM((3, 512, 128), F32),
            pltpu.VMEM((2, 512, 128), F32),
            pltpu.VMEM((4, 8, 512), F32),
            DMA((3,)), DMA((3,)), DMA((3,)), DMA((3,)), DMA((3,)),
        ],
        compiler_params=params(7), cost_estimate=COST, name='attention_backward',
    )(q0, k0, v0, q_rot, k_rot, stats, gains, cos_tab, sin_tab, grad_o)


def grads_kernel(*refs):
    parts = refs[:NM]
    gx_part, gy = refs[NM:NM + 2]
    outs = refs[NM + 2:2 * NM + 2]
    gx_out = refs[2 * NM + 2]
    (r1, r2, loc, rg, gloc, s1s, s1r, s2s, s2r, ags, agr, d2s, d2r, fws, fwr, lws, lsem, gs, gr, gsem) = refs[2 * NM + 3:]
    x, z, y, c = (lax.axis_index(n) for n in ('sp', 'z', 'y', 'c'))

    def mod4(v):
        return lax.rem(v + 8, 4)

    p1 = (1 - c) * y + c * z
    p2 = (1 - c) * z + c * y
    dirs = (1, -1)

    def axis1(d):
        return (x, mod4(z + d * c), mod4(y + d * (1 - c)), c)

    def axis2(d):
        return (x, mod4(z + d * (1 - c)), mod4(y + d * c), c)

    def xdev(d, core):
        return (mod4(x + d), z, y, core)

    partner = (x, z, y, 1 - c)
    peers = [axis1(1), axis1(-1), axis2(1), axis2(-1), xdev(1, c), xdev(-1, c), xdev(1, 1 - c), xdev(-1, 1 - c), partner]
    barrier = pltpu.get_barrier_semaphore()
    for peer in peers:
        pl.semaphore_signal(barrier, inc=1, device_id=peer, device_id_type=MESH_ID)
    pl.semaphore_wait(barrier, len(peers))

    def seg_rows(b, j):
        zz = (1 - c) * j + c * b
        yy = (1 - c) * b + c * j
        return pl.ds(pl.multiple_of(zz * 1024 + yy * SEG, SEG), SEG)

    def remote(src, dst, ss, rs, dev):
        return pltpu.make_async_remote_copy(src_ref=src, dst_ref=dst, send_sem=ss, recv_sem=rs, device_id=dev, device_id_type=MESH_ID)

    def send1(m, t, kk, jj):
        d = dirs[kk]
        if t == 0:
            rows = seg_rows(mod4(p1 - d), mod4(p2 - d * (1 + jj)))
            src = parts[m].at[rows, pl.ds(kk * SEG, SEG)]
        else:
            src = r1.at[m, kk, t - 1, jj]
        return remote(src, r1.at[m, kk, t, jj], s1s.at[m, kk, t, jj], s1r.at[m, kk, t, jj], axis1(d))

    def load(m, t, kk, jj):
        d = dirs[kk]
        par = (3 * m + t) % 2
        rows = seg_rows(mod4(p1 - d * (2 + t)), mod4(p2 - d * (1 + jj)))
        return pltpu.make_async_copy(parts[m].at[rows, pl.ds(kk * SEG, SEG)], loc.at[par, kk, jj], lsem.at[par, kk, jj])

    def send2(m, u, kk):
        return remote(r1.at[m, kk, 2, u], r2.at[m, kk, u], s2s.at[m, kk, u], s2r.at[m, kk, u], axis2(dirs[kk]))

    def out_cols(k, xs):
        return pl.ds(pl.multiple_of(k * 1024 + xs * SEG, SEG), SEG)

    def ag_send(m, kk, di, h):
        k = 2 * c + kk
        return remote(r1.at[m, kk, 2, 3, pl.ds(h * 128, 128)], outs[m].at[:, out_cols(k, x)], ags.at[m, kk, di, h], agr.at[m, di, k], xdev(dirs[di], h))

    def ag_recv(m, di, k):
        cols = out_cols(k, mod4(x - dirs[di]))
        return remote(outs[m].at[:, cols], outs[m].at[:, cols], ags.at[m, 0, di, 0], agr.at[m, di, k], xdev(dirs[di], c))

    def pair_send(m, kk):
        k = 2 * c + kk
        rows = pl.ds(pl.multiple_of((1 - c) * 128, 128), 128)
        return remote(r1.at[m, kk, 2, 3, rows], outs[m].at[:, out_cols(k, x)], d2s.at[m, kk], d2r.at[m, kk], partner)

    def own_store(m, kk):
        k = 2 * c + kk
        rows = pl.ds(pl.multiple_of(c * 128, 128), 128)
        return pltpu.make_async_copy(r1.at[m, kk, 2, 3, rows], outs[m].at[:, out_cols(k, x)], lws.at[m, kk])

    def forward(m, k):
        di = k % 2
        cols = out_cols(k, mod4(x - dirs[di]))
        return remote(outs[m].at[:, cols], outs[m].at[:, cols], fws.at[m, k], fwr.at[m, k], xdev(dirs[di], c))

    def gcols(kk, jj):
        return pl.ds(pl.multiple_of(kk * 2048 + jj * 512, 512), 512)

    def gsend(t, kk, jj):
        d = dirs[kk]
        if t == 0:
            src = gx_part.at[pl.ds(pl.multiple_of(mod4(x - d) * 128, 128), 128), gcols(kk, jj)]
        else:
            src = rg.at[kk, t - 1, jj]
        return remote(src, rg.at[kk, t, jj], gs.at[kk, t, jj], gr.at[kk, t, jj], xdev(d, c))

    def gload(t, kk, jj):
        rows = pl.ds(pl.multiple_of(mod4(x - dirs[kk] * (2 + t)) * 128, 128), 128)
        return pltpu.make_async_copy(gx_part.at[rows, gcols(kk, jj)], gloc.at[t % 2, kk, jj], gsem.at[t % 2, kk, jj])

    def each(fn):
        def step(jj, carry):
            for kk in range(2):
                fn(kk, jj)
            return carry
        lax.fori_loop(0, 4, step, 0)

    each(lambda kk, jj: send1(0, 0, kk, jj).start())
    each(lambda kk, jj: load(0, 0, kk, jj).start())
    each(lambda kk, jj: gsend(0, kk, jj).start())
    each(lambda kk, jj: gload(0, kk, jj).start())

    def phase2(m, u):
        for kk in range(2):
            send2(m, u - 1, kk).wait_recv()
            r1[m, kk, 2, u] = r1[m, kk, 2, u] + r2[m, kk, u - 1]
            if u < 3:
                send2(m, u, kk).start()
            else:
                own_store(m, kk).start()
                for di in range(2):
                    for h in range(2):
                        ag_send(m, kk, di, h).start()
                pair_send(m, kk).start()

    def do_forward(m):
        for k in range(4):
            ag_recv(m, k % 2, k).wait_recv()
            forward(m, k).start()

    def gx_step(t):
        if t < 2:
            each(lambda kk, jj: gload(t + 1, kk, jj).start())

        def item(kk, jj):
            gsend(t, kk, jj).wait_recv()
            gload(t, kk, jj).wait()
            total = rg[kk, t, jj] + gloc[t % 2, kk, jj]
            if t < 2:
                rg[kk, t, jj] = total
                gsend(t + 1, kk, jj).start()
            else:
                gx_out[:, gcols(kk, jj)] = (total + gy[:, gcols(kk, jj)].astype(F32)).astype(BF16)
        each(item)

    last = 3 * NM
    for r in range(last):
        m, t = divmod(r, 3)
        if r + 1 < last:
            mn, tn = divmod(r + 1, 3)
            each(lambda kk, jj: load(mn, tn, kk, jj).start())

        def item(kk, jj):
            send1(m, t, kk, jj).wait_recv()
            load(m, t, kk, jj).wait()
            r1[m, kk, t, jj] = r1[m, kk, t, jj] + loc[r % 2, kk, jj]
            if t < 2:
                send1(m, t + 1, kk, jj).start()
            elif m + 1 < NM:
                send1(m + 1, 0, kk, jj).start()

        each(item)
        if t == 2:
            for kk in range(2):
                send2(m, 0, kk).start()
        if m > 0 and t == 0:
            phase2(m - 1, 1)
        if m > 0 and t == 1:
            phase2(m - 1, 2)
        if m > 0 and t == 2:
            phase2(m - 1, 3)
        if m > 1 and t == 0:
            do_forward(m - 2)
        if r in (2, 4, 6):
            gx_step((r - 2) // 2)
    for u in (1, 2, 3):
        phase2(NM - 1, u)
    if NM > 1:
        do_forward(NM - 2)
    do_forward(NM - 1)

    for m in range(NM):
        for t in range(3):
            each(lambda kk, jj: send1(m, t, kk, jj).wait_send())
        for kk in range(2):
            for u in range(3):
                send2(m, u, kk).wait_send()
            for di in range(2):
                for h in range(2):
                    ag_send(m, kk, di, h).wait_send()
            pair_send(m, kk).wait()
            own_store(m, kk).wait()
        for k in range(4):
            ag_recv(m, 1 - k % 2, k).wait_recv()
            forward(m, k).wait()
    for t in range(3):
        each(lambda kk, jj: gsend(t, kk, jj).wait_send())


def reduce_grads(parts, gx_part, gy):
    nm = len(parts)
    dma = pltpu.SemaphoreType.DMA
    vmem = pl.BlockSpec(memory_space=pltpu.VMEM)
    hbm = pl.BlockSpec(memory_space=HBM)
    return pl.pallas_call(
        grads_kernel,
        out_shape=[jax.ShapeDtypeStruct((128, 4096), F32)] * nm + [jax.ShapeDtypeStruct((128, 4096), BF16)],
        in_specs=[hbm] * (nm + 1) + [vmem],
        out_specs=[hbm] * nm + [vmem],
        scratch_shapes=[
            pltpu.VMEM((nm, 2, 3, 4, SEG, SEG), F32),
            pltpu.VMEM((nm, 2, 3, SEG, SEG), F32),
            pltpu.VMEM((2, 2, 4, SEG, SEG), F32),
            pltpu.VMEM((2, 3, 4, 128, 512), F32),
            pltpu.VMEM((2, 2, 4, 128, 512), F32),
            dma((nm, 2, 3, 4)), dma((nm, 2, 3, 4)),
            dma((nm, 2, 3)), dma((nm, 2, 3)),
            dma((nm, 2, 2, 2)), dma((nm, 2, 4)),
            dma((nm, 2)), dma((nm, 2)),
            dma((nm, 4)), dma((nm, 4)),
            dma((nm, 2)), dma((2, 2, 4)),
            dma((2, 3, 4)), dma((2, 3, 4)), dma((2, 2, 4)),
        ],
        compiler_params=pltpu.CompilerParams(collective_id=4, has_side_effects=True, vmem_limit_bytes=60 * 1024 * 1024),
        cost_estimate=pl.CostEstimate(flops=10 ** 11, bytes_accessed=10 ** 8, transcendentals=0),
        name='reduce_grads',
    )(*parts, gx_part, gy)


def solution(mesh):
    mesh4 = Mesh(mesh.devices.reshape(4, 4, 4, 2), ('sp', 'z', 'y', 'c'))
    tok_spec = P(FS, 'sp', None)
    row_spec = P(FS, None)
    vec_spec = P(FS)

    def local_step(x, grad_y, wq_rows, wk_rows, wv_rows, wo_rows, gq_rows, gk_rows, gpost_rows):
        _, tok_len, width = x.shape
        lw = width // 4
        s, zi, yi, ci = coords()
        x_tok, gy_tok = x[0], grad_y[0]

        gains = jnp.concatenate([jnp.stack([gq_rows, gk_rows, gpost_rows]), jnp.zeros((61, HEAD_DIM), F32)], axis=0)
        gains = lax.all_gather(gains, FS, axis=0, tiled=False)[:, :3].reshape(4, 4, 2, 3, HEAD_DIM)
        gains = lax.dynamic_index_in_dim(gains, s, 1, False).transpose(2, 0, 1, 3).reshape(3, lw)
        cos_tab, sin_tab = rope_tables(4 * tok_len)

        gy_split = gy_tok.reshape(tok_len, 4, 4, lw // 4).transpose(2, 0, 1, 3).reshape(4, tok_len, lw)
        w_q, w_k, w_v, x_two, q0, k0, v0, gy_cols, stats = gather_project(wq_rows, wk_rows, wv_rows, x_tok, gy_split)
        y, q_rot, k_rot, o_two, ga_two, grad_o, post = attention_forward(
            q0, k0, v0, stats, gains, cos_tab, sin_tab, gy_cols, x_two, wo_rows)
        dq, dk, dv, d_two, gain_parts = attention_backward(q0, k0, v0, q_rot, k_rot, stats, gains, cos_tab, sin_tab, grad_o)

        def weight_part(left, right):
            return lax.dot_general(left, right, (((0,), (0,)), ((), ())), preferred_element_type=F32)

        def back(g, w):
            return lax.dot_general(g, w, (((1,), (1,)), ((), ())), preferred_element_type=F32)

        po = weight_part(o_two, ga_two)
        pv, pk, pq = (weight_part(x_two, d_two[m]) for m in range(3))
        gx_part = back(dq, w_q) + back(dk, w_k) + back(dv, w_v)
        dwo, dwv, dwk, dwq, grad_x = reduce_grads([po, pv, pk, pq], gx_part, gy_tok)

        parts = jnp.concatenate([gain_parts, post], axis=0)
        every = lax.all_gather(parts, ('sp',) + FS, axis=0, tiled=False).reshape(4, 32, 3, 4, 2, HEAD_DIM)
        every = lax.dynamic_slice(every, (yi, 0, 0, zi, ci, 0), (1, 32, 3, 1, 1, HEAD_DIM))
        gn = jnp.sum(every, axis=(0, 1, 3, 4))
        return y[None], grad_x[None], dwq, dwk, dwv, dwo, gn[0], gn[1], gn[2]

    return jax.shard_map(local_step, mesh=mesh4,
                         in_specs=(tok_spec, tok_spec, row_spec, row_spec, row_spec, row_spec, vec_spec, vec_spec, vec_spec),
                         out_specs=(tok_spec, tok_spec, row_spec, row_spec, row_spec, row_spec, vec_spec, vec_spec, vec_spec),
                         check_vma=False)
```

time: 1880 us -> 586 us (0.31)
  waiting for transfers between devices: 1240 us -> 0.06 us
  Pallas kernels: 0 us -> 469 us
  blocking collectives: 277 us -> 0 us
  matrix products: 251 us -> 65.9 us
  local copies, waits for them, and re-layouts: 43.6 us -> 20.8 us
  other arithmetic: 25.5 us -> 5.12 us
  starting transfers between devices: 20.1 us -> 0.08 us
    reduce_scatter x4 -> x0, waiting for transfers between devices: 835 us -> none  [reduce_rows(): lax.psum_scatter(grad_part, 'fsdp', scatter_dimension=0, tiled=True)]
    pallas_call x0 -> x4, Pallas kernels: none -> 469 us  [the longest x1 211 us: reduce_grads(): pl.pallas_call(grads_kernel, out_shape=[jax.ShapeDtypeStruct((128, 4096),...]
    all_gather x4 -> x2, waiting for transfers between devices: 274 us -> 0.02 us  [the longest x1 0.02 us: local_step(): lax.all_gather(parts, ('sp',) + FS, axis=0, tiled=False)]
    dot_general x17 -> x7, matrix products: 242 us -> 65.9 us  [the longest x3 33.7 us: back(): lax.dot_general(g, w, (((1,), (1,)), ((), ())), preferred_element_type=F32)]
    unnamed x1 -> x0, blocking collectives: 127 us -> none
    psum x1 -> x0, waiting for transfers between devices: 108 us -> none  [reduce_rows(): lax.psum(lax.psum_scatter(grad_part, 'fsdp', scatter_dimension=0, tiled=T...]
    all_gather x5 -> x0, blocking collectives: 97 us -> none  [the longest x1 28 us: local_step(): gain_post = lax.all_gather(gpost_rows, 'fsdp', axis=0, tiled=True)]
    all_to_all x3 -> x0, blocking collectives: 37.4 us -> none  [to_tokens(): lax.all_to_all(blocks, 'sp', 1, 2, tiled=True)]
  transfers between devices with their start and end apart: 14 -> 2, of which waited for: 10 -> 0; matrix products, arithmetic and copies ran while one was open for 14% -> 8% of each run, Pallas kernels for 0% -> 54%
where the time goes in v2:
time: 586 us; the launch traced here: 576 us
  Pallas kernels  469 us (80%)
  matrix products  65.9 us (11%)
  local copies, waits for them, and re-layouts  20.8 us (4%)
  between operations  14.7 us (3%)
    pallas_call x1, Pallas kernels, reduce_grads(): pl.pallas_call(grads_kernel, out_shape=[jax.ShapeDtypeStruct((128, 4096),...  211 us
    pallas_call x1, Pallas kernels, attention_forward(): pl.pallas_call(forward_kernel, out_shape=[SDS((128, 4096), BF16), act, ac...  120 us
    pallas_call x1, Pallas kernels, gather_project(): pl.pallas_call(gather_kernel, out_shape=[SDS((4096, 1024), BF16)] * 3 + [...  98.6 us
    pallas_call x1, Pallas kernels, attention_backward(): pl.pallas_call(backward_kernel, out_shape=[act, act, act, SDS((3, 1024, 5...  39 us
    dot_general x3, matrix products, back(): lax.dot_general(g, w, (((1,), (1,)), ((), ())), preferred_element_type=F32)  33.7 us
    dot_general x4, matrix products, weight_part(): lax.dot_general(left, right, (((0,), (0,)), ((), ())), preferred_element_...  32.2 us
  transfers between devices with their start and end apart: 2, of which 0 were waited for; matrix products, arithmetic and copies ran while one was open for 8% of the time, Pallas kernels for 54%

profile of v2, /device:TPU:1, one launch (start us, length us, event | category | flops | bytes accessed | tf_op | source)
XLA Modules:
  0.0 575.6 jit_solution(8918118870961269963)
XLA Ops:
  7.2 0.0 all-gather.6.cloned.1.call-start
  7.2 0.1 pad.9.clone
  7.3 1.4 maximum_maximum_fusion
  8.7 0.0 all-gather.8.cloned.1.call-start
  8.8 1.9 reshape_squeeze.3
  10.6 0.4 copy.34
  11.0 1.5 reshape.40.gy_in
  12.6 98.6 %gather_project.1 = (bf16[4096,1024]{1,0:T(8,128)(2,1)}, bf16[4096,1024]{1,0:T(8,128)(2,1)}, bf16[4096,1024]{1,0:T(8,128)(2,1)}, bf16[1024,4096]{1,0:T(8,128)(2,...) custom-call(bf16[128,4096]{1,0:T(8,128)(2,1)} %wq_in.1, ...), custom_call_target="tpu_custom_call" | custom-call | flops 99999997952 | bytes 100000000 | tf_op jit(solution)/shard_map/gather_project/pallas_call | solution.py:346
  111.2 1.0 fusion.9
  112.2 1.0 pad_maximum_fusion
  113.2 0.9 slice.28
  114.2 0.6 reshape.42.gains
  114.8 120.4 %attention_forward.1 = (bf16[128,4096]{1,0:T(8,128)(2,1)}, bf16[512,1024]{1,0:T(8,128)(2,1)}, bf16[512,1024]{1,0:T(8,128)(2,1)}, bf16[1024,4096]{1,0:T(8,128)(2,...) custom-call(bf16[512,1024]{1,0:T(8,128)(2,1)} %get-tuple-element.35.q0, ...), custom_call_target="tpu_custom_call" | custom-call | flops 99999997952 | bytes 100000000 | tf_op jit(solution)/shard_map/attention_forward/pallas_call | solution.py:634
  235.3 39.0 %attention_backward.1 = (bf16[512,1024]{1,0:T(8,128)(2,1)}, bf16[512,1024]{1,0:T(8,128)(2,1)}, bf16[512,1024]{1,0:T(8,128)(2,1)}, bf16[3,1024,512]{2,1,0:T(8,128)(2,1)}, f32[2,1024]{1,0:T(2,128)}) custom-call(bf16[512,1024]{1,0:T(8,128)(2,1)} %get-tuple-element.35.q0, bf16[512,1024]{1,0:T(8,128)(2,1)} %get-tuple-element.36.k0, ...), custom_call_target="tpu_custom_call" | custom-call | flops 99999997952 | bytes 100000000 | tf_op jit(solution)/shard_map/attention_backward/pallas_call | solution.py:731
  274.3 11.6 %fusion.refs_3_ = f32[4096,512]{1,0:T(8,128)} fusion(bf16[1024,4096]{1,0:T(8,128)(2,1)} %get-tuple-element.40.x_two, bf16[3,1024,512]{2,1,0:T(8,128)(2,1)} %get-tuple-element.47), kind=kOutput, calls=%fused_computation.1 | convolution fusion | flops 4294967296 | bytes 17825792 | tf_op jit(solution)/shard_map/dot_general | solution.py:998
  285.9 6.9 %fusion.2.refs_2_ = f32[4096,512]{1,0:T(8,128)} fusion(bf16[1024,4096]{1,0:T(8,128)(2,1)S(1)} %copy-done.7, bf16[3,1024,512]{2,1,0:T(8,128)(2,1)S(1)} %copy-done.10), kind=kOutput, calls=%fused_computation.3 | convolution fusion | flops 4294967296 | bytes 17825792 | tf_op jit(solution)/shard_map/dot_general | solution.py:998
  292.8 6.9 %fusion.4.refs_1_ = f32[4096,512]{1,0:T(8,128)} fusion(bf16[1024,4096]{1,0:T(8,128)(2,1)S(1)} %copy-done.7, bf16[3,1024,512]{2,1,0:T(8,128)(2,1)S(1)} %copy-done.10), kind=kOutput, calls=%fused_computation.5 | convolution fusion | flops 4294967296 | bytes 17825792 | tf_op jit(solution)/shard_map/dot_general | solution.py:998
  299.7 0.6 maximum_bitcast_fusion
  300.4 10.3 %fusion.12 = f32[512,4096]{1,0:T(8,128)} fusion(bf16[512,1024]{1,0:T(8,128)(2,1)S(1)} %copy-done.9, bf16[4096,1024]{1,0:T(8,128)(2,1)} %get-tuple-element.51), kind=kOutput, calls=%fused_computation.27 | convolution fusion | flops 4294967296 | bytes 17825792 | tf_op jit(solution)/shard_map/dot_general | solution.py:1001
  310.7 10.6 %fusion.11 = f32[512,4096]{1,0:T(8,128)} fusion(bf16[512,1024]{1,0:T(8,128)(2,1)S(1)} %copy-done.8, bf16[4096,1024]{1,0:T(8,128)(2,1)} %get-tuple-element.49), kind=kOutput, calls=%fused_computation.26 | convolution fusion | flops 4294967296 | bytes 17825792 | tf_op jit(solution)/shard_map/dot_general | solution.py:1001
  321.3 6.9 %fusion.10.refs_0_ = f32[4096,512]{1,0:T(8,128)} fusion(bf16[1024,4096]{1,0:T(8,128)(2,1)S(1)} %bitcast.55, bf16[1024,512]{1,0:T(8,128)(2,1)S(1)} %copy-done.11), kind=kOutput, calls=%fused_computation.25 | convolution fusion | flops 4294967296 | bytes 17825792 | tf_op jit(solution)/shard_map/dot_general | solution.py:998
  328.1 12.8 %add_add_fusion.refs_4_ = f32[512,4096]{1,0:T(8,128)} fusion(f32[512,4096]{1,0:T(8,128)} %fusion.11, f32[512,4096]{1,0:T(8,128)} %fusion.12, bf16[512,1024]{1,0:T(8,128)(2,1)S(1)} %copy-done.6, bf16[4096,1024]{1,0:T(8,128)(2,1)} %get-tuple-element.53), kind=kOutput, calls=%fused_computation | convolution fusion | flops 4299161600 | bytes 34603008 | tf_op jit(solution)/shard_map/dot_general | solution.py:1001
  341.0 210.9 %reduce_grads.1 = (f32[128,4096]{1,0:T(8,128)}, f32[128,4096]{1,0:T(8,128)}, f32[128,4096]{1,0:T(8,128)}, f32[128,4096]{1,0:T(8,128)}, bf16[128,4096]{1,0:T(8,128)(2,1)}) custom-call(f32[4096,512]{1,0:T(8,128)} %fusion.10.refs_0_, f32[4096,512]{1,0:T(8,128)} %fusion.4.refs_1_, f32[4096,512]{1,0:T(8,128)} %fusion.2.refs_2_, f32[4096,512]{1,0:T(8,128)} %fusion.refs_3_, ...), custom_call_target="tpu_custom_call" | custom-call | flops 99999997952 | bytes 100000000 | tf_op jit(solution)/shard_map/reduce_grads/pallas_call | solution.py:949
  551.9 4.4 reshape.50
  556.3 1.1 dynamic-slice_reduce_fusion
  557.5 0.5 slice_bitcast_fusion
  558.0 1.0 copy.41
  559.0 2.3 copy.42
  561.3 3.1 copy.43
  564.4 1.3 copy.44
  565.7 1.3 copy.45
  567.0 1.3 copy.46
  (38 shorter events, 0.1 us)
Async XLA Ops:
  7.2 106.1 %all-gather.6.cloned.1.call-start = ((), (), s32[]{:S(2)}) async-start(), calls=%async_computation | async-start | bytes 1081344 | tf_op jit(solution)/shard_map/all_gather | solution.py:987
  8.7 543.2 %all-gather.8.cloned.1.call-start = ((), (), s32[]{:S(2)}) async-start(), calls=%async_computation.1 | async-start | bytes 2113536 | tf_op jit(solution)/shard_map/all_gather | solution.py:1009
  274.3 11.6 %copy-start.7 = (bf16[1024,4096]{1,0:T(8,128)(2,1)S(1)}, bf16[1024,4096]{1,0:T(8,128)(2,1)}, u32[]{:S(2)}) copy-start(bf16[1024,4096]{1,0:T(8,128)(2,1)} %get-tuple-element.40.x_two) | copy-start | bytes 25165828
  274.3 11.6 %copy-start.10 = (bf16[3,1024,512]{2,1,0:T(8,128)(2,1)S(1)}, bf16[3,1024,512]{2,1,0:T(8,128)(2,1)}, u32[]{:S(2)}) copy-start(bf16[3,1024,512]{2,1,0:T(8,128)(2,1)} %get-tuple-element.47) | copy-start | bytes 9437188
  292.8 6.9 %copy-start.4 = (f32[2,1024]{1,0:T(2,128)S(1)}, f32[2,1024]{1,0:T(2,128)}, u32[]{:S(2)}) copy-start(f32[2,1024]{1,0:T(2,128)} %get-tuple-element.59) | copy-start | bytes 24580
  292.8 6.9 %copy-start.5 = (f32[1,1024]{1,0:T(1,128)S(1)}, f32[1,1024]{1,0:T(1,128)}, u32[]{:S(2)}) copy-start(f32[1,1024]{1,0:T(1,128)} %get-tuple-element.60) | copy-start | bytes 12292
  292.8 7.5 %copy-start.9 = (bf16[512,1024]{1,0:T(8,128)(2,1)S(1)}, bf16[512,1024]{1,0:T(8,128)(2,1)}, u32[]{:S(2)}) copy-start(bf16[512,1024]{1,0:T(8,128)(2,1)} %get-tuple-element.50) | copy-start | bytes 3145732
  300.4 10.3 %copy-start.8 = (bf16[512,1024]{1,0:T(8,128)(2,1)S(1)}, bf16[512,1024]{1,0:T(8,128)(2,1)}, u32[]{:S(2)}) copy-start(bf16[512,1024]{1,0:T(8,128)(2,1)} %get-tuple-element.48) | copy-start | bytes 3145732
  300.4 20.9 %slice-start = ((s8[8388608]{0:T(1024)(128)(4,1)}), s8[4194304]{0:T(1024)(128)(4,1)S(1)}, s32[]{:S(2)}) async-start(s8[8388608]{0:T(1024)(128)(4,1)} %bitcast.54), calls=%async_computation.2 | async-start | bytes 8388608
  310.7 10.6 %slice-start.1 = ((s8[8388608]{0:T(1024)(128)(4,1)}), s8[4194304]{0:T(1024)(128)(4,1)S(1)}, s32[]{:S(2)}) async-start(s8[8388608]{0:T(1024)(128)(4,1)} %bitcast.54), calls=%async_computation.3 | async-start | bytes 8388608
  310.7 10.6 %copy-start.11 = (bf16[1024,512]{1,0:T(8,128)(2,1)S(1)}, bf16[1024,512]{1,0:T(8,128)(2,1)}, u32[]{:S(2)}) copy-start(bf16[1024,512]{1,0:T(8,128)(2,1)} %get-tuple-element.43) | copy-start | bytes 3145732
  321.3 6.9 %copy-start.6 = (bf16[512,1024]{1,0:T(8,128)(2,1)S(1)}, bf16[512,1024]{1,0:T(8,128)(2,1)}, u32[]{:S(2)}) copy-start(bf16[512,1024]{1,0:T(8,128)(2,1)} %get-tuple-element.52) | copy-start | bytes 3145732
  341.0 217.0 %copy-start.3 = (bf16[128,4096]{1,0:T(8,128)(2,1)S(1)}, bf16[128,4096]{1,0:T(8,128)(2,1)}, u32[]{:S(2)}) copy-start(bf16[128,4096]{1,0:T(8,128)(2,1)} %get-tuple-element.41) | copy-start | bytes 3145732
  551.9 13.8 %copy-start.1 = (f32[128,4096]{1,0:T(8,128)S(1)}, f32[128,4096]{1,0:T(8,128)}, u32[]{:S(2)}) copy-start(f32[128,4096]{1,0:T(8,128)} %get-tuple-element.82) | copy-start | bytes 6291460
  556.3 8.1 %copy-start.2 = (f32[128,4096]{1,0:T(8,128)S(1)}, f32[128,4096]{1,0:T(8,128)}, u32[]{:S(2)}) copy-start(f32[128,4096]{1,0:T(8,128)} %get-tuple-element.81) | copy-start | bytes 6291460
  558.0 9.1 %copy-start = (f32[128,4096]{1,0:T(8,128)S(1)}, f32[128,4096]{1,0:T(8,128)}, u32[]{:S(2)}) copy-start(f32[128,4096]{1,0:T(8,128)} %get-tuple-element.83) | copy-start | bytes 6291460
Sparse Core Ops, SparseCore 0:
  10.8 47.4 all-gather.5
  300.5 63.2 all-gather.7

commit v3 on v0

v3 whole, which is shorter than its diff:
```python
import jax
import jax.numpy as jnp
import numpy as np
from jax import lax
from jax.experimental import pallas as pl
from jax.experimental.pallas import tpu as pltpu
from jax.sharding import Mesh, PartitionSpec as P

HEAD_DIM = 128
RMS_EPSILON = 1e-6
ROPE_THETA = 500000.0
FS = ('z', 'y', 'c')
F32 = jnp.float32
BF16 = jnp.bfloat16
MESH_ID = pl.DeviceIdType.MESH
HBM = pl.ANY
SEG = 256


def rope_tables(seq_len):
    half_dim = HEAD_DIM // 2
    angles = np.arange(seq_len)[:, None] * ROPE_THETA ** (-np.arange(half_dim) * (2.0 / HEAD_DIM))[None, :]
    cos_half, sin_half = np.cos(angles), np.sin(angles)
    tables = np.concatenate([cos_half, cos_half], axis=1), np.concatenate([-sin_half, sin_half], axis=1)
    return tuple(jnp.asarray(t, F32) for t in tables)


def coords():
    return tuple(lax.axis_index(n) for n in ('sp', 'z', 'y', 'c'))


def mod4(v):
    return lax.rem(v + 8, 4)


def remote(src, dst, ss, rs, dev):
    return pltpu.make_async_remote_copy(src_ref=src, dst_ref=dst, send_sem=ss, recv_sem=rs, device_id=dev, device_id_type=MESH_ID)


def at256(v):
    return pl.ds(pl.multiple_of(v, SEG), SEG)


def at128(v):
    return pl.ds(pl.multiple_of(v, 128), 128)


def each(fn, n=4):
    def step(jj, carry):
        for kk in range(2):
            fn(kk, jj)
        return carry
    lax.fori_loop(0, n, step, 0)


def loop(lo, hi, fn):
    def step(n, carry):
        fn(n)
        return carry
    lax.fori_loop(lo, hi, step, 0)


def greet(peers):
    barrier = pltpu.get_barrier_semaphore()
    for peer in peers:
        pl.semaphore_signal(barrier, inc=1, device_id=peer, device_id_type=MESH_ID)
    return lambda: pl.semaphore_wait(barrier, len(peers))


class Torus:
    def __init__(self):
        self.x, self.z, self.y, self.c = x, z, y, c = coords()
        self.p1 = (1 - c) * y + c * z
        self.p2 = (1 - c) * z + c * y
        self.partner = (x, z, y, 1 - c)

    def axis1(self, d):
        return (self.x, mod4(self.z + d * self.c), mod4(self.y + d * (1 - self.c)), self.c)

    def axis2(self, d):
        return (self.x, mod4(self.z + d * (1 - self.c)), mod4(self.y + d * self.c), self.c)

    def xdev(self, d, core=None):
        return (mod4(self.x + d), self.z, self.y, self.c if core is None else core)

    def seg_rows(self, b, j):
        zz = (1 - self.c) * j + self.c * b
        yy = (1 - self.c) * b + self.c * j
        return at256(zz * 1024 + yy * SEG)


DIRS = (1, -1)
RING_SEMS = 8


def ring_sems(nw):
    dma = pltpu.SemaphoreType.DMA
    return [dma((nw,)), dma((nw,)), dma((nw,)), dma((nw, 3)), dma((nw,)), dma((nw, 3, 4)), dma((nw,)), dma((nw,))]


class WeightRings:
    def __init__(self, g, w, slots, sems):
        self.g, self.w, self.slots = g, w, slots
        self.d0s, self.d0r, self.a1s, self.a1r, self.a2s, self.a2r, self.f3s, self.f3r = sems
        self.my_rows = at128(g.z * 1024 + g.y * SEG + g.c * 128)

    def pair_send(self, m):
        ref = self.w.at[self.slots[m], self.my_rows]
        return remote(ref, ref, self.d0s.at[m], self.d0r.at[m], self.g.partner)

    def same(self, m, kk, rows, ss, rs, dev):
        ref = self.w.at[self.slots[m], rows, at256((2 * self.g.c + kk) * SEG)]
        return remote(ref, ref, ss, rs, dev)

    def bulk(self, m, n, ss, rs):
        ref = self.w.at[self.slots[m], pl.ds(0, n * 128), pl.ds(0, 512)]
        return remote(ref, ref, ss, rs, self.g.partner)

    def send1(self, m, u, kk):
        g, d = self.g, DIRS[kk]
        return self.same(m, kk, g.seg_rows(g.p1, mod4(g.p2 - d * u)), self.a1s.at[m], self.a1r.at[m, u], g.axis2(d))

    def far1(self, m, e, kk):
        g = self.g
        rows = g.seg_rows(g.p1, g.p2)
        return self.same(m, kk, rows, self.a1s.at[m], self.a1r.at[m, e - 1], g.axis2(DIRS[kk] * e))

    def fwd1(self, m, u, kk):
        g = self.g
        rows = g.seg_rows(g.p1, mod4(g.p2 - DIRS[kk] * (u + 1)))
        return self.same(m, kk, rows, self.f3s.at[m], self.f3r.at[m], g.partner)

    def send2(self, m, t, kk, jj):
        g, d = self.g, DIRS[kk]
        rows = g.seg_rows(mod4(g.p1 - d * t), mod4(g.p2 - d * jj))
        return self.same(m, kk, rows, self.a2s.at[m], self.a2r.at[m, t, jj], g.axis1(d))

    def fwd2(self, m, t, kk, jj):
        g, d = self.g, DIRS[kk]
        rows = g.seg_rows(mod4(g.p1 - d * (t + 1)), mod4(g.p2 - d * jj))
        return self.same(m, kk, rows, self.f3s.at[m], self.f3r.at[m], g.partner)

    def first(self, m, far=False):
        self.pair_send(m).wait_recv()
        for kk in range(2):
            if far:
                for e in (1, 2, 3):
                    self.far1(m, e, kk).start()
            else:
                self.send1(m, 0, kk).start()
            self.send2(m, 0, kk, 0).start()

    def second(self, m, u, far=False):
        self.bulk(m, 2, self.a1s.at[m], self.a1r.at[m, u]).wait_recv()
        for kk in range(2):
            if u < 2 and not far:
                self.send1(m, u + 1, kk).start()
            self.send2(m, 0, kk, u + 1).start()
            self.fwd1(m, u, kk).start()

    def item(self, m, t, jj):
        self.bulk(m, 2, self.a2s.at[m], self.a2r.at[m, t, jj]).wait_recv()

        def pass_on():
            for kk in range(2):
                self.send2(m, t + 1, kk, jj).start()
        if isinstance(t, int):
            if t < 2:
                pass_on()
        else:
            pl.when(t < 2)(pass_on)
        for kk in range(2):
            self.fwd2(m, t, kk, jj).start()

    def round(self, m, t, extra=None):
        def step(jj):
            self.item(m, t, jj)
            if extra is not None:
                extra(jj)
        loop(0, 4, step)

    def pair_done(self, m):
        self.bulk(m, 30, self.f3s.at[m], self.f3r.at[m]).wait_recv()

    def drain(self, m):
        self.pair_send(m).wait_send()
        for sems, n in ((self.a1s, 6), (self.a2s, 24), (self.f3s, 30)):
            self.bulk(m, n, sems.at[m], self.f3r.at[m]).wait_send()


class StatExchange:
    def __init__(self, g, st, ss, rs):
        self.g, self.st, self.ss, self.rs = g, st, ss, rs

    def copy(self, i):
        return remote(self.st.at[0], self.st.at[1 + i], self.ss.at[i], self.rs.at[i], self.g.xdev((1, -1, 2)[i]))

    def put(self, i, lanes):
        self.st[0, i:i + 1] = jnp.sum(lanes.T, axis=0, keepdims=True)

    def start(self):
        for i in range(3):
            self.copy(i).start()

    def total(self):
        for i in range(3):
            self.copy(i).wait()
        return (self.st[0] + self.st[1]) + (self.st[2] + self.st[3])


def params(cid, vmem_mib=60.0):
    return pltpu.CompilerParams(collective_id=cid, has_side_effects=True, vmem_limit_bytes=int(vmem_mib * 1024 * 1024))


COST = pl.CostEstimate(flops=10 ** 11, bytes_accessed=10 ** 8, transcendentals=0)
DMA = pltpu.SemaphoreType.DMA
IN_VMEM = pl.BlockSpec(memory_space=pltpu.VMEM)
IN_HBM = pl.BlockSpec(memory_space=pl.ANY)
SDS = jax.ShapeDtypeStruct


SCALE = HEAD_DIM ** -0.5
TN = (((0,), (0,)), ((), ()))
NT = (((1,), (1,)), ((), ()))
W_SLOTS = (0, 1, 2, 0, 1)


def rope_turn(u, cos_tab, sin_tab):
    return u * cos_tab + pltpu.roll(u, 64, 1) * sin_tab


def causal_scores(q_blk, keys, i, n):
    s = lax.dot_general(q_blk, keys, NT, preferred_element_type=F32) * SCALE
    rows = lax.broadcasted_iota(jnp.int32, (128, n), 0) + i * 128
    return jnp.where(rows >= lax.broadcasted_iota(jnp.int32, (128, n), 1), s, -1e30)


def inv_column(total, i):
    return lax.rsqrt(total.T[:, i:i + 1] / 4096.0 + RMS_EPSILON)


def forward_kernel(wq_in, wk_in, wv_in, wo_in, x_in, gy_in, gq_in, gk_in, gp_in, cos_tab, sin_tab,
                   wq_out, wk_out, wv_out, x_t, q_out, k_out, v_out, qr_out, kr_out, y_out, a_out, p_out, go_out, gains, stats, post,
                   w, x_full, xt, gyc, xcv, qkv, gains_in, a_acc, o_full, ga_all, gtw, sq, st, st2, r1, s0, a_seg, stage,
                   ld, xls, xs, xr, xfs, xfr, gls, gys, gyr, sts, strv, sts2, strv2, wos, xps, xpr, xst, outs,
                   g1s, g1r, g2s, g2r, g3s, g3r, free,
                   scs, scr, osd, orv, ofs, ofr, ops, opr, gsd, grv, gfs, gfr, gps, gpr, s1s, s1r, sgs, *ring):
    w_in, w_out, qkv_out = (wq_in, wk_in, wv_in, wo_in), (wq_out, wk_out, wv_out), (q_out, k_out, v_out)
    nw = 3
    cols_m, rows_m = 3, 4
    g = Torus()
    x, z, y, c, p1, p2 = g.x, g.z, g.y, g.c, g.p1, g.p2
    rings = WeightRings(g, w, W_SLOTS, ring)
    plane = [(x, mod4(z + d), y, c) for d in (1, 2, 3)] + [(x, z, mod4(y + d), c) for d in (1, 2, 3)] + [g.partner]
    ready = greet(plane + [g.xdev(1), g.xdev(-1), g.xdev(2)])

    def load(m, k):
        src = w_in[m].at[:, at256(k * 1024 + x * SEG)]
        return pltpu.make_async_copy(src, w.at[W_SLOTS[m], rings.my_rows, pl.ds(k * SEG, SEG)], ld.at[m])

    def load_wait(m):
        ref = w.at[W_SLOTS[m], rings.my_rows]
        pltpu.make_async_copy(ref, ref, ld.at[m]).wait()

    def xseg(b, s):
        return x_full.at[at128(b * 128), pl.ds(s * 1024, 1024)]

    x_own = pltpu.make_async_copy(x_in, x_full.at[at128(x * 128)], xls)

    def xsend(di, s):
        ref = xseg(x, s)
        return remote(ref, ref, xs, xr.at[di, s], g.xdev(DIRS[di]))

    def xfwd(s):
        d = DIRS[s // 2]
        ref = xseg(mod4(x - d), s)
        return remote(ref, ref, xfs, xfr.at[s], g.xdev(d))

    gy_rows = at128(x * 128)

    def gy_own(k):
        return pltpu.make_async_copy(gy_in.at[:, at256(k * 1024 + x * SEG)], gyc.at[gy_rows, pl.ds(k * SEG, SEG)], gls)

    def gy_send(i, k):
        d = (1, -1, 2)[i]
        src = gy_in.at[:, at256(k * 1024 + mod4(x + d) * SEG)]
        return remote(src, gyc.at[gy_rows, pl.ds(k * SEG, SEG)], gys, gyr, g.xdev(d))

    def gblock(zh, ch):
        return gains.at[:, at128(zh * SEG + ch * 128)]

    def gain1(d):
        return remote(gains_in, gblock(z, c), g1s, g1r, (x, z, mod4(y + d), c))

    def gain2(d):
        ref = gblock(z, c)
        return remote(ref, ref, g2s, g2r, (x, mod4(z + d), y, c))

    def gain3(zh):
        ref = gblock(zh, c)
        return remote(ref, ref, g3s, g3r, g.partner)

    stat = StatExchange(g, st, sts, strv)
    stat2 = StatExchange(g, st2, sts2, strv2)

    def xt_pair(b):
        return remote(xt.at[lax.rem(b, 2)], x_t.at[pl.ds(pl.multiple_of(b * 1024, 1024), 1024), pl.ds(512, 512)], xps.at[b], xpr.at[b], g.partner)

    def xt_store(b):
        return pltpu.make_async_copy(xt.at[lax.rem(b, 2)], x_t.at[pl.ds(pl.multiple_of(b * 1024, 1024), 1024), pl.ds(0, 512)], xst.at[b])

    def turn(b):
        @pl.when(b >= 2)
        def _():
            xt_pair(b - 2).wait_send()
            xt_store(b - 2).wait()

        def step(i):
            xt[lax.rem(b, 2), at256(i * SEG), :] = x_full[:, at256(b * 1024 + i * SEG)].T
        loop(0, 4, step)
        xt_pair(b).start()
        xt_store(b).start()

    def w_store(m, theirs):
        cols = pl.ds(pl.multiple_of(((1 - c) if theirs else c) * 512, 512), 512)
        return pltpu.make_async_copy(w.at[m, :, cols], w_out[m].at[:, cols], wos.at[m, int(theirs)])

    def qkv_store(m):
        return pltpu.make_async_copy(qkv.at[m], qkv_out[m], outs.at[m])

    rot_store = [pltpu.make_async_copy(qkv.at[0], qr_out, outs.at[3]), pltpu.make_async_copy(qkv.at[1], kr_out, outs.at[4])]
    y_store = pltpu.make_async_copy(xcv, y_out, outs.at[5])
    a_store = pltpu.make_async_copy(a_seg, a_out, outs.at[6])
    go_store = pltpu.make_async_copy(qkv.at[0], go_out, outs.at[7])

    st[0] = jnp.zeros((8, 512), F32)
    st2[0] = jnp.zeros((8, 512), F32)
    sq[...] = jnp.zeros((2, 512, 128), F32)
    gains_in[...] = jnp.concatenate([gq_in[...], gk_in[...], gp_in[...], jnp.zeros((5, 128), F32)], axis=0)
    for k in range(4):
        load(0, k).start()
    x_own.start()
    for m in range(1, nw):
        for k in range(4):
            load(m, k).start()
    for k in range(4):
        gy_own(k).start()
    ready()
    for m in range(nw):
        load_wait(m)
        rings.pair_send(m).start()
        if m == 0:
            x_own.wait()
            for s in range(4):
                for di in range(2):
                    xsend(di, (s + 2 * di) % 4).start()

    @pl.when(y == x)
    def _():
        gains[:, at128(z * SEG + c * 128)] = gains_in[...]
        for d in (1, 2, 3):
            gain1(d).start()

    def chunk(m, theirs, i):
        cols = at256((2 * ((1 - c) if theirs else c) + i) * SEG)
        acc_ref = a_acc.at[:, pl.ds(0, SEG)]

        def accumulate(kc):
            rows = pl.ds(pl.multiple_of(kc * 2048, 2048), 2048)
            acc_ref[...] = acc_ref[...] + jnp.dot(x_full[:, rows], w[m, rows, cols], preferred_element_type=F32)
        acc_ref[...] = jnp.zeros((512, SEG), F32)
        loop(0, 2, accumulate)
        acc = acc_ref[...].astype(BF16)
        qkv[m, :, cols] = acc
        if m < 2:
            sqv = acc.astype(F32)
            sqv = sqv * sqv
            sq[m] = sq[m] + (sqv[:, :128] + sqv[:, 128:])

    def chunk_beside(m, theirs):
        return lambda jj: pl.when(lax.rem(jj, 2) == 1)(lambda: chunk(m, theirs, jj // 2))

    rings.first(0, True)
    rings.first(1)
    for u in range(3):
        rings.second(0, u, True)

    def beside(m, t):
        if (m, t) == (1, 1):
            own = chunk_beside(0, False)

            def both(jj):
                turn(jj)
                own(jj)
            return both
        return {(1, 2): chunk_beside(0, True), (2, 0): chunk_beside(1, False), (2, 1): chunk_beside(1, True)}.get((m, t))

    for m in range(nw):
        for t in range(3):
            if (m, t) == (2, 1):
                rings.pair_done(1)
                w_store(1, True).start()
            rings.round(m, t, beside(m, t))
            if m + 1 < nw:
                rings.second(m + 1, t)
            if (m, t) == (0, 0):
                @pl.when(y != x)
                def _():
                    remote(gains_in, gblock(z, c), g1s, g1r, g.partner).wait_recv()
                for d in (1, 2, 3):
                    gain2(d).start()
            if (m, t) == (0, 1):
                rings.first(2)
                for s in range(4):
                    xsend(s // 2, s).wait_recv()
                    xfwd(s).start()
                for k in range(4):
                    for i in range(3):
                        gy_send(i, k).start()
            if (m, t) == (0, 2):
                w_store(0, False).start()
                gain_rest = gains.at[:, pl.ds(0, 384)]
                remote(gain_rest, gain_rest, g2s, g2r, g.partner).wait()
                for zh in range(4):
                    gain3(zh).start()
            if (m, t) == (1, 0):
                rings.pair_done(0)
                w_store(0, True).start()
                for s in range(4):
                    xsend(1 - s // 2, s).wait_recv()
                    xfwd(s).wait_recv()
            if (m, t) == (1, 2):
                w_store(1, False).start()
                qkv_store(0).start()
                for k in range(4):
                    xcv[:, pl.ds(k * SEG, SEG)] = x_full[:, at256(k * 1024 + x * SEG)]
                rings.drain(0)
                w_store(0, False).wait()
                w_store(0, True).wait()
                for k in range(4):
                    load(cols_m, k).start()
            if (m, t) == (2, 1):
                qkv_store(1).start()
                for i in range(2):
                    stat.put(i, sq[i])
                stat.start()
                rings.drain(1)
                w_store(1, False).wait()
                w_store(1, True).wait()
                half_x, quarter_x = x_full.at[:, pl.ds(0, 2048)], x_full.at[:, pl.ds(0, 1024)]
                remote(half_x, half_x, xs, xr.at[0, 0], g.partner).wait_send()
                remote(quarter_x, quarter_x, xfs, xr.at[0, 0], g.partner).wait_send()
                for peer in plane:
                    pl.semaphore_signal(free, inc=1, device_id=peer, device_id_type=MESH_ID)
                qkv_store(0).wait()

    load_wait(cols_m)
    pl.semaphore_wait(free, len(plane))
    rings.pair_send(cols_m).start()

    def scatter(d):
        to = mod4(y + d)
        dst = w.at[1, at128(z * 1024 + to * SEG + c * 128)]
        return remote(wo_in.at[:, pl.ds(pl.multiple_of(to * 1024, 1024), 1024)], dst, scs.at[d], scr, (x, z, to, c))

    own_rows = pltpu.make_async_copy(wo_in.at[:, pl.ds(pl.multiple_of(y * 1024, 1024), 1024)], w.at[1, rings.my_rows], scs.at[0])

    @pl.when(y == x)
    def _():
        own_rows.start()
        for d in (1, 3, 2):
            scatter(d).start()
    w_store(2, False).start()
    total = stat.total()
    stats[...] = total
    inv_q, inv_k = inv_column(total, 0), inv_column(total, 1)
    loop(0, 2, lambda i: chunk(2, False, i))
    rings.first(cols_m, True)
    gain_half = gains.at[:, pl.ds(0, 512)]
    remote(gain_half, gain_half, g3s, g3r, g.partner).wait()
    qkv_store(1).wait()

    def heads_prep(base):
        def step(i):
            cols = at128((base + i) * 128)
            for j, inv in ((0, inv_q), (1, inv_k)):
                u = qkv[j, :, cols].astype(F32) * inv * gains[j:j + 1, cols]
                qkv[j, :, cols] = rope_turn(u, cos_tab[...], sin_tab[...]).astype(BF16)
        loop(0, 4, step)

    def oblk(k, s):
        return o_full.at[:, at256(k * 1024 + s * SEG)]

    def osend(di, k):
        ref = oblk(k, x)
        return remote(ref, ref, osd, orv.at[di, k], g.xdev(DIRS[di]))

    def ofwd(k, di):
        d = DIRS[di]
        ref = oblk(k, mod4(x - d))
        return remote(ref, ref, ofs, ofr.at[k], g.xdev(d))

    def attend(k):
        for ch in range(2):
            cols = at128(k * SEG + ch * 128)
            qh, kh, vh = qkv[0, :, cols], qkv[1, :, cols], qkv[2, :, cols]
            for i in range(4):
                n = (i + 1) * 128
                s = causal_scores(qh[i * 128:n], kh[:n], i, n)
                e = jnp.exp(s - jnp.max(s, axis=-1, keepdims=True))
                p = (e * (1.0 / jnp.sum(e, axis=-1, keepdims=True))).astype(BF16)
                o = jnp.dot(p, vh[:n], preferred_element_type=F32).astype(BF16)
                o_full[pl.ds(i * 128, 128), at128(k * 1024 + x * SEG + ch * 128)] = o
        for di in range(2):
            osend(di, k).start()

    def cols_items(lo, hi):
        loop(lo, hi, lambda it: rings.item(cols_m, it // 4, lax.rem(it, 4)))

    def o_forward(base):
        for i in range(2):
            osend(i, base + i).wait_recv()
            ofwd(base + i, i).start()

    own_k, pair_k = 2 * c, 2 * (1 - c)

    def groups(half):
        @pl.when(half == 1)
        def _():
            rings.pair_done(2)
            w_store(2, True).start()
            loop(0, 2, lambda i: chunk(2, True, i))
            qkv_store(2).start()
        base = own_k + half * (pair_k - own_k)
        heads_prep(2 * base)

        def one(i):
            attend(base + i)

            @pl.when(half == 0)
            def _():
                @pl.when(i == 0)
                def _():
                    for u in range(3):
                        rings.second(cols_m, u, True)

            @pl.when(half == 1)
            def _():
                for r in range(2):
                    it = 2 * i + r
                    rings.item(cols_m, it // 4, lax.rem(it, 4))
        loop(0, 2, one)
    loop(0, 2, groups)
    rot_store[0].start()
    rot_store[1].start()
    cols_items(4, 8)
    o_forward(own_k)

    @pl.when(y == x)
    def _():
        own_rows.wait()

    @pl.when(y != x)
    def _():
        ref = w.at[1, rings.my_rows]
        remote(ref, ref, scs.at[1], scr, g.partner).wait_recv()
    rings.pair_send(rows_m).start()
    cols_items(8, 12)
    rings.first(rows_m, True)
    o_forward(pair_k)
    rings.pair_done(cols_m)

    def a_part(s, init=False):
        def step(i):
            cols = pl.ds(pl.multiple_of(i * 512, 512), 512)
            acc = None
            for k in range(4):
                dot = jnp.dot(o_full[:, at256(k * 1024 + s * SEG)], w[0, at256(k * 1024 + s * SEG), cols], preferred_element_type=F32)
                acc = dot if acc is None else acc + dot
            a_acc[:, cols] = acc if init else a_acc[:, cols] + acc
        loop(0, 2, step)

    a_part(x, True)
    for k in range(4):
        osend(1 - k % 2, k).wait_recv()
    loop(0, 2, lambda i: a_part(mod4(x + 2 * i - 1)))
    for u in range(3):
        rings.second(rows_m, u, True)
    for k in range(4):
        ofwd(k, k % 2).wait_recv()
    a_part(mod4(x + 2))
    o_oth = x_full
    o_pair = remote(o_full, o_oth, ops, opr, g.partner)
    o_pair.start()
    gy_mine, gy_rest = gyc.at[pl.ds(0, 128)], gyc.at[pl.ds(0, 384)]
    pltpu.make_async_copy(gy_mine, gy_mine, gls).wait()
    remote(gy_rest, gy_rest, gys, gyr, g.partner).wait()

    gpost = gains[2:3, :]
    sq[...] = jnp.zeros((2, 512, 128), F32)

    def a_stats(h):
        cols = at128(h * 128)
        a = a_acc[:, cols].astype(BF16).astype(F32)
        gh = gyc[:, cols].astype(F32) * gains[2:3, cols]
        sq[0] = sq[0] + a * a
        sq[1] = sq[1] + gh * a
    loop(0, 8, a_stats)
    for i in range(2):
        stat2.put(i, sq[i])
    stat2.start()
    rings.round(rows_m, 0)
    total2 = stat2.total()
    inv_a = inv_column(total2, 0)
    mean_a = total2.T[:, 1:2] * inv_a / 4096.0

    def gblk(k, s):
        return ga_all.at[s, :, pl.ds(k * SEG, SEG)]

    def gsend(di, k):
        ref = gblk(k, x)
        return remote(ref, ref, gsd, grv.at[di, k], g.xdev(DIRS[di]))

    def gfwd(k):
        d = DIRS[k % 2]
        ref = gblk(k, mod4(x - d))
        return remote(ref, ref, gfs, gfr.at[k], g.xdev(d))

    theirs = pl.ds(pl.multiple_of((1 - c) * 512, 512), 512)
    mine = pl.ds(pl.multiple_of(c * 512, 512), 512)
    ga_pair = remote(ga_all.at[x, :, theirs], gtw.at[pl.ds(512, 512)], gps, gpr, g.partner)

    for k in range(4):
        cols = pl.ds(k * SEG, SEG)
        a_hat = a_acc[:, cols].astype(BF16).astype(F32) * inv_a
        gyv = gyc[:, cols].astype(F32)
        ga_all[x, :, cols] = (inv_a * (gyv * gpost[:, k * SEG:(k + 1) * SEG] - a_hat * mean_a)).astype(BF16)
        for di in range(2):
            gsend(di, k).start()
    ga_pair.start()
    gtw[0:512] = ga_all[x, :, mine]
    for k in range(4):
        cols = pl.ds(k * SEG, SEG)
        a_hat = a_acc[:, cols].astype(BF16).astype(F32) * inv_a
        xcv[:, cols] = (xcv[:, cols].astype(F32) + a_hat * gpost[:, k * SEG:(k + 1) * SEG]).astype(BF16)
        post[0:1, cols] = jnp.sum(gyc[:, cols].astype(F32) * a_hat, axis=0, keepdims=True)
    y_store.start()
    o_pair.wait_recv()
    ga_pair.wait_recv()

    def slot(kk, t, jj):
        return a_seg.at[kk, jj] if t == 2 else r1.at[kk, t, jj]

    def send1(t, kk, jj):
        src = s0.at[kk, jj] if t == 0 else slot(kk, t - 1, jj)
        return remote(src, slot(kk, t, jj), s1s.at[t], s1r.at[t, jj], g.axis1(1 - 2 * kk))

    def p_store(kk, tt, jj):
        d = 1 - 2 * kk
        rows = g.seg_rows(mod4(p1 - d * (1 + tt)), mod4(p2 - d * (1 + jj)))
        par = lax.rem(jj, 2)
        return pltpu.make_async_copy(stage.at[kk, par], p_out.at[rows, at128(kk * 128)], sgs.at[par])

    def p_wait(par):
        pltpu.make_async_copy(stage.at[pl.ds(0, 2), par], stage.at[pl.ds(0, 2), par], sgs.at[par]).wait()

    def tile(kk, tt, jj):
        d = 1 - 2 * kk
        cols = g.seg_rows(mod4(p1 - d * (1 + tt)), mod4(p2 - d * (1 + jj)))
        right = at256(kk * SEG)
        full = (lax.dot_general(o_full[:, cols], gtw[0:512, right], TN, preferred_element_type=F32)
                + lax.dot_general(o_oth[:, cols], gtw[512:1024, right], TN, preferred_element_type=F32))
        stage[kk, lax.rem(jj, 2)] = full[:, 128:]
        p_store(kk, tt, jj).start()
        return full[:, :128]

    def start_item(jj):
        pl.when(jj >= 2)(lambda: p_wait(lax.rem(jj, 2)))

        def color(kk):
            s0[kk, jj] = tile(kk, 0, jj)
            send1(0, kk, jj).start()
        loop(0, 2, color)

    def ring_item(t, jj):
        p_wait(lax.rem(jj, 2))
        ref = a_seg.at[0, pl.ds(0, 2)]
        remote(ref, ref, s1s.at[t], s1r.at[t, jj], g.partner).wait_recv()

        def color(kk):
            dst = slot(kk, t, jj)
            dst[...] = dst[...] + tile(kk, t + 1, jj)
            if t < 2:
                send1(t + 1, kk, jj).start()
        loop(0, 2, color)

    loop(0, 4, start_item)
    rings.round(rows_m, 1)
    loop(0, 4, lambda jj: ring_item(0, jj))
    rings.round(rows_m, 2)

    def g_forward(lo):
        for k in (lo, lo + 1):
            gsend(k % 2, k).wait_recv()
            gfwd(k).start()

    g_forward(0)
    rings.pair_done(rows_m)
    g_forward(2)

    def go_part(s, init=False):
        def step(zi):
            cols = at256(zi * SEG)
            acc = None
            for k in range(4):
                dot = lax.dot_general(ga_all[s, :, k * SEG:(k + 1) * SEG], w[1, at256(zi * 1024 + k * SEG), at256(s * SEG)],
                                      NT, preferred_element_type=F32)
                acc = dot if acc is None else acc + dot
            a_acc[:, cols] = acc if init else a_acc[:, cols] + acc
        loop(0, 4, step)

    go_part(x, True)
    loop(0, 4, lambda jj: ring_item(1, jj))
    for k in range(4):
        gsend(1 - k % 2, k).wait_recv()
    loop(0, 2, lambda i: go_part(mod4(x + 2 * i - 1)))
    loop(0, 4, lambda jj: ring_item(2, jj))
    a_store.start()
    @pl.when(y == x)
    def _():
        remote(gain_rest, gain_rest, g1s, g1r, g.partner).wait_send()
        for d in (1, 2, 3):
            scatter(d).wait_send()
    for b in range(4):
        if b >= 2:
            xt_pair(b).wait_send()
            xt_store(b).wait()
        xt_pair(b).wait_recv()
    w_store(2, False).wait()
    w_store(2, True).wait()
    qkv_store(2).wait()
    rot_store[0].wait()
    rot_store[1].wait()
    y_store.wait()
    o_pair.wait_send()
    ga_pair.wait_send()
    both = ga_all.at[pl.ds(0, 2)]
    one = ga_all.at[0]
    remote(both, both, osd, opr, g.partner).wait_send()
    remote(both, both, gsd, opr, g.partner).wait_send()
    remote(one, one, ofs, opr, g.partner).wait_send()
    for m in (2, cols_m, rows_m):
        rings.drain(m)
    for k in range(4):
        gfwd(k).wait_recv()
    go_part(mod4(x + 2))
    qkv[0] = a_acc[...].astype(BF16)
    go_store.start()

    a_store.wait()
    remote(one, one, gfs, opr, g.partner).wait_send()
    for t in range(3):
        remote(a_seg, a_seg, s1s.at[t], opr, g.partner).wait_send()
    p_wait(0)
    p_wait(1)
    go_store.wait()


def forward_pass(w_q, w_k, w_v, w_o, x_tok, gy_tok, gq, gk, gp, cos_tab, sin_tab):
    act = SDS((512, 1024), BF16)
    return pl.pallas_call(
        forward_kernel,
        out_shape=[SDS((4096, 1024), BF16)] * 4 + [act] * 6 + [SDS((2, 4, SEG, 128), F32), SDS((4096, SEG), F32), act]
        + [SDS((8, 1024), F32), SDS((8, 512), F32), SDS((1, 1024), F32)],
        in_specs=[IN_HBM] * 6 + [IN_VMEM] * 5,
        out_specs=[IN_HBM] * 13 + [IN_VMEM] * 3,
        scratch_shapes=[
            pltpu.VMEM((3, 4096, 1024), BF16),
            pltpu.VMEM((512, 4096), BF16),
            pltpu.VMEM((2, 1024, 512), BF16),
            pltpu.VMEM((512, 1024), BF16),
            pltpu.VMEM((512, 1024), BF16),
            pltpu.VMEM((3, 512, 1024), BF16),
            pltpu.VMEM((8, 128), F32),
            pltpu.VMEM((512, 1024), F32),
            pltpu.VMEM((512, 4096), BF16),
            pltpu.VMEM((4, 512, 1024), BF16),
            pltpu.VMEM((1024, 512), BF16),
            pltpu.VMEM((2, 512, 128), F32),
            pltpu.VMEM((4, 8, 512), F32),
            pltpu.VMEM((4, 8, 512), F32),
            pltpu.VMEM((2, 2, 4, SEG, 128), F32),
            pltpu.VMEM((2, 4, SEG, 128), F32),
            pltpu.VMEM((2, 4, SEG, 128), F32),
            pltpu.VMEM((2, 2, SEG, 128), F32),
            DMA((4,)), DMA(()), DMA(()), DMA((2, 4)), DMA(()), DMA((4,)),
            DMA(()), DMA(()), DMA(()), DMA((3,)), DMA((3,)), DMA((3,)), DMA((3,)),
            DMA((3, 2)), DMA((4,)), DMA((4,)), DMA((4,)), DMA((8,)),
            DMA(()), DMA(()), DMA(()), DMA(()), DMA(()), DMA(()), pltpu.SemaphoreType.REGULAR,
            DMA((4,)), DMA(()), DMA(()), DMA((2, 4)), DMA(()), DMA((4,)), DMA(()), DMA(()),
            DMA(()), DMA((2, 4)), DMA(()), DMA((4,)), DMA(()), DMA(()),
            DMA((3,)), DMA((3, 4)), DMA((2,)),
        ] + ring_sems(5),
        compiler_params=params(5, 63.5), cost_estimate=COST, name='forward_pass',
    )(w_q, w_k, w_v, w_o, x_tok, gy_tok, gq, gk, gp, cos_tab, sin_tab)


NU = 4
WOA, WOB = 4, 5


def backward_kernel(q0_in, k0_in, v0_in, q_rot_in, k_rot_in, grad_o_in, stats, gains, cos_tab, sin_tab, gy, post, y_in, aseg_in, p_in,
                    x_t, wq, wk, wv,
                    dwv, dwk, dwq, dwo, y_out, gx_part, gx_out, gain_out,
                    r1, r1h, r2, r2h, r2w, s0, aseg, rg, buf, acts, dall, rt, lt, gxc, p_all, ds_all, lanes, st, ge,
                    s1s, s1t, s1r, s2s, s2r, ags, agr, agx, d2s, d2r, fws, fwr, lws, lts, pls, gs, gr, gls, wls, gxs, acs, ass, dps, dpr, sts, strv,
                    ysd, yrv, yst, e1s, e1r, e2s, e2r, e3s, e3r, e4s, e4r):
    outs = (dwv, dwk, dwq, dwq, dwo, dwo)
    widths = (SEG, SEG, 128, 128, 128, 128)
    shifts = (0, 0, 0, 128, 0, 128)
    weights = (wv, wk, wq)
    g = Torus()
    x, z, y, c, p1, p2 = g.x, g.z, g.y, g.c, g.p1, g.p2
    ready = greet([(x, mod4(z + d), y, c) for d in (1, 2, 3)] + [(x, z, mod4(y + d), c) for d in (1, 2, 3)]
                  + [g.partner, g.xdev(2)] + [g.xdev(d, h) for d in DIRS for h in (0, 1)])

    def block(kk, tt, jj):
        d = 1 - 2 * kk
        return g.seg_rows(mod4(p1 - d * (1 + tt)), mod4(p2 - d * (1 + jj)))

    def aload(n, kk):
        par = lax.rem(n, 2)
        return pltpu.make_async_copy(x_t.at[block(kk, 1 + n // 4, lax.rem(n, 4))], lt.at[0, par, kk], lts.at[0, par])

    def bload(jj, kk):
        par = lax.rem(jj, 2)
        return pltpu.make_async_copy(x_t.at[block(kk, 0, jj)], lt.at[1, par, kk], lts.at[1, par])

    def load_wait(kind, par):
        pltpu.make_async_copy(lt.at[kind, par], lt.at[kind, par], lts.at[kind, par]).wait()

    def tile(kind, m, par, kk):
        cols = pl.ds(pl.multiple_of(kk * SEG + shifts[m], 128), widths[m])
        return jnp.dot(lt[kind, par, kk], rt[min(m, 2), :, cols], preferred_element_type=F32)

    def slot(m, kk, t, jj):
        if m == WOA:
            return aseg.at[kk, jj]
        return r1.at[m, kk, t, jj] if m < 2 else r1h.at[0 if m == 2 else 1, kk, t, jj]

    def slot2(m, kk, u):
        return r2.at[m, kk, u] if m < 2 else r2w.at[kk, u] if m == WOA else r2h.at[0 if m == 2 else 1, kk, u]

    def first_slot(m, kk, jj):
        return s0.at[kk, jj, :, pl.ds(shifts[m], widths[m])]

    def send1(m, t, kk, jj, first=False):
        if m == WOB and first:
            src = p_in.at[block(kk, 0, jj), at128(kk * 128)]
        else:
            src = first_slot(m, kk, jj) if first else slot(m, kk, t - 1, jj)
        ss = s1s.at[m, jj] if first and m < 2 else s1t.at[m if m < NU else NU]
        return remote(src, slot(m, kk, t, jj), ss, s1r.at[m if m < NU else NU, t, jj], g.axis1(1 - 2 * kk))

    def recv1(m, t, jj):
        ref = r1.at[0, 0, 0, pl.ds(0, 2)] if m < 2 else r1h.at[0, 0, 0, pl.ds(0, 2)]
        remote(ref, ref, s1t.at[0], s1r.at[m if m < NU else NU, t, jj], g.partner).wait_recv()

    def send2(m, u, kk):
        return remote(slot(m, kk, 2, u), slot2(m, kk, u), s2s.at[m], s2r.at[m, u], g.axis2(DIRS[kk]))

    def start_item(m, jj):
        load_wait(1, lax.rem(jj, 2))
        if m in (1, 2):
            ref = s0.at[0, pl.ds(0, 2)]
            remote(ref, ref, s1s.at[m - 1, jj], s2r.at[0, 0], g.partner).wait_send()

        def color(kk):
            first_slot(m, kk, jj)[...] = tile(1, m, lax.rem(jj, 2), kk)
            send1(m, 0, kk, jj, True).start()
        loop(0, 2, color)
        for kk in range(2):
            pl.when(jj < 2)(lambda: bload(jj + 2, kk).start())
            if m + 1 < NU:
                pl.when(jj >= 2)(lambda: bload(jj - 2, kk).start())

    def ring_item(m, n):
        t, jj = n // 4, lax.rem(n, 4)
        load_wait(0, lax.rem(n, 2))
        recv1(m, t, jj)

        def color(kk):
            ref = slot(m, kk, t, jj)
            ref[...] = ref[...] + tile(0, m, lax.rem(n, 2), kk)
            pl.when(t < 2)(lambda: send1(m, t + 1, kk, jj).start())
        loop(0, 2, color)
        for kk in range(2):
            pl.when(n < 10)(lambda: aload(n + 2, kk).start())
            if m + 1 < NU:
                pl.when(n >= 10)(lambda: aload(n - 10, kk).start())

    def p_block(n, kk):
        i = lax.rem(n, 4)
        return gxc.at[kk, at256(i // 2 * SEG), at128(SEG + lax.rem(i, 2) * 128)]

    def pload(n, kk):
        src = p_in.at[block(kk, 1 + n // 4, lax.rem(n, 4)), at128(kk * 128)]
        return pltpu.make_async_copy(src, p_block(n, kk), pls.at[lax.rem(n, 4)])

    def wo_item(n):
        t, jj = n // 4, lax.rem(n, 4)
        ref = aseg.at[0, pl.ds(0, 2)]
        pltpu.make_async_copy(ref, ref, pls.at[jj]).wait()
        recv1(WOB, t, jj)

        def color(kk):
            dst = slot(WOB, kk, t, jj)
            dst[...] = dst[...] + p_block(n, kk)[...]
            pl.when(t < 2)(lambda: send1(WOB, t + 1, kk, jj).start())
            pl.when(n < 8)(lambda: pload(n + 4, kk).start())
        loop(0, 2, color)

    def out_cols(k, xs, m=0):
        return pl.ds(pl.multiple_of(k * 1024 + xs * SEG + shifts[m], 128), widths[m])

    def ag_send(m, kk, di, h):
        k = 2 * c + kk
        return remote(slot(m, kk, 2, 3).at[pl.ds(h * 128, 128)], outs[m].at[:, out_cols(k, x, m)], ags.at[m],
                      agr.at[m, di] if di == kk else agx.at[m],
                      g.xdev(DIRS[di], h))

    def pair_send(m, kk):
        src = slot(m, kk, 2, 3).at[at128((1 - c) * 128)]
        return remote(src, outs[m].at[:, out_cols(2 * c + kk, x, m)], d2s.at[m], d2r.at[m], g.partner)

    def own_store(m, kk):
        return pltpu.make_async_copy(slot(m, kk, 2, 3).at[at128(c * 128)], outs[m].at[:, out_cols(2 * c + kk, x, m)], lws.at[m])

    def forward(m, k):
        di = k % 2
        ref = outs[m].at[:, out_cols(k, mod4(x - DIRS[di]), m)]
        return remote(ref, ref, fws.at[m], fwr.at[m], g.xdev(DIRS[di]))

    def phase2(m, u):
        if u > 0:
            ref = r2.at[0, 0, pl.ds(0, 2)] if m < 2 else r2w.at[0, pl.ds(0, 2)]
            remote(ref, ref, s2s.at[m], s2r.at[m, u - 1], g.partner).wait_recv()
        for kk in range(2):
            if u > 0:
                ref = slot(m, kk, 2, u)
                ref[...] = ref[...] + slot2(m, kk, u - 1)[...]
            if u < 3:
                send2(m, u, kk).start()
            else:
                own_store(m, kk).start()
                for di in range(2):
                    for h in range(2):
                        ag_send(m, kk, di, h).start()
                pair_send(m, kk).start()

    def do_forward(m):
        for di in range(2):
            ref = outs[m].at[:, pl.ds(0, 2 * widths[m])]
            remote(ref, ref, ags.at[m], agr.at[m, di], g.partner).wait_recv()
            for k in (di, di + 2):
                forward(m, k).start()

    def bytes_of(m, n, ss, rs):
        ref = outs[m].at[:, pl.ds(0, n * widths[m])]
        return remote(ref, ref, ss, rs, g.partner)

    def drain_slots(m):
        if m != WOA:
            ref = r1.at[m, pl.ds(0, 2), pl.ds(0, 2)] if m < 2 else r1h.at[0]
            remote(ref, ref, s1t.at[m if m < NU else NU], d2r.at[m], g.partner).wait_send()
        bytes_of(m, 12, s2s.at[m], d2r.at[m]).wait_send()
        bytes_of(m, 8, ags.at[m], agx.at[m]).wait_send()
        bytes_of(m, 2, d2s.at[m], d2r.at[m]).wait_send()
        ref = outs[m].at[:, pl.ds(0, 2 * widths[m])]
        pltpu.make_async_copy(ref, ref, lws.at[m]).wait()

    def drain_unit(m):
        if m != WOB:
            drain_slots(m)
        bytes_of(m, 4, ags.at[m], agx.at[m]).wait_recv()
        bytes_of(m, 2, d2s.at[m], d2r.at[m]).wait_recv()
        bytes_of(m, 4, fws.at[m], fwr.at[m]).wait()

    def gcols(kk, jj):
        return pl.ds(pl.multiple_of(kk * 2048 + jj * 512, 512), 512)

    def gsend(t, kk, jj):
        d = DIRS[kk]
        if t == 0:
            src = gx_part.at[at128(mod4(x - d) * 128), gcols(kk, jj)]
        else:
            src = rg.at[kk, t - 1, jj]
        return remote(src, rg.at[kk, t, jj], gs, gr.at[t, jj], g.xdev(d))

    def gbuf(t, kk, jj):
        return (t % 2, at128(jj * 128), pl.ds(kk * 512, 512))

    def gload(t, kk, jj):
        src = gx_part.at[at128(mod4(x - DIRS[kk] * (2 + t)) * 128), gcols(kk, jj)]
        return pltpu.make_async_copy(src, buf.at[gbuf(t, kk, jj)], gls.at[t % 2, jj])

    def gloads(t):
        each(lambda kk, jj: gload(t, kk, jj).start())

    def chunk_rows(e):
        return pl.ds(pl.multiple_of((lax.rem(e, 2) * 4 + e // 2) * 512, 512), 512)

    def wload(e, i):
        par = lax.rem(e, 2)
        return pltpu.make_async_copy(weights[i].at[chunk_rows(e)], acts.at[3 * par + i], wls.at[par])

    def gx_store(e):
        par = lax.rem(e, 2)
        return pltpu.make_async_copy(gxc.at[par], gx_part.at[:, chunk_rows(e)], gxs.at[par])

    def gx_ship(e, kk):
        gx_store(e).wait()
        gsend(0, kk, e // 2).start()

    def gx_chunk(e):
        par = lax.rem(e, 2)
        acc = None
        ref = acts.at[pl.ds(0, 3)]
        pltpu.make_async_copy(ref, ref, wls.at[par]).wait()
        for i in range(3):
            dot = lax.dot_general(dall[i], acts[3 * par + i], NT, preferred_element_type=F32)
            acc = dot if acc is None else acc + dot
        gxc[par] = acc
        gx_store(e).start()

        @pl.when(e < 6)
        def _():
            for i in range(3):
                wload(e + 2, i).start()
        for kk in range(2):
            pl.when(jnp.logical_and(e > 0, lax.rem(e, 2) == 1 - kk))(lambda: gx_ship(e - 1, kk))

    def gx_item(t, jj):
        ref = rg.at[0, 0, pl.ds(0, 2)]
        remote(ref, ref, gs, gr.at[t, jj], g.partner).wait_recv()
        pltpu.make_async_copy(ref, ref, gls.at[t % 2, jj]).wait()
        for kk in range(2):
            total = rg[kk, t, jj] + buf[gbuf(t, kk, jj)]
            if t < 2:
                rg[kk, t, jj] = total
                gsend(t + 1, kk, jj).start()
            else:
                gx_out[:, gcols(kk, jj)] = (total + gy[:, gcols(kk, jj)].astype(F32)).astype(BF16)

    def y_send(i, k):
        d = (1, -1, 2)[i]
        src = y_in.at[at128(mod4(x + d) * 128), pl.ds(k * SEG, SEG)]
        return remote(src, y_out.at[:, out_cols(k, x)], ysd, yrv, g.xdev(d))

    def y_own(k):
        return pltpu.make_async_copy(y_in.at[at128(x * 128), pl.ds(k * SEG, SEG)], y_out.at[:, out_cols(k, x)], yst)

    gain1 = remote(ge.at[0], ge.at[1], e1s, e1r, g.partner)

    def gain2(d):
        return remote(ge.at[8], ge.at[1 + d], e2s.at[d - 1], e2r.at[d - 1], (x, mod4(z + d), y, c))

    def gain3(d):
        return remote(ge.at[9], ge.at[4 + d], e3s.at[d - 1], e3r.at[d - 1], (x, z, mod4(y + d), c))

    my_head = at128(z * SEG + c * 128)

    def gain4(d):
        return remote(ge.at[10, :, my_head], gain_out, e4s.at[d - 1], e4r, g.xdev(d))

    def act_load(i):
        return pltpu.make_async_copy((q0_in, k0_in, v0_in, q_rot_in, k_rot_in, grad_o_in)[i], acts.at[i], acs)

    aseg_load = pltpu.make_async_copy(aseg_in, aseg, ass)
    stat = StatExchange(g, st, sts, strv)
    theirs = pl.ds(pl.multiple_of((1 - c) * 512, 512), 512)
    mine = pl.ds(pl.multiple_of(c * 512, 512), 512)

    def swap(i):
        return remote(dall.at[i, :, theirs], rt.at[i, pl.ds(512, 512)], dps.at[i], dpr.at[i], g.partner)

    def share(i):
        rt[i, 0:512] = dall[i, :, mine]
        swap(i).start()

    aseg_load.start()
    for i in (2, 3, 4, 5, 0, 1):
        act_load(i).start()
    for kk in range(2):
        for jj in range(2):
            bload(jj, kk).start()
            aload(jj, kk).start()
    inv = [gxc.at[0, :, pl.ds(i * 128, 128)] for i in range(2)]
    proj = [gxc.at[1, :, pl.ds(i * 128, 128)] for i in range(2)]
    for i in range(2):
        inv[i][...] = jnp.broadcast_to(inv_column(stats[...], i), (512, 128))
    lanes[...] = jnp.zeros((2, 512, 128), F32)
    st[0] = jnp.zeros((8, 512), F32)
    ge[0] = jnp.zeros((8, 1024), F32)
    ge[0, 2:3] = post[...]

    p_all[...] = jnp.zeros((512, 512), BF16)
    ds_all[...] = jnp.zeros((512, 512), BF16)

    def norm_back(i, src_rows, cols, gn):
        hat = acts[i, src_rows, cols].astype(F32) * inv[i][src_rows, :]
        prod = gn * hat
        gain = gains[i:i + 1, cols]
        buf[i, src_rows, cols] = gn * gain
        lanes[i, src_rows] = lanes[i, src_rows] + prod * gain
        return jnp.sum(prod, axis=0, keepdims=True)

    def head(h):
        cols = at128(h * 128)
        vh, qh, kh, do = (acts[i, :, cols] for i in (2, 3, 4, 5))
        gain_q = None
        for i in range(4):
            n = (i + 1) * 128
            rows = pl.ds(i * 128, 128)
            s = causal_scores(qh[i * 128:n], kh[:n], i, n)
            e = jnp.exp(s - jnp.max(s, axis=-1, keepdims=True))
            p = e * (1.0 / jnp.sum(e, axis=-1, keepdims=True))
            dp = lax.dot_general(do[i * 128:n], vh[:n], NT, preferred_element_type=F32)
            ds = (p * (dp - jnp.sum(p * dp, axis=-1, keepdims=True)) * SCALE).astype(BF16)
            p_all[rows, 0:n] = p.astype(BF16)
            ds_all[rows, 0:n] = ds
            dq = jnp.dot(ds, kh[:n], preferred_element_type=F32)
            part = norm_back(0, rows, cols, rope_turn(dq, cos_tab[rows, :], -sin_tab[rows, :]))
            gain_q = part if gain_q is None else gain_q + part
        ge[0, 0:1, cols] = gain_q
        dall[0, :, cols] = lax.dot_general(p_all[...], do, TN, preferred_element_type=F32).astype(BF16)
        dk = lax.dot_general(ds_all[...], qh, TN, preferred_element_type=F32)
        ge[0, 1:2, cols] = norm_back(1, pl.ds(0, 512), cols, rope_turn(dk, cos_tab[...], -sin_tab[...]))

    def finish(i, m, column):
        proj[i][...] = jnp.broadcast_to(column, (512, 128))

        def step(h):
            cols = at128(h * 128)
            scale = inv[i][...]
            hat = acts[i, :, cols].astype(F32) * scale
            dall[m, :, cols] = (scale * (buf[i, :, cols] - hat * proj[i][...])).astype(BF16)
        loop(0, 8, step)

    ready()
    for jj in range(4):
        for kk in range(2):
            send1(WOB, 0, kk, jj, True).start()
            pload(jj, kk).start()
    aseg_load.wait()
    phase2(WOA, 0)
    for k in range(4):
        for i in range(3):
            y_send(i, k).start()
        y_own(k).start()
    pltpu.make_async_copy(acts, acts, acs).wait()

    def head_step(h):
        head(h)
        wo_item(h)
        pl.when(h == 2)(lambda: phase2(WOA, 1))
        pl.when(h == 4)(lambda: phase2(WOA, 2))
    loop(0, 8, head_step)
    share(0)
    for i in range(2):
        stat.put(i, lanes[i])
    stat.start()
    gain1.start()
    phase2(WOA, 3)
    swap(0).wait_recv()

    def begin(n):
        start_item(0, n - 8)
        wo_item(n)
        pl.when(n == 8)(lambda: phase2(WOB, 0))
        pl.when(n == 10)(lambda: phase2(WOB, 1))
    loop(8, 12, begin)
    total = stat.total().T / 4096.0
    finish(1, 1, total[:, 1:2])
    share(1)
    finish(0, 2, total[:, 0:1])
    share(2)
    for e in range(2):
        for i in range(3):
            wload(e, i).start()
    do_forward(WOA)

    for m in range(NU):
        def early(n, m=m):
            ring_item(m, n)
            prev = m - 1 if m > 0 else WOB
            pl.when(n == 0)(lambda: phase2(prev, 2))
            pl.when(n == 2)(lambda: phase2(prev, 3))
            if m == 0:
                gx_chunk(n)
            elif m == 1:
                pl.when(n >= 4)(lambda: gx_item(1, n - 4))

        loop(0, 8, early)
        if m == 0:
            gx_ship(7, 1)
            gloads(0)
            gloads(1)
            do_forward(WOB)
            drain_slots(WOB)
            gain1.wait_recv()
            ge[8] = ge[0] + ge[1]
            for d in (1, 2, 3):
                gain2(d).start()
            swap(1).wait_recv()
            swap(2).wait_recv()
        if m == 1:
            for d in (1, 2, 3):
                gain2(d).wait_recv()
            ge[9] = (ge[8] + ge[2]) + (ge[3] + ge[4])
            for d in (1, 2, 3):
                gain3(d).start()
        if m == 3:
            do_forward(1)
        if m == 2:
            for d in (1, 2, 3):
                gain3(d).wait_recv()
            ge[10] = (ge[9] + ge[5]) + (ge[6] + ge[7])

            @pl.when(y == x)
            def _():
                gain_out[...] = ge[10, :, my_head]
                for d in (1, 2, 3):
                    gain4(d).start()

        def late(n, m=m):
            if m + 1 < NU:
                start_item(m + 1, n - 8)
            ring_item(m, n)
            pl.when(n == 8)(lambda: phase2(m, 0))
            pl.when(n == 10)(lambda: phase2(m, 1))
            if m in (0, 2):
                gx_item(m, n - 8)

        loop(8, 12, late)
        if m == 0:
            gloads(2)
        if m == 1:
            do_forward(0)
        if m == 3:
            do_forward(2)
    for u in (2, 3):
        phase2(NU - 1, u)
    do_forward(NU - 1)

    @pl.when(y == x)
    def _():
        for d in (1, 2, 3):
            gain4(d).wait_send()

    @pl.when(y != x)
    def _():
        gain4(1).wait_recv()
    gain1.wait_send()
    for d in (1, 2, 3):
        gain2(d).wait_send()
        gain3(d).wait_send()
    y_all, y_mine = y_out.at[:, pl.ds(0, 3072)], y_out.at[:, pl.ds(0, 1024)]
    remote(y_all, y_all, ysd, yrv, g.partner).wait()
    pltpu.make_async_copy(y_mine, y_mine, yst).wait()
    for m in range(NU + 2):
        drain_unit(m)
    most = gx_part.at[:, pl.ds(0, 3072)]
    remote(most, most, gs, gr.at[0, 0], g.partner).wait_send()
    for i in range(3):
        swap(i).wait_send()


def backward_pass(q0, k0, v0, q_rot, k_rot, grad_o, stats, gains, cos_tab, sin_tab, gy, post, y_cols, a_seg, p_rest, x_t, w_q, w_k, w_v):
    return pl.pallas_call(
        backward_kernel,
        out_shape=[SDS((128, 4096), F32)] * 4 + [SDS((128, 4096), BF16), SDS((512, 4096), F32), SDS((128, 4096), BF16), SDS((8, 128), F32)],
        in_specs=[IN_HBM] * 6 + [IN_VMEM] * 6 + [IN_HBM] * 7,
        out_specs=[IN_HBM] * 6 + [IN_VMEM] * 2,
        scratch_shapes=[
            pltpu.VMEM((2, 2, 3, 4, SEG, SEG), F32),
            pltpu.VMEM((2, 2, 3, 4, SEG, 128), F32),
            pltpu.VMEM((2, 2, 3, SEG, SEG), F32),
            pltpu.VMEM((2, 2, 3, SEG, 128), F32),
            pltpu.VMEM((2, 3, SEG, 128), F32),
            pltpu.VMEM((2, 4, SEG, SEG), F32),
            pltpu.VMEM((2, 4, SEG, 128), F32),
            pltpu.VMEM((2, 3, 4, 128, 512), F32),
            pltpu.VMEM((2, 512, 1024), F32),
            pltpu.VMEM((6, 512, 1024), BF16),
            pltpu.VMEM((3, 512, 1024), BF16),
            pltpu.VMEM((3, 1024, 512), BF16),
            pltpu.VMEM((2, 2, 2, SEG, 1024), BF16),
            pltpu.VMEM((2, 512, 512), F32),
            pltpu.VMEM((512, 512), BF16),
            pltpu.VMEM((512, 512), BF16),
            pltpu.VMEM((2, 512, 128), F32),
            pltpu.VMEM((4, 8, 512), F32),
            pltpu.VMEM((11, 8, 1024), F32),
            DMA((2, 4)), DMA((NU + 1,)), DMA((NU + 1, 3, 4)), DMA((NU + 2,)), DMA((NU + 2, 3)),
            DMA((NU + 2,)), DMA((NU + 2, 2)), DMA((NU + 2,)), DMA((NU + 2,)), DMA((NU + 2,)), DMA((NU + 2,)), DMA((NU + 2,)), DMA((NU + 2,)),
            DMA((2, 2)), DMA((4,)), DMA(()), DMA((3, 4)), DMA((2, 4)), DMA((2,)), DMA((2,)), DMA(()), DMA(()),
            DMA((3,)), DMA((3,)), DMA((3,)), DMA((3,)),
            DMA(()), DMA(()), DMA(()), DMA(()), DMA(()), DMA((3,)), DMA((3,)), DMA((3,)), DMA((3,)), DMA((3,)), DMA(()),
        ],
        compiler_params=params(7, 63.9), cost_estimate=COST, name='backward_pass',
    )(q0, k0, v0, q_rot, k_rot, grad_o, stats, gains, cos_tab, sin_tab, gy, post, y_cols, a_seg, p_rest, x_t, w_q, w_k, w_v)


def copy_kernel(*refs):
    n = (len(refs) - 7) // 5
    gain_src, gain_dst, gain_buf, gain_sems = refs[n], refs[2 * n + 1:2 * n + 4], refs[3 * n + 4], refs[5 * n + 5:]
    srcs, dsts, bufs = refs[:n], refs[n + 1:2 * n + 1], refs[2 * n + 4:3 * n + 4]
    loads, stores = refs[3 * n + 5:4 * n + 5], refs[4 * n + 5:5 * n + 5]
    parts = 4

    def rows(i, p):
        step = srcs[i].shape[0] // parts
        return pl.ds(p * step, step)

    def load(i, p):
        return pltpu.make_async_copy(srcs[i].at[rows(i, p)], bufs[i].at[rows(i, p)], loads[i].at[p])

    def store(i, p):
        return pltpu.make_async_copy(bufs[i].at[rows(i, p)], dsts[i].at[rows(i, p)], stores[i].at[p])

    gain_load = pltpu.make_async_copy(gain_src, gain_buf, gain_sems[0])
    gain_stores = [pltpu.make_async_copy(gain_buf.at[pl.ds(i, 1)], gain_dst[i], gain_sems[1].at[i]) for i in range(3)]
    order = [(i, p) for i in range(n) for p in range(parts)]
    gain_load.start()
    for i, p in order:
        load(i, p).start()
    gain_load.wait()
    for copy in gain_stores:
        copy.start()
    for i, p in order:
        load(i, p).wait()
        store(i, p).start()
    for i, p in order:
        store(i, p).wait()
    for copy in gain_stores:
        copy.wait()


def copy_out(gains, *arrays):
    n = len(arrays)
    return pl.pallas_call(
        copy_kernel,
        out_shape=[SDS(a.shape, a.dtype) for a in arrays] + [SDS((1, 128), F32)] * 3,
        in_specs=[IN_HBM] * (n + 1),
        out_specs=[IN_HBM] * (n + 3),
        scratch_shapes=[pltpu.VMEM(a.shape, a.dtype) for a in arrays] + [pltpu.VMEM((8, 128), F32)] + [DMA((4,))] * (2 * n) + [DMA(()), DMA((3,))],
        compiler_params=pltpu.CompilerParams(vmem_limit_bytes=63 * 1024 * 1024), cost_estimate=COST, name='copy_out',
    )(*arrays, gains)


def solution(mesh):
    mesh4 = Mesh(mesh.devices.reshape(4, 4, 4, 2), ('sp', 'z', 'y', 'c'))
    tok_spec = P(FS, 'sp', None)
    row_spec = P(FS, None)
    vec_spec = P(FS)

    def local_step(x, grad_y, wq_rows, wk_rows, wv_rows, wo_rows, gq_rows, gk_rows, gpost_rows):
        x_tok, gy_tok = x[0], grad_y[0]
        cos_tab, sin_tab = rope_tables(4 * x_tok.shape[0])
        w_q, w_k, w_v, x_t, q0, k0, v0, q_rot, k_rot, y_cols, a_seg, p_rest, grad_o, gains, stats, post = forward_pass(
            wq_rows, wk_rows, wv_rows, wo_rows, x_tok, gy_tok, gq_rows[None], gk_rows[None], gpost_rows[None], cos_tab, sin_tab)
        dwv, dwk, dwq, dwo, y, _, grad_x, gn = backward_pass(
            q0, k0, v0, q_rot, k_rot, grad_o, stats, gains, cos_tab, sin_tab, gy_tok, post, y_cols, a_seg, p_rest, x_t, w_q, w_k, w_v)
        dwv, dwk, dwq, dwo, y, grad_x, *gn = copy_out(gn, dwv, dwk, dwq, dwo, y, grad_x)
        return y[None], grad_x[None], dwq, dwk, dwv, dwo, gn[0][0], gn[1][0], gn[2][0]

    return jax.shard_map(local_step, mesh=mesh4,
                         in_specs=(tok_spec, tok_spec, row_spec, row_spec, row_spec, row_spec, vec_spec, vec_spec, vec_spec),
                         out_specs=(tok_spec, tok_spec, row_spec, row_spec, row_spec, row_spec, vec_spec, vec_spec, vec_spec),
                         check_vma=False)
```

time: 1880 us -> 382 us (0.20)
  waiting for transfers between devices: 1240 us -> 0 us
  Pallas kernels: 0 us -> 381 us
  blocking collectives: 277 us -> 0 us
  matrix products: 251 us -> 0 us
  local copies, waits for them, and re-layouts: 43.6 us -> 0 us
  other arithmetic: 25.5 us -> 0 us
  starting transfers between devices: 20.1 us -> 0 us
    reduce_scatter x4 -> x0, waiting for transfers between devices: 835 us -> none  [reduce_rows(): lax.psum_scatter(grad_part, 'fsdp', scatter_dimension=0, tiled=True)]
    pallas_call x0 -> x3, Pallas kernels: none -> 381 us  [the longest x1 190 us: backward_pass(): pl.pallas_call(backward_kernel, out_shape=[SDS((128, 4096), F32)] * 4 + [...]
    all_gather x4 -> x0, waiting for transfers between devices: 274 us -> none  [the longest x1 96.3 us: local_step(): w_q = lax.all_gather(wq_rows, 'fsdp', axis=0, tiled=True)]
    dot_general x17 -> x0, matrix products: 242 us -> none  [the longest x1 23.9 us: local_step(): jnp.einsum('btd,bte->de', x, grad_q_tok, preferred_element_type=jnp.float32)]
    unnamed x1 -> x0, blocking collectives: 127 us -> none
    psum x1 -> x0, waiting for transfers between devices: 108 us -> none  [reduce_rows(): lax.psum(lax.psum_scatter(grad_part, 'fsdp', scatter_dimension=0, tiled=T...]
    all_gather x5 -> x0, blocking collectives: 97 us -> none  [the longest x1 28 us: local_step(): gain_post = lax.all_gather(gpost_rows, 'fsdp', axis=0, tiled=True)]
    all_to_all x3 -> x0, blocking collectives: 37.4 us -> none  [to_tokens(): lax.all_to_all(blocks, 'sp', 1, 2, tiled=True)]
  transfers between devices with their start and end apart: 14 -> 0, of which waited for: 10 -> 0; matrix products, arithmetic and copies ran while one was open for 14% -> 0% of each run, Pallas kernels for 0% -> 0%
where the time goes in v3:
time: 382 us
  Pallas kernels  381 us (100%)
    pallas_call x1, Pallas kernels, backward_pass(): pl.pallas_call(backward_kernel, out_shape=[SDS((128, 4096), F32)] * 4 + [...  190 us
    pallas_call x1, Pallas kernels, forward_pass(): pl.pallas_call(forward_kernel, out_shape=[SDS((4096, 1024), BF16)] * 4 +...  184 us

profile of v3, /device:TPU:1, one launch (start us, length us, event | category | flops | bytes accessed | tf_op | source)
XLA Modules:
  0.0 381.6 jit_solution(4799584137640398577)
XLA Ops:
  0.6 183.6 %forward_pass.1 = (bf16[4096,1024]{1,0:T(8,128)(2,1)}, bf16[4096,1024]{1,0:T(8,128)(2,1)}, bf16[4096,1024]{1,0:T(8,128)(2,1)}, bf16[4096,1024]{1,0:T(8,128)(2,1)...) custom-call(bf16[128,4096]{1,0:T(8,128)(2,1)} %wq_in.1, ...), custom_call_target="tpu_custom_call" | custom-call | flops 99999997952 | bytes 100000000 | tf_op jit(solution)/shard_map/forward_pass/pallas_call | solution.py:771
  184.2 189.9 %backward_pass.1 = (f32[128,4096]{1,0:T(8,128)}, f32[128,4096]{1,0:T(8,128)}, f32[128,4096]{1,0:T(8,128)}, f32[128,4096]{1,0:T(8,128)}, bf16[128,4096]{1,0:T(8,1...) custom-call(bf16[512,1024]{1,0:T(8,128)(2,1)} %get-tuple-element.41.q0_in, ...), custom_call_target="tpu_custom_call" | custom-call | flops 99999997952 | bytes 100000000 | tf_op jit(solution)/shard_map/backward_pass/pallas_call | solution.py:1280
  374.1 7.4 %copy_out.1 = (f32[128,4096]{1,0:T(8,128)}, f32[128,4096]{1,0:T(8,128)}, f32[128,4096]{1,0:T(8,128)}, f32[128,4096]{1,0:T(8,128)}, bf16[128,4096]{1,0:T(8,128)(2...) custom-call(f32[128,4096]{1,0:T(8,128)} %get-tuple-element.57.refs_0_, ...), custom_call_target="tpu_custom_call" | custom-call | flops 99999997952 | bytes 100000000 | tf_op jit(solution)/shard_map/copy_out/pallas_call | solution.py:1352

commit v4 on v3

--- a/solution.py
+++ b/solution.py
@@ -106,7 +106,7 @@
 
     def pair_send(self, m):
         ref = self.w.at[self.slots[m], self.my_rows]
-        return remote(ref, ref, self.d0s.at[m], self.d0r.at[m], self.g.partner)
+        return remote(ref, ref, self.d0s.at[self.slots[m]], self.d0r.at[self.slots[m]], self.g.partner)
 
     def same(self, m, kk, rows, ss, rs, dev):
         ref = self.w.at[self.slots[m], rows, at256((2 * self.g.c + kk) * SEG)]
@@ -118,27 +118,27 @@
 
     def send1(self, m, u, kk):
         g, d = self.g, DIRS[kk]
-        return self.same(m, kk, g.seg_rows(g.p1, mod4(g.p2 - d * u)), self.a1s.at[m], self.a1r.at[m, u], g.axis2(d))
+        return self.same(m, kk, g.seg_rows(g.p1, mod4(g.p2 - d * u)), self.a1s.at[self.slots[m]], self.a1r.at[self.slots[m], u], g.axis2(d))
 
     def far1(self, m, e, kk):
         g = self.g
         rows = g.seg_rows(g.p1, g.p2)
-        return self.same(m, kk, rows, self.a1s.at[m], self.a1r.at[m, e - 1], g.axis2(DIRS[kk] * e))
+        return self.same(m, kk, rows, self.a1s.at[self.slots[m]], self.a1r.at[self.slots[m], e - 1], g.axis2(DIRS[kk] * e))
 
     def fwd1(self, m, u, kk):
         g = self.g
         rows = g.seg_rows(g.p1, mod4(g.p2 - DIRS[kk] * (u + 1)))
-        return self.same(m, kk, rows, self.f3s.at[m], self.f3r.at[m], g.partner)
+        return self.same(m, kk, rows, self.f3s.at[self.slots[m]], self.f3r.at[self.slots[m]], g.partner)
 
     def send2(self, m, t, kk, jj):
         g, d = self.g, DIRS[kk]
         rows = g.seg_rows(mod4(g.p1 - d * t), mod4(g.p2 - d * jj))
-        return self.same(m, kk, rows, self.a2s.at[m], self.a2r.at[m, t, jj], g.axis1(d))
+        return self.same(m, kk, rows, self.a2s.at[self.slots[m]], self.a2r.at[self.slots[m], t, jj], g.axis1(d))
 
     def fwd2(self, m, t, kk, jj):
         g, d = self.g, DIRS[kk]
         rows = g.seg_rows(mod4(g.p1 - d * (t + 1)), mod4(g.p2 - d * jj))
-        return self.same(m, kk, rows, self.f3s.at[m], self.f3r.at[m], g.partner)
+        return self.same(m, kk, rows, self.f3s.at[self.slots[m]], self.f3r.at[self.slots[m]], g.partner)
 
     def first(self, m, far=False):
         self.pair_send(m).wait_recv()
@@ -151,7 +151,7 @@
             self.send2(m, 0, kk, 0).start()
 
     def second(self, m, u, far=False):
-        self.bulk(m, 2, self.a1s.at[m], self.a1r.at[m, u]).wait_recv()
+        self.bulk(m, 2, self.a1s.at[self.slots[m]], self.a1r.at[self.slots[m], u]).wait_recv()
         for kk in range(2):
             if u < 2 and not far:
                 self.send1(m, u + 1, kk).start()
@@ -159,7 +159,7 @@
             self.fwd1(m, u, kk).start()
 
     def item(self, m, t, jj):
-        self.bulk(m, 2, self.a2s.at[m], self.a2r.at[m, t, jj]).wait_recv()
+        self.bulk(m, 2, self.a2s.at[self.slots[m]], self.a2r.at[self.slots[m], t, jj]).wait_recv()
 
         def pass_on():
             for kk in range(2):
@@ -180,12 +180,12 @@
         loop(0, 4, step)
 
     def pair_done(self, m):
-        self.bulk(m, 30, self.f3s.at[m], self.f3r.at[m]).wait_recv()
+        self.bulk(m, 30, self.f3s.at[self.slots[m]], self.f3r.at[self.slots[m]]).wait_recv()
 
     def drain(self, m):
         self.pair_send(m).wait_send()
         for sems, n in ((self.a1s, 6), (self.a2s, 24), (self.f3s, 30)):
-            self.bulk(m, n, sems.at[m], self.f3r.at[m]).wait_send()
+            self.bulk(m, n, sems.at[self.slots[m]], self.f3r.at[self.slots[m]]).wait_send()
 
 
 class StatExchange:
@@ -229,34 +229,46 @@
     return u * cos_tab + pltpu.roll(u, 64, 1) * sin_tab
 
 
-def causal_scores(q_blk, keys, i, n):
-    s = lax.dot_general(q_blk, keys, NT, preferred_element_type=F32) * SCALE
-    rows = lax.broadcasted_iota(jnp.int32, (128, n), 0) + i * 128
-    return jnp.where(rows >= lax.broadcasted_iota(jnp.int32, (128, n), 1), s, -1e30)
+def causal_scores(keys, q_blk, i, n):
+    s = lax.dot_general(keys, q_blk, NT, preferred_element_type=F32) * SCALE
+    query = lax.broadcasted_iota(jnp.int32, (n, 128), 1) + i * 128
+    return jnp.where(query >= lax.broadcasted_iota(jnp.int32, (n, 128), 0), s, -1e30)
 
 
 def inv_column(total, i):
     return lax.rsqrt(total.T[:, i:i + 1] / 4096.0 + RMS_EPSILON)
 
 
-def forward_kernel(wq_in, wk_in, wv_in, wo_in, x_in, gy_in, gq_in, gk_in, gp_in, cos_tab, sin_tab,
-                   wq_out, wk_out, wv_out, x_t, q_out, k_out, v_out, qr_out, kr_out, y_out, a_out, p_out, go_out, gains, stats, post,
-                   w, x_full, xt, gyc, xcv, qkv, gains_in, a_acc, o_full, ga_all, gtw, sq, st, st2, r1, s0, a_seg, stage,
-                   ld, xls, xs, xr, xfs, xfr, gls, gys, gyr, sts, strv, sts2, strv2, wos, xps, xpr, xst, outs,
-                   g1s, g1r, g2s, g2r, g3s, g3r, free,
-                   scs, scr, osd, orv, ofs, ofr, ops, opr, gsd, grv, gfs, gfr, gps, gpr, s1s, s1r, sgs, *ring):
-    w_in, w_out, qkv_out = (wq_in, wk_in, wv_in, wo_in), (wq_out, wk_out, wv_out), (q_out, k_out, v_out)
+def forward_phase(io, keep, w, x_full, xt, gyc, xcv, gains_in, a_acc, o_full, ga_all, gtw, sq, st, st2, r1, p_all, tmp,
+            ld, xls, xs, xr, xfs, xfr, gls, gys, gyr, sts, strv, sts2, strv2, wos, xps, xpr, xst, yst,
+            g1s, g1r, g2s, g2r, g3s, g3r, free,
+            scl, sc1s, sc1r, sc2s, sc2r, osd, orv, ofs, ofr, ops, opr, gsd, grv, gfs, gfr, gps, gpr, s1s, s1r, *ring):
+    (wq_in, wk_in, wv_in, wo_in, x_in, gy_in, gq_in, gk_in, gp_in, cos_tab, sin_tab, wq_out, wk_out, wv_out, x_t, y_cols) = io
+    acts, gains, stats, post, wo_seg, wo_add, wor = keep
+    s0 = wo_add
+    w_in, w_out = (wq_in, wk_in, wv_in, wo_in), (wq_out, wk_out, wv_out)
     nw = 3
     cols_m, rows_m = 3, 4
     g = Torus()
     x, z, y, c, p1, p2 = g.x, g.z, g.y, g.c, g.p1, g.p2
     rings = WeightRings(g, w, W_SLOTS, ring)
     plane = [(x, mod4(z + d), y, c) for d in (1, 2, 3)] + [(x, z, mod4(y + d), c) for d in (1, 2, 3)] + [g.partner]
-    ready = greet(plane + [g.xdev(1), g.xdev(-1), g.xdev(2)])
+    everyone = plane + [g.xdev(1), g.xdev(-1), g.xdev(2)]
+    ready = greet(everyone)
 
     def load(m, k):
         src = w_in[m].at[:, at256(k * 1024 + x * SEG)]
         return pltpu.make_async_copy(src, w.at[W_SLOTS[m], rings.my_rows, pl.ds(k * SEG, SEG)], ld.at[m])
+
+    def rows_y(d):
+        to = mod4(y + d)
+        return remote(wo_in.at[:, at256(to * 1024 + x * SEG)], tmp.at[y], sc1s, sc1r, (x, z, to, c))
+
+    def rows_x(d):
+        return remote(tmp.at[mod4(x + d)], w.at[1, rings.my_rows, at256(x * SEG)], sc2s, sc2r, g.xdev(d))
+
+    tmp_own = pltpu.make_async_copy(wo_in.at[:, at256(y * 1024 + x * SEG)], tmp.at[y], scl)
+    tmp3 = tmp.at[pl.ds(0, 3)]
 
     def load_wait(m):
         ref = w.at[W_SLOTS[m], rings.my_rows]
@@ -325,16 +337,11 @@
         cols = pl.ds(pl.multiple_of(((1 - c) if theirs else c) * 512, 512), 512)
         return pltpu.make_async_copy(w.at[m, :, cols], w_out[m].at[:, cols], wos.at[m, int(theirs)])
 
-    def qkv_store(m):
-        return pltpu.make_async_copy(qkv.at[m], qkv_out[m], outs.at[m])
-
-    rot_store = [pltpu.make_async_copy(qkv.at[0], qr_out, outs.at[3]), pltpu.make_async_copy(qkv.at[1], kr_out, outs.at[4])]
-    y_store = pltpu.make_async_copy(xcv, y_out, outs.at[5])
-    a_store = pltpu.make_async_copy(a_seg, a_out, outs.at[6])
-    go_store = pltpu.make_async_copy(qkv.at[0], go_out, outs.at[7])
+    y_store = pltpu.make_async_copy(xcv, y_cols, yst)
 
     st[0] = jnp.zeros((8, 512), F32)
     st2[0] = jnp.zeros((8, 512), F32)
+    p_all[...] = jnp.zeros((512, 512), BF16)
     sq[...] = jnp.zeros((2, 512, 128), F32)
     gains_in[...] = jnp.concatenate([gq_in[...], gk_in[...], gp_in[...], jnp.zeros((5, 128), F32)], axis=0)
     for k in range(4):
@@ -371,7 +378,7 @@
         acc_ref[...] = jnp.zeros((512, SEG), F32)
         loop(0, 2, accumulate)
         acc = acc_ref[...].astype(BF16)
-        qkv[m, :, cols] = acc
+        acts[m, :, cols] = acc
         if m < 2:
             sqv = acc.astype(F32)
             sqv = sqv * sqv
@@ -431,7 +438,6 @@
                     xfwd(s).wait_recv()
             if (m, t) == (1, 2):
                 w_store(1, False).start()
-                qkv_store(0).start()
                 for k in range(4):
                     xcv[:, pl.ds(k * SEG, SEG)] = x_full[:, at256(k * 1024 + x * SEG)]
                 rings.drain(0)
@@ -440,7 +446,6 @@
                 for k in range(4):
                     load(cols_m, k).start()
             if (m, t) == (2, 1):
-                qkv_store(1).start()
                 for i in range(2):
                     stat.put(i, sq[i])
                 stat.start()
@@ -450,26 +455,21 @@
                 half_x, quarter_x = x_full.at[:, pl.ds(0, 2048)], x_full.at[:, pl.ds(0, 1024)]
                 remote(half_x, half_x, xs, xr.at[0, 0], g.partner).wait_send()
                 remote(quarter_x, quarter_x, xfs, xr.at[0, 0], g.partner).wait_send()
-                for peer in plane:
+                tmp_own.start()
+                for d in (1, 2, 3):
+                    rows_y(d).start()
+                for peer in everyone:
                     pl.semaphore_signal(free, inc=1, device_id=peer, device_id_type=MESH_ID)
-                qkv_store(0).wait()
 
     load_wait(cols_m)
-    pl.semaphore_wait(free, len(plane))
+    pl.semaphore_wait(free, len(everyone))
     rings.pair_send(cols_m).start()
 
-    def scatter(d):
-        to = mod4(y + d)
-        dst = w.at[1, at128(z * 1024 + to * SEG + c * 128)]
-        return remote(wo_in.at[:, pl.ds(pl.multiple_of(to * 1024, 1024), 1024)], dst, scs.at[d], scr, (x, z, to, c))
-
-    own_rows = pltpu.make_async_copy(wo_in.at[:, pl.ds(pl.multiple_of(y * 1024, 1024), 1024)], w.at[1, rings.my_rows], scs.at[0])
-
-    @pl.when(y == x)
-    def _():
-        own_rows.start()
-        for d in (1, 3, 2):
-            scatter(d).start()
+    remote(tmp3, tmp3, sc1s, sc1r, g.partner).wait_recv()
+    tmp_own.wait()
+    for d in (1, -1, 2):
+        rows_x(d).start()
+    w[1, rings.my_rows, at256(x * SEG)] = tmp[x]
     w_store(2, False).start()
     total = stat.total()
     stats[...] = total
@@ -478,14 +478,13 @@
     rings.first(cols_m, True)
     gain_half = gains.at[:, pl.ds(0, 512)]
     remote(gain_half, gain_half, g3s, g3r, g.partner).wait()
-    qkv_store(1).wait()
 
     def heads_prep(base):
         def step(i):
             cols = at128((base + i) * 128)
             for j, inv in ((0, inv_q), (1, inv_k)):
-                u = qkv[j, :, cols].astype(F32) * inv * gains[j:j + 1, cols]
-                qkv[j, :, cols] = rope_turn(u, cos_tab[...], sin_tab[...]).astype(BF16)
+                u = acts[j, :, cols].astype(F32) * inv * gains[j:j + 1, cols]
+                acts[3 + j, :, cols] = rope_turn(u, cos_tab[...], sin_tab[...]).astype(BF16)
         loop(0, 4, step)
 
     def oblk(k, s):
@@ -503,16 +502,21 @@
     def attend(k):
         for ch in range(2):
             cols = at128(k * SEG + ch * 128)
-            qh, kh, vh = qkv[0, :, cols], qkv[1, :, cols], qkv[2, :, cols]
+            qh, kh, vh = acts[3, :, cols], acts[4, :, cols], acts[2, :, cols]
             for i in range(4):
                 n = (i + 1) * 128
-                s = causal_scores(qh[i * 128:n], kh[:n], i, n)
-                e = jnp.exp(s - jnp.max(s, axis=-1, keepdims=True))
-                p = (e * (1.0 / jnp.sum(e, axis=-1, keepdims=True))).astype(BF16)
-                o = jnp.dot(p, vh[:n], preferred_element_type=F32).astype(BF16)
-                o_full[pl.ds(i * 128, 128), at128(k * 1024 + x * SEG + ch * 128)] = o
+                s = causal_scores(kh[:n], qh[i * 128:n], i, n)
+                e = jnp.exp(s - jnp.max(s, axis=0, keepdims=True))
+                p_all[0:n, pl.ds(i * 128, 128)] = (e * (1.0 / jnp.sum(e, axis=0, keepdims=True))).astype(BF16)
+            o = lax.dot_general(p_all[...], vh, TN, preferred_element_type=F32).astype(BF16)
+            o_full[:, at128(k * 1024 + x * SEG + ch * 128)] = o
         for di in range(2):
             osend(di, k).start()
+
+    def o_pair(s):
+        for k in range(4):
+            cols = at256(k * 1024 + s * SEG)
+            remote(o_full.at[:, cols], x_full.at[:, cols], ops, opr, g.partner).start()
 
     def cols_items(lo, hi):
         loop(lo, hi, lambda it: rings.item(cols_m, it // 4, lax.rem(it, 4)))
@@ -524,13 +528,17 @@
 
     own_k, pair_k = 2 * c, 2 * (1 - c)
 
+    rest = w.at[1, rings.my_rows, pl.ds(0, 768)]
+
     def groups(half):
         @pl.when(half == 1)
         def _():
+            remote(rest, rest, sc2s, sc2r, g.partner).wait_recv()
+            rings.pair_send(rows_m).start()
             rings.pair_done(2)
             w_store(2, True).start()
             loop(0, 2, lambda i: chunk(2, True, i))
-            qkv_store(2).start()
+            rings.first(rows_m, True)
         base = own_k + half * (pair_k - own_k)
         heads_prep(2 * base)
 
@@ -551,52 +559,41 @@
                     rings.item(cols_m, it // 4, lax.rem(it, 4))
         loop(0, 2, one)
     loop(0, 2, groups)
-    rot_store[0].start()
-    rot_store[1].start()
     cols_items(4, 8)
     o_forward(own_k)
 
-    @pl.when(y == x)
-    def _():
-        own_rows.wait()
-
-    @pl.when(y != x)
-    def _():
-        ref = w.at[1, rings.my_rows]
-        remote(ref, ref, scs.at[1], scr, g.partner).wait_recv()
-    rings.pair_send(rows_m).start()
+    for u in range(3):
+        rings.second(rows_m, u, True)
     cols_items(8, 12)
-    rings.first(rows_m, True)
     o_forward(pair_k)
     rings.pair_done(cols_m)
+    o_pair(x)
 
     def a_part(s, init=False):
         def step(i):
-            cols = pl.ds(pl.multiple_of(i * 512, 512), 512)
+            cols = at256(i * SEG)
             acc = None
             for k in range(4):
                 dot = jnp.dot(o_full[:, at256(k * 1024 + s * SEG)], w[0, at256(k * 1024 + s * SEG), cols], preferred_element_type=F32)
                 acc = dot if acc is None else acc + dot
             a_acc[:, cols] = acc if init else a_acc[:, cols] + acc
-        loop(0, 2, step)
+        loop(0, 4, step)
 
     a_part(x, True)
     for k in range(4):
         osend(1 - k % 2, k).wait_recv()
+    o_pair(mod4(x + 1))
+    o_pair(mod4(x + 3))
     loop(0, 2, lambda i: a_part(mod4(x + 2 * i - 1)))
-    for u in range(3):
-        rings.second(rows_m, u, True)
+    rings.round(rows_m, 0)
     for k in range(4):
         ofwd(k, k % 2).wait_recv()
     a_part(mod4(x + 2))
     o_oth = x_full
-    o_pair = remote(o_full, o_oth, ops, opr, g.partner)
-    o_pair.start()
     gy_mine, gy_rest = gyc.at[pl.ds(0, 128)], gyc.at[pl.ds(0, 384)]
     pltpu.make_async_copy(gy_mine, gy_mine, gls).wait()
     remote(gy_rest, gy_rest, gys, gyr, g.partner).wait()
 
-    gpost = gains[2:3, :]
     sq[...] = jnp.zeros((2, 512, 128), F32)
 
     def a_stats(h):
@@ -609,10 +606,11 @@
     for i in range(2):
         stat2.put(i, sq[i])
     stat2.start()
-    rings.round(rows_m, 0)
+    rings.round(rows_m, 1)
     total2 = stat2.total()
     inv_a = inv_column(total2, 0)
-    mean_a = total2.T[:, 1:2] * inv_a / 4096.0
+    sq[0] = jnp.broadcast_to(inv_a, (512, 128))
+    sq[1] = jnp.broadcast_to(total2.T[:, 1:2] * inv_a / 4096.0, (512, 128))
 
     def gblk(k, s):
         return ga_all.at[s, :, pl.ds(k * SEG, SEG)]
@@ -620,6 +618,11 @@
     def gsend(di, k):
         ref = gblk(k, x)
         return remote(ref, ref, gsd, grv.at[di, k], g.xdev(DIRS[di]))
+
+    def gsend_start(di, k):
+        for i in range(4):
+            ref = ga_all.at[x, pl.ds(i * 128, 128), at256(k * SEG)]
+            remote(ref, ref, gsd, grv.at[di, k], g.xdev(DIRS[di])).start()
 
     def gfwd(k):
         d = DIRS[k % 2]
@@ -630,83 +633,77 @@
     mine = pl.ds(pl.multiple_of(c * 512, 512), 512)
     ga_pair = remote(ga_all.at[x, :, theirs], gtw.at[pl.ds(512, 512)], gps, gpr, g.partner)
 
-    for k in range(4):
-        cols = pl.ds(k * SEG, SEG)
-        a_hat = a_acc[:, cols].astype(BF16).astype(F32) * inv_a
-        gyv = gyc[:, cols].astype(F32)
-        ga_all[x, :, cols] = (inv_a * (gyv * gpost[:, k * SEG:(k + 1) * SEG] - a_hat * mean_a)).astype(BF16)
+    def send_grad_a(k):
+        def step(i):
+            cols = at128(k * SEG + i * 128)
+            scale = sq[0]
+            a_hat = a_acc[:, cols].astype(BF16).astype(F32) * scale
+            ga_all[x, :, cols] = (scale * (gyc[:, cols].astype(F32) * gains[2:3, cols] - a_hat * sq[1])).astype(BF16)
+        loop(0, 2, step)
         for di in range(2):
-            gsend(di, k).start()
+            gsend_start(di, k)
+    loop(0, 4, send_grad_a)
     ga_pair.start()
+    o_pair(mod4(x + 2))
     gtw[0:512] = ga_all[x, :, mine]
-    for k in range(4):
-        cols = pl.ds(k * SEG, SEG)
-        a_hat = a_acc[:, cols].astype(BF16).astype(F32) * inv_a
-        xcv[:, cols] = (xcv[:, cols].astype(F32) + a_hat * gpost[:, k * SEG:(k + 1) * SEG]).astype(BF16)
+    def finish_y(h):
+        cols = at128(h * 128)
+        a_hat = a_acc[:, cols].astype(BF16).astype(F32) * sq[0]
+        xcv[:, cols] = (xcv[:, cols].astype(F32) + a_hat * gains[2:3, cols]).astype(BF16)
         post[0:1, cols] = jnp.sum(gyc[:, cols].astype(F32) * a_hat, axis=0, keepdims=True)
+    loop(0, 8, finish_y)
     y_store.start()
-    o_pair.wait_recv()
+    rings.round(rows_m, 2)
+    remote(o_full, o_oth, ops, opr, g.partner).wait_recv()
     ga_pair.wait_recv()
 
     def slot(kk, t, jj):
-        return a_seg.at[kk, jj] if t == 2 else r1.at[kk, t, jj]
+        return wo_seg.at[kk, jj] if t == 2 else r1.at[kk, t, jj]
 
     def send1(t, kk, jj):
-        src = s0.at[kk, jj] if t == 0 else slot(kk, t - 1, jj)
-        return remote(src, slot(kk, t, jj), s1s.at[t], s1r.at[t, jj], g.axis1(1 - 2 * kk))
-
-    def p_store(kk, tt, jj):
-        d = 1 - 2 * kk
-        rows = g.seg_rows(mod4(p1 - d * (1 + tt)), mod4(p2 - d * (1 + jj)))
-        par = lax.rem(jj, 2)
-        return pltpu.make_async_copy(stage.at[kk, par], p_out.at[rows, at128(kk * 128)], sgs.at[par])
-
-    def p_wait(par):
-        pltpu.make_async_copy(stage.at[pl.ds(0, 2), par], stage.at[pl.ds(0, 2), par], sgs.at[par]).wait()
+        src = s0.at[kk, jj] if t == 0 else r1.at[kk, t - 1, jj]
+        rs = wor.at[jj] if t == 2 else s1r.at[t, jj]
+        return remote(src, slot(kk, t, jj), s1s.at[t], rs, g.axis1(1 - 2 * kk))
 
     def tile(kk, tt, jj):
         d = 1 - 2 * kk
         cols = g.seg_rows(mod4(p1 - d * (1 + tt)), mod4(p2 - d * (1 + jj)))
         right = at256(kk * SEG)
-        full = (lax.dot_general(o_full[:, cols], gtw[0:512, right], TN, preferred_element_type=F32)
+        return (lax.dot_general(o_full[:, cols], gtw[0:512, right], TN, preferred_element_type=F32)
                 + lax.dot_general(o_oth[:, cols], gtw[512:1024, right], TN, preferred_element_type=F32))
-        stage[kk, lax.rem(jj, 2)] = full[:, 128:]
-        p_store(kk, tt, jj).start()
-        return full[:, :128]
 
     def start_item(jj):
-        pl.when(jj >= 2)(lambda: p_wait(lax.rem(jj, 2)))
-
         def color(kk):
             s0[kk, jj] = tile(kk, 0, jj)
             send1(0, kk, jj).start()
         loop(0, 2, color)
 
     def ring_item(t, jj):
-        p_wait(lax.rem(jj, 2))
-        ref = a_seg.at[0, pl.ds(0, 2)]
+        ref = s0.at[0, pl.ds(0, 2)]
         remote(ref, ref, s1s.at[t], s1r.at[t, jj], g.partner).wait_recv()
 
         def color(kk):
-            dst = slot(kk, t, jj)
+            dst = r1.at[kk, t, jj]
             dst[...] = dst[...] + tile(kk, t + 1, jj)
-            if t < 2:
-                send1(t + 1, kk, jj).start()
+            send1(t + 1, kk, jj).start()
         loop(0, 2, color)
 
-    loop(0, 4, start_item)
-    rings.round(rows_m, 1)
-    loop(0, 4, lambda jj: ring_item(0, jj))
-    rings.round(rows_m, 2)
+    def last_tiles(jj):
+        def color(kk):
+            wo_add[kk, jj] = tile(kk, 3, jj)
+        loop(0, 2, color)
 
     def g_forward(lo):
         for k in (lo, lo + 1):
             gsend(k % 2, k).wait_recv()
             gfwd(k).start()
 
+    loop(0, 4, start_item)
     g_forward(0)
+    loop(0, 2, lambda jj: ring_item(0, jj))
+    g_forward(2)
+    loop(2, 4, lambda jj: ring_item(0, jj))
     rings.pair_done(rows_m)
-    g_forward(2)
 
     def go_part(s, init=False):
         def step(zi):
@@ -724,13 +721,13 @@
     for k in range(4):
         gsend(1 - k % 2, k).wait_recv()
     loop(0, 2, lambda i: go_part(mod4(x + 2 * i - 1)))
-    loop(0, 4, lambda jj: ring_item(2, jj))
-    a_store.start()
+    remote(s0, s0, s1s.at[0], opr, g.partner).wait_send()
+    loop(0, 4, last_tiles)
     @pl.when(y == x)
     def _():
         remote(gain_rest, gain_rest, g1s, g1r, g.partner).wait_send()
-        for d in (1, 2, 3):
-            scatter(d).wait_send()
+    remote(tmp3, tmp3, sc1s, sc1r, g.partner).wait_send()
+    remote(rest, rest, sc2s, sc2r, g.partner).wait_send()
     for b in range(4):
         if b >= 2:
             xt_pair(b).wait_send()
@@ -738,11 +735,8 @@
         xt_pair(b).wait_recv()
     w_store(2, False).wait()
     w_store(2, True).wait()
-    qkv_store(2).wait()
-    rot_store[0].wait()
-    rot_store[1].wait()
     y_store.wait()
-    o_pair.wait_send()
+    remote(o_full, o_oth, ops, opr, g.partner).wait_send()
     ga_pair.wait_send()
     both = ga_all.at[pl.ds(0, 2)]
     one = ga_all.at[0]
@@ -754,75 +748,64 @@
     for k in range(4):
         gfwd(k).wait_recv()
     go_part(mod4(x + 2))
-    qkv[0] = a_acc[...].astype(BF16)
-    go_store.start()
-
-    a_store.wait()
+
+    def keep_grad_o(h):
+        cols = at128(h * 128)
+        acts[5, :, cols] = a_acc[:, cols].astype(BF16)
+    loop(0, 8, keep_grad_o)
+
     remote(one, one, gfs, opr, g.partner).wait_send()
-    for t in range(3):
-        remote(a_seg, a_seg, s1s.at[t], opr, g.partner).wait_send()
-    p_wait(0)
-    p_wait(1)
-    go_store.wait()
-
-
-def forward_pass(w_q, w_k, w_v, w_o, x_tok, gy_tok, gq, gk, gp, cos_tab, sin_tab):
-    act = SDS((512, 1024), BF16)
-    return pl.pallas_call(
-        forward_kernel,
-        out_shape=[SDS((4096, 1024), BF16)] * 4 + [act] * 6 + [SDS((2, 4, SEG, 128), F32), SDS((4096, SEG), F32), act]
-        + [SDS((8, 1024), F32), SDS((8, 512), F32), SDS((1, 1024), F32)],
-        in_specs=[IN_HBM] * 6 + [IN_VMEM] * 5,
-        out_specs=[IN_HBM] * 13 + [IN_VMEM] * 3,
-        scratch_shapes=[
-            pltpu.VMEM((3, 4096, 1024), BF16),
-            pltpu.VMEM((512, 4096), BF16),
-            pltpu.VMEM((2, 1024, 512), BF16),
-            pltpu.VMEM((512, 1024), BF16),
-            pltpu.VMEM((512, 1024), BF16),
-            pltpu.VMEM((3, 512, 1024), BF16),
-            pltpu.VMEM((8, 128), F32),
-            pltpu.VMEM((512, 1024), F32),
-            pltpu.VMEM((512, 4096), BF16),
-            pltpu.VMEM((4, 512, 1024), BF16),
-            pltpu.VMEM((1024, 512), BF16),
-            pltpu.VMEM((2, 512, 128), F32),
-            pltpu.VMEM((4, 8, 512), F32),
-            pltpu.VMEM((4, 8, 512), F32),
-            pltpu.VMEM((2, 2, 4, SEG, 128), F32),
-            pltpu.VMEM((2, 4, SEG, 128), F32),
-            pltpu.VMEM((2, 4, SEG, 128), F32),
-            pltpu.VMEM((2, 2, SEG, 128), F32),
-            DMA((4,)), DMA(()), DMA(()), DMA((2, 4)), DMA(()), DMA((4,)),
-            DMA(()), DMA(()), DMA(()), DMA((3,)), DMA((3,)), DMA((3,)), DMA((3,)),
-            DMA((3, 2)), DMA((4,)), DMA((4,)), DMA((4,)), DMA((8,)),
-            DMA(()), DMA(()), DMA(()), DMA(()), DMA(()), DMA(()), pltpu.SemaphoreType.REGULAR,
-            DMA((4,)), DMA(()), DMA(()), DMA((2, 4)), DMA(()), DMA((4,)), DMA(()), DMA(()),
-            DMA(()), DMA((2, 4)), DMA(()), DMA((4,)), DMA(()), DMA(()),
-            DMA((3,)), DMA((3, 4)), DMA((2,)),
-        ] + ring_sems(5),
-        compiler_params=params(5, 63.5), cost_estimate=COST, name='forward_pass',
-    )(w_q, w_k, w_v, w_o, x_tok, gy_tok, gq, gk, gp, cos_tab, sin_tab)
+    for t in (1, 2):
+        remote(s0, s0, s1s.at[t], opr, g.partner).wait_send()
+
+
+FORWARD_SCRATCH = [
+    pltpu.VMEM((3, 4096, 1024), BF16),
+    pltpu.VMEM((512, 4096), BF16),
+    pltpu.VMEM((2, 1024, 512), BF16),
+    pltpu.VMEM((512, 1024), BF16),
+    pltpu.VMEM((512, 1024), BF16),
+    pltpu.VMEM((8, 128), F32),
+    pltpu.VMEM((512, 1024), F32),
+    pltpu.VMEM((512, 4096), BF16),
+    pltpu.VMEM((4, 512, 1024), BF16),
+    pltpu.VMEM((1024, 512), BF16),
+    pltpu.VMEM((2, 512, 128), F32),
+    pltpu.VMEM((4, 8, 512), F32),
+    pltpu.VMEM((4, 8, 512), F32),
+    pltpu.VMEM((2, 2, 4, SEG, SEG), F32),
+    pltpu.VMEM((512, 512), BF16),
+    pltpu.VMEM((4, 128, SEG), BF16),
+    DMA((4,)), DMA(()), DMA(()), DMA((2, 4)), DMA(()), DMA((4,)),
+    DMA(()), DMA(()), DMA(()), DMA((3,)), DMA((3,)), DMA((3,)), DMA((3,)),
+    DMA((3, 2)), DMA((4,)), DMA((4,)), DMA((4,)), DMA(()),
+    DMA(()), DMA(()), DMA(()), DMA(()), DMA(()), DMA(()), pltpu.SemaphoreType.REGULAR(()),
+    DMA(()), DMA(()), DMA(()), DMA(()), DMA(()), DMA(()), DMA((2, 4)), DMA(()), DMA((4,)), DMA(()), DMA(()),
+    DMA(()), DMA((2, 4)), DMA(()), DMA((4,)), DMA(()), DMA(()),
+    DMA((3,)), DMA((2, 4)),
+] + ring_sems(3)
 
 
 NU = 4
-WOA, WOB = 4, 5
-
-
-def backward_kernel(q0_in, k0_in, v0_in, q_rot_in, k_rot_in, grad_o_in, stats, gains, cos_tab, sin_tab, gy, post, y_in, aseg_in, p_in,
-                    x_t, wq, wk, wv,
-                    dwv, dwk, dwq, dwo, y_out, gx_part, gx_out, gain_out,
-                    r1, r1h, r2, r2h, r2w, s0, aseg, rg, buf, acts, dall, rt, lt, gxc, p_all, ds_all, lanes, st, ge,
-                    s1s, s1t, s1r, s2s, s2r, ags, agr, agx, d2s, d2r, fws, fwr, lws, lts, pls, gs, gr, gls, wls, gxs, acs, ass, dps, dpr, sts, strv,
-                    ysd, yrv, yst, e1s, e1r, e2s, e2r, e3s, e3r, e4s, e4r):
-    outs = (dwv, dwk, dwq, dwq, dwo, dwo)
-    widths = (SEG, SEG, 128, 128, 128, 128)
-    shifts = (0, 0, 0, 128, 0, 128)
+WO = 4
+
+
+def backward_phase(io, keep, r1, r1h, r2, r2h, rg, buf, dall, rt, lt, gxc, p_all, ds_all, lanes, st, ge, gy, gxo,
+            s1s, s1t, s1r, s2s, s2r, ags, agr, agx, d2s, d2r, fws, fwr, lws, lts, gs, gr, gls, wls, gxs, gyl, dps, dpr, sts, strv,
+            e1s, e1r, e2s, e2r, e3s, e3r, e4s):
+    gy_in, cos_tab, sin_tab, wq, wk, wv, x_t, y_cols, dwv, dwk, dwq, dwo, y_out, gx_part, gx_out, gain_out = io
+    acts, gains, stats, post, wo_seg, wo_add, wor, inside, ysd, yrv, yst, e4r = keep
+    s0 = wo_add
+    outs = (dwv, dwk, dwq, dwq, dwo)
+    widths = (SEG, SEG, 128, 128, SEG)
+    shifts = (0, 0, 0, 128, 0)
     weights = (wv, wk, wq)
     g = Torus()
     x, z, y, c, p1, p2 = g.x, g.z, g.y, g.c, g.p1, g.p2
-    ready = greet([(x, mod4(z + d), y, c) for d in (1, 2, 3)] + [(x, z, mod4(y + d), c) for d in (1, 2, 3)]
-                  + [g.partner, g.xdev(2)] + [g.xdev(d, h) for d in DIRS for h in (0, 1)])
+    peers = ([(x, mod4(z + d), y, c) for d in (1, 2, 3)] + [(x, z, mod4(y + d), c) for d in (1, 2, 3)]
+             + [g.partner, g.xdev(2)] + [g.xdev(d, h) for d in DIRS for h in (0, 1)])
+    for peer in peers:
+        pl.semaphore_signal(inside, inc=1, device_id=peer, device_id_type=MESH_ID)
 
     def block(kk, tt, jj):
         d = 1 - 2 * kk
@@ -844,27 +827,24 @@
         return jnp.dot(lt[kind, par, kk], rt[min(m, 2), :, cols], preferred_element_type=F32)
 
     def slot(m, kk, t, jj):
-        if m == WOA:
-            return aseg.at[kk, jj]
-        return r1.at[m, kk, t, jj] if m < 2 else r1h.at[0 if m == 2 else 1, kk, t, jj]
+        if m == WO:
+            return wo_seg.at[kk, jj]
+        return r1.at[m, kk, t, jj] if m < 2 else r1h.at[m - 2, kk, t, jj]
 
     def slot2(m, kk, u):
-        return r2.at[m, kk, u] if m < 2 else r2w.at[kk, u] if m == WOA else r2h.at[0 if m == 2 else 1, kk, u]
+        return r2h.at[m - 2, kk, u] if m in (2, 3) else r2.at[min(m, 2), kk, u]
 
     def first_slot(m, kk, jj):
         return s0.at[kk, jj, :, pl.ds(shifts[m], widths[m])]
 
     def send1(m, t, kk, jj, first=False):
-        if m == WOB and first:
-            src = p_in.at[block(kk, 0, jj), at128(kk * 128)]
-        else:
-            src = first_slot(m, kk, jj) if first else slot(m, kk, t - 1, jj)
-        ss = s1s.at[m, jj] if first and m < 2 else s1t.at[m if m < NU else NU]
-        return remote(src, slot(m, kk, t, jj), ss, s1r.at[m if m < NU else NU, t, jj], g.axis1(1 - 2 * kk))
+        src = first_slot(m, kk, jj) if first else slot(m, kk, t - 1, jj)
+        ss = s1s.at[m, jj] if first and m < 2 else s1t.at[m]
+        return remote(src, slot(m, kk, t, jj), ss, s1r.at[m, t, jj], g.axis1(1 - 2 * kk))
 
     def recv1(m, t, jj):
         ref = r1.at[0, 0, 0, pl.ds(0, 2)] if m < 2 else r1h.at[0, 0, 0, pl.ds(0, 2)]
-        remote(ref, ref, s1t.at[0], s1r.at[m if m < NU else NU, t, jj], g.partner).wait_recv()
+        remote(ref, ref, s1t.at[0], s1r.at[m, t, jj], g.partner).wait_recv()
 
     def send2(m, u, kk):
         return remote(slot(m, kk, 2, u), slot2(m, kk, u), s2s.at[m], s2r.at[m, u], g.axis2(DIRS[kk]))
@@ -899,25 +879,12 @@
             if m + 1 < NU:
                 pl.when(n >= 10)(lambda: aload(n - 10, kk).start())
 
-    def p_block(n, kk):
-        i = lax.rem(n, 4)
-        return gxc.at[kk, at256(i // 2 * SEG), at128(SEG + lax.rem(i, 2) * 128)]
-
-    def pload(n, kk):
-        src = p_in.at[block(kk, 1 + n // 4, lax.rem(n, 4)), at128(kk * 128)]
-        return pltpu.make_async_copy(src, p_block(n, kk), pls.at[lax.rem(n, 4)])
-
-    def wo_item(n):
-        t, jj = n // 4, lax.rem(n, 4)
-        ref = aseg.at[0, pl.ds(0, 2)]
-        pltpu.make_async_copy(ref, ref, pls.at[jj]).wait()
-        recv1(WOB, t, jj)
+    def wo_item(jj):
+        ref = s0.at[0, pl.ds(0, 2)]
+        remote(ref, ref, s1t.at[0], wor.at[jj], g.partner).wait_recv()
 
         def color(kk):
-            dst = slot(WOB, kk, t, jj)
-            dst[...] = dst[...] + p_block(n, kk)[...]
-            pl.when(t < 2)(lambda: send1(WOB, t + 1, kk, jj).start())
-            pl.when(n < 8)(lambda: pload(n + 4, kk).start())
+            wo_seg[kk, jj] = wo_seg[kk, jj] + wo_add[kk, jj]
         loop(0, 2, color)
 
     def out_cols(k, xs, m=0):
@@ -941,9 +908,16 @@
         ref = outs[m].at[:, out_cols(k, mod4(x - DIRS[di]), m)]
         return remote(ref, ref, fws.at[m], fwr.at[m], g.xdev(DIRS[di]))
 
+    def hand_out(m, kk):
+        own_store(m, kk).start()
+        for di in range(2):
+            for h in range(2):
+                ag_send(m, kk, di, h).start()
+        pair_send(m, kk).start()
+
     def phase2(m, u):
         if u > 0:
-            ref = r2.at[0, 0, pl.ds(0, 2)] if m < 2 else r2w.at[0, pl.ds(0, 2)]
+            ref = r2h.at[0, 0, pl.ds(0, 2)] if m in (2, 3) else r2.at[0, 0, pl.ds(0, 2)]
             remote(ref, ref, s2s.at[m], s2r.at[m, u - 1], g.partner).wait_recv()
         for kk in range(2):
             if u > 0:
@@ -952,11 +926,19 @@
             if u < 3:
                 send2(m, u, kk).start()
             else:
-                own_store(m, kk).start()
-                for di in range(2):
-                    for h in range(2):
-                        ag_send(m, kk, di, h).start()
-                pair_send(m, kk).start()
+                hand_out(m, kk)
+
+    def direct2(m, u, kk):
+        return remote(slot(m, kk, 2, u), slot2(m, kk, u), s2s.at[m], s2r.at[m, u], g.axis2(-(1 + u) * DIRS[kk]))
+
+    def last_phase2(m):
+        for u in range(3):
+            ref = r2h.at[0, 0, pl.ds(0, 2)]
+            remote(ref, ref, s2s.at[m], s2r.at[m, u], g.partner).wait_recv()
+        for kk in range(2):
+            ref = slot(m, kk, 2, 3)
+            ref[...] = (ref[...] + slot2(m, kk, 0)[...]) + (slot2(m, kk, 1)[...] + slot2(m, kk, 2)[...])
+            hand_out(m, kk)
 
     def do_forward(m):
         for di in range(2):
@@ -970,9 +952,9 @@
         return remote(ref, ref, ss, rs, g.partner)
 
     def drain_slots(m):
-        if m != WOA:
+        if m != WO:
             ref = r1.at[m, pl.ds(0, 2), pl.ds(0, 2)] if m < 2 else r1h.at[0]
-            remote(ref, ref, s1t.at[m if m < NU else NU], d2r.at[m], g.partner).wait_send()
+            remote(ref, ref, s1t.at[m], d2r.at[m], g.partner).wait_send()
         bytes_of(m, 12, s2s.at[m], d2r.at[m]).wait_send()
         bytes_of(m, 8, ags.at[m], agx.at[m]).wait_send()
         bytes_of(m, 2, d2s.at[m], d2r.at[m]).wait_send()
@@ -980,8 +962,7 @@
         pltpu.make_async_copy(ref, ref, lws.at[m]).wait()
 
     def drain_unit(m):
-        if m != WOB:
-            drain_slots(m)
+        drain_slots(m)
         bytes_of(m, 4, ags.at[m], agx.at[m]).wait_recv()
         bytes_of(m, 2, d2s.at[m], d2r.at[m]).wait_recv()
         bytes_of(m, 4, fws.at[m], fwr.at[m]).wait()
@@ -1024,13 +1005,17 @@
 
     def gx_chunk(e):
         par = lax.rem(e, 2)
-        acc = None
         ref = acts.at[pl.ds(0, 3)]
         pltpu.make_async_copy(ref, ref, wls.at[par]).wait()
-        for i in range(3):
-            dot = lax.dot_general(dall[i], acts[3 * par + i], NT, preferred_element_type=F32)
-            acc = dot if acc is None else acc + dot
-        gxc[par] = acc
+
+        def rows_half(r):
+            rows = at256(r * SEG)
+            acc = None
+            for i in range(3):
+                dot = lax.dot_general(dall[i, rows, :], acts[3 * par + i], NT, preferred_element_type=F32)
+                acc = dot if acc is None else acc + dot
+            gxc[par, rows, :] = acc
+        loop(0, 2, rows_half)
         gx_store(e).start()
 
         @pl.when(e < 6)
@@ -1039,6 +1024,8 @@
                 wload(e + 2, i).start()
         for kk in range(2):
             pl.when(jnp.logical_and(e > 0, lax.rem(e, 2) == 1 - kk))(lambda: gx_ship(e - 1, kk))
+
+    gx_save = pltpu.make_async_copy(gxo, gx_out, gyl)
 
     def gx_item(t, jj):
         ref = rg.at[0, 0, pl.ds(0, 2)]
@@ -1050,15 +1037,15 @@
                 rg[kk, t, jj] = total
                 gsend(t + 1, kk, jj).start()
             else:
-                gx_out[:, gcols(kk, jj)] = (total + gy[:, gcols(kk, jj)].astype(F32)).astype(BF16)
+                gxo[:, gcols(kk, jj)] = (total + gy[:, gcols(kk, jj)].astype(F32)).astype(BF16)
 
     def y_send(i, k):
         d = (1, -1, 2)[i]
-        src = y_in.at[at128(mod4(x + d) * 128), pl.ds(k * SEG, SEG)]
+        src = y_cols.at[at128(mod4(x + d) * 128), pl.ds(k * SEG, SEG)]
         return remote(src, y_out.at[:, out_cols(k, x)], ysd, yrv, g.xdev(d))
 
     def y_own(k):
-        return pltpu.make_async_copy(y_in.at[at128(x * 128), pl.ds(k * SEG, SEG)], y_out.at[:, out_cols(k, x)], yst)
+        return pltpu.make_async_copy(y_cols.at[at128(x * 128), pl.ds(k * SEG, SEG)], y_out.at[:, out_cols(k, x)], yst)
 
     gain1 = remote(ge.at[0], ge.at[1], e1s, e1r, g.partner)
 
@@ -1073,10 +1060,7 @@
     def gain4(d):
         return remote(ge.at[10, :, my_head], gain_out, e4s.at[d - 1], e4r, g.xdev(d))
 
-    def act_load(i):
-        return pltpu.make_async_copy((q0_in, k0_in, v0_in, q_rot_in, k_rot_in, grad_o_in)[i], acts.at[i], acs)
-
-    aseg_load = pltpu.make_async_copy(aseg_in, aseg, ass)
+    gy_load = pltpu.make_async_copy(gy_in, gy, gyl)
     stat = StatExchange(g, st, sts, strv)
     theirs = pl.ds(pl.multiple_of((1 - c) * 512, 512), 512)
     mine = pl.ds(pl.multiple_of(c * 512, 512), 512)
@@ -1088,9 +1072,11 @@
         rt[i, 0:512] = dall[i, :, mine]
         swap(i).start()
 
-    aseg_load.start()
-    for i in (2, 3, 4, 5, 0, 1):
-        act_load(i).start()
+    gy_load.start()
+    for k in range(4):
+        for i in range(3):
+            y_send(i, k).start()
+        y_own(k).start()
     for kk in range(2):
         for jj in range(2):
             bload(jj, kk).start()
@@ -1118,24 +1104,20 @@
     def head(h):
         cols = at128(h * 128)
         vh, qh, kh, do = (acts[i, :, cols] for i in (2, 3, 4, 5))
-        gain_q = None
         for i in range(4):
             n = (i + 1) * 128
-            rows = pl.ds(i * 128, 128)
-            s = causal_scores(qh[i * 128:n], kh[:n], i, n)
-            e = jnp.exp(s - jnp.max(s, axis=-1, keepdims=True))
-            p = e * (1.0 / jnp.sum(e, axis=-1, keepdims=True))
-            dp = lax.dot_general(do[i * 128:n], vh[:n], NT, preferred_element_type=F32)
-            ds = (p * (dp - jnp.sum(p * dp, axis=-1, keepdims=True)) * SCALE).astype(BF16)
-            p_all[rows, 0:n] = p.astype(BF16)
-            ds_all[rows, 0:n] = ds
-            dq = jnp.dot(ds, kh[:n], preferred_element_type=F32)
-            part = norm_back(0, rows, cols, rope_turn(dq, cos_tab[rows, :], -sin_tab[rows, :]))
-            gain_q = part if gain_q is None else gain_q + part
-        ge[0, 0:1, cols] = gain_q
-        dall[0, :, cols] = lax.dot_general(p_all[...], do, TN, preferred_element_type=F32).astype(BF16)
-        dk = lax.dot_general(ds_all[...], qh, TN, preferred_element_type=F32)
-        ge[0, 1:2, cols] = norm_back(1, pl.ds(0, 512), cols, rope_turn(dk, cos_tab[...], -sin_tab[...]))
+            block_i = pl.ds(i * 128, 128)
+            s = causal_scores(kh[:n], qh[i * 128:n], i, n)
+            e = jnp.exp(s - jnp.max(s, axis=0, keepdims=True))
+            p = e * (1.0 / jnp.sum(e, axis=0, keepdims=True))
+            dp = lax.dot_general(vh[:n], do[i * 128:n], NT, preferred_element_type=F32)
+            p_all[0:n, block_i] = p.astype(BF16)
+            ds_all[0:n, block_i] = (p * (dp - jnp.sum(p * dp, axis=0, keepdims=True)) * SCALE).astype(BF16)
+        dall[0, :, cols] = jnp.dot(p_all[...], do, preferred_element_type=F32).astype(BF16)
+        dq = lax.dot_general(ds_all[...], kh, TN, preferred_element_type=F32)
+        dk = jnp.dot(ds_all[...], qh, preferred_element_type=F32)
+        for i, grad in ((0, dq), (1, dk)):
+            ge[0, i:i + 1, cols] = norm_back(i, pl.ds(0, 512), cols, rope_turn(grad, cos_tab[...], -sin_tab[...]))
 
     def finish(i, m, column):
         proj[i][...] = jnp.broadcast_to(column, (512, 128))
@@ -1147,40 +1129,35 @@
             dall[m, :, cols] = (scale * (buf[i, :, cols] - hat * proj[i][...])).astype(BF16)
         loop(0, 8, step)
 
-    ready()
-    for jj in range(4):
-        for kk in range(2):
-            send1(WOB, 0, kk, jj, True).start()
-            pload(jj, kk).start()
-    aseg_load.wait()
-    phase2(WOA, 0)
-    for k in range(4):
-        for i in range(3):
-            y_send(i, k).start()
-        y_own(k).start()
-    pltpu.make_async_copy(acts, acts, acs).wait()
-
-    def head_step(h):
-        head(h)
-        wo_item(h)
-        pl.when(h == 2)(lambda: phase2(WOA, 1))
-        pl.when(h == 4)(lambda: phase2(WOA, 2))
+    def head_step(i):
+        head(i)
+
+        @pl.when(i == 1)
+        def _():
+            pl.semaphore_wait(inside, len(peers))
+            wo_item(0)
+            phase2(WO, 0)
+
+        @pl.when(i == 3)
+        def _():
+            wo_item(1)
+            phase2(WO, 1)
+
+        @pl.when(i == 5)
+        def _():
+            wo_item(2)
+            phase2(WO, 2)
     loop(0, 8, head_step)
     share(0)
     for i in range(2):
         stat.put(i, lanes[i])
     stat.start()
     gain1.start()
-    phase2(WOA, 3)
+    wo_item(3)
     swap(0).wait_recv()
-
-    def begin(n):
-        start_item(0, n - 8)
-        wo_item(n)
-        pl.when(n == 8)(lambda: phase2(WOB, 0))
-        pl.when(n == 10)(lambda: phase2(WOB, 1))
-    loop(8, 12, begin)
+    loop(0, 4, lambda jj: start_item(0, jj))
     total = stat.total().T / 4096.0
+    phase2(WO, 3)
     finish(1, 1, total[:, 1:2])
     share(1)
     finish(0, 2, total[:, 0:1])
@@ -1188,14 +1165,14 @@
     for e in range(2):
         for i in range(3):
             wload(e, i).start()
-    do_forward(WOA)
+    gy_load.wait()
 
     for m in range(NU):
         def early(n, m=m):
             ring_item(m, n)
-            prev = m - 1 if m > 0 else WOB
-            pl.when(n == 0)(lambda: phase2(prev, 2))
-            pl.when(n == 2)(lambda: phase2(prev, 3))
+            if m > 0:
+                pl.when(n == 0)(lambda: phase2(m - 1, 2))
+                pl.when(n == 2)(lambda: phase2(m - 1, 3))
             if m == 0:
                 gx_chunk(n)
             elif m == 1:
@@ -1206,8 +1183,7 @@
             gx_ship(7, 1)
             gloads(0)
             gloads(1)
-            do_forward(WOB)
-            drain_slots(WOB)
+            do_forward(WO)
             gain1.wait_recv()
             ge[8] = ge[0] + ge[1]
             for d in (1, 2, 3):
@@ -1221,6 +1197,7 @@
             for d in (1, 2, 3):
                 gain3(d).start()
         if m == 3:
+            gx_save.start()
             do_forward(1)
         if m == 2:
             for d in (1, 2, 3):
@@ -1237,8 +1214,13 @@
             if m + 1 < NU:
                 start_item(m + 1, n - 8)
             ring_item(m, n)
-            pl.when(n == 8)(lambda: phase2(m, 0))
-            pl.when(n == 10)(lambda: phase2(m, 1))
+            if m < 3:
+                pl.when(n == 8)(lambda: phase2(m, 0))
+                pl.when(n == 10)(lambda: phase2(m, 1))
+            else:
+                for u in range(3):
+                    for kk in range(2):
+                        pl.when(n == 8 + u)(lambda: direct2(m, u, kk).start())
             if m in (0, 2):
                 gx_item(m, n - 8)
 
@@ -1249,8 +1231,7 @@
             do_forward(0)
         if m == 3:
             do_forward(2)
-    for u in (2, 3):
-        phase2(NU - 1, u)
+    last_phase2(NU - 1)
     do_forward(NU - 1)
 
     @pl.when(y == x)
@@ -1268,48 +1249,69 @@
     y_all, y_mine = y_out.at[:, pl.ds(0, 3072)], y_out.at[:, pl.ds(0, 1024)]
     remote(y_all, y_all, ysd, yrv, g.partner).wait()
     pltpu.make_async_copy(y_mine, y_mine, yst).wait()
-    for m in range(NU + 2):
+    for m in range(NU + 1):
         drain_unit(m)
     most = gx_part.at[:, pl.ds(0, 3072)]
     remote(most, most, gs, gr.at[0, 0], g.partner).wait_send()
     for i in range(3):
         swap(i).wait_send()
-
-
-def backward_pass(q0, k0, v0, q_rot, k_rot, grad_o, stats, gains, cos_tab, sin_tab, gy, post, y_cols, a_seg, p_rest, x_t, w_q, w_k, w_v):
+    gx_save.wait()
+
+
+BACKWARD_SCRATCH = [
+    pltpu.VMEM((2, 2, 3, 4, SEG, SEG), F32),
+    pltpu.VMEM((2, 2, 3, 4, SEG, 128), F32),
+    pltpu.VMEM((3, 2, 3, SEG, SEG), F32),
+    pltpu.VMEM((2, 2, 3, SEG, 128), F32),
+    pltpu.VMEM((2, 3, 4, 128, 512), F32),
+    pltpu.VMEM((2, 512, 1024), F32),
+    pltpu.VMEM((3, 512, 1024), BF16),
+    pltpu.VMEM((3, 1024, 512), BF16),
+    pltpu.VMEM((2, 2, 2, SEG, 1024), BF16),
+    pltpu.VMEM((2, 512, 512), F32),
+    pltpu.VMEM((512, 512), BF16),
+    pltpu.VMEM((512, 512), BF16),
+    pltpu.VMEM((2, 512, 128), F32),
+    pltpu.VMEM((4, 8, 512), F32),
+    pltpu.VMEM((11, 8, 1024), F32),
+    pltpu.VMEM((128, 4096), BF16),
+    pltpu.VMEM((128, 4096), BF16),
+    DMA((2, 4)), DMA((NU,)), DMA((NU, 3, 4)), DMA((NU + 1,)), DMA((NU + 1, 3)),
+    DMA((NU + 1,)), DMA((NU + 1, 2)), DMA((NU + 1,)), DMA((NU + 1,)), DMA((NU + 1,)), DMA((NU + 1,)), DMA((NU + 1,)), DMA((NU + 1,)),
+    DMA((2, 2)), DMA(()), DMA((3, 4)), DMA((2, 4)), DMA((2,)), DMA((2,)), DMA(()),
+    DMA((3,)), DMA((3,)), DMA((3,)), DMA((3,)),
+    DMA(()), DMA(()), DMA((3,)), DMA((3,)), DMA((3,)), DMA((3,)), DMA((3,)),
+]
+
+
+def layer_kernel(wq_in, wk_in, wv_in, wo_in, x_in, gy_in, gq_in, gk_in, gp_in, cos_tab, sin_tab,
+                 dwv, dwk, dwq, dwo, y_out, gx_out, wq_out, wk_out, wv_out, x_t, y_cols, gx_part, gain_out,
+                 acts, gains, stats, post, wo_seg, wo_add, wor, inside, ysd, yrv, yst, e4r):
+    keep = (acts, gains, stats, post, wo_seg, wo_add, wor)
+    first = (wq_in, wk_in, wv_in, wo_in, x_in, gy_in, gq_in, gk_in, gp_in, cos_tab, sin_tab, wq_out, wk_out, wv_out, x_t, y_cols)
+    second = (gy_in, cos_tab, sin_tab, wq_out, wk_out, wv_out, x_t, y_cols, dwv, dwk, dwq, dwo, y_out, gx_part, gx_out, gain_out)
+    pl.run_scoped(lambda *refs: forward_phase(first, keep, *refs), *FORWARD_SCRATCH)
+    pl.run_scoped(lambda *refs: backward_phase(second, keep + (inside, ysd, yrv, yst, e4r), *refs), *BACKWARD_SCRATCH)
+
+
+def layer(w_q, w_k, w_v, w_o, x_tok, gy_tok, gq, gk, gp, cos_tab, sin_tab):
+    grad, tok, mat = SDS((128, 4096), F32), SDS((128, 4096), BF16), SDS((4096, 1024), BF16)
     return pl.pallas_call(
-        backward_kernel,
-        out_shape=[SDS((128, 4096), F32)] * 4 + [SDS((128, 4096), BF16), SDS((512, 4096), F32), SDS((128, 4096), BF16), SDS((8, 128), F32)],
-        in_specs=[IN_HBM] * 6 + [IN_VMEM] * 6 + [IN_HBM] * 7,
-        out_specs=[IN_HBM] * 6 + [IN_VMEM] * 2,
+        layer_kernel,
+        out_shape=[grad] * 4 + [tok] * 2 + [mat] * 4 + [SDS((512, 1024), BF16), SDS((512, 4096), F32), SDS((8, 128), F32)],
+        in_specs=[IN_HBM] * 6 + [IN_VMEM] * 5,
+        out_specs=[IN_HBM] * 12 + [IN_VMEM],
         scratch_shapes=[
-            pltpu.VMEM((2, 2, 3, 4, SEG, SEG), F32),
-            pltpu.VMEM((2, 2, 3, 4, SEG, 128), F32),
-            pltpu.VMEM((2, 2, 3, SEG, SEG), F32),
-            pltpu.VMEM((2, 2, 3, SEG, 128), F32),
-            pltpu.VMEM((2, 3, SEG, 128), F32),
+            pltpu.VMEM((6, 512, 1024), BF16),
+            pltpu.VMEM((8, 1024), F32),
+            pltpu.VMEM((8, 512), F32),
+            pltpu.VMEM((1, 1024), F32),
             pltpu.VMEM((2, 4, SEG, SEG), F32),
-            pltpu.VMEM((2, 4, SEG, 128), F32),
-            pltpu.VMEM((2, 3, 4, 128, 512), F32),
-            pltpu.VMEM((2, 512, 1024), F32),
-            pltpu.VMEM((6, 512, 1024), BF16),
-            pltpu.VMEM((3, 512, 1024), BF16),
-            pltpu.VMEM((3, 1024, 512), BF16),
-            pltpu.VMEM((2, 2, 2, SEG, 1024), BF16),
-            pltpu.VMEM((2, 512, 512), F32),
-            pltpu.VMEM((512, 512), BF16),
-            pltpu.VMEM((512, 512), BF16),
-            pltpu.VMEM((2, 512, 128), F32),
-            pltpu.VMEM((4, 8, 512), F32),
-            pltpu.VMEM((11, 8, 1024), F32),
-            DMA((2, 4)), DMA((NU + 1,)), DMA((NU + 1, 3, 4)), DMA((NU + 2,)), DMA((NU + 2, 3)),
-            DMA((NU + 2,)), DMA((NU + 2, 2)), DMA((NU + 2,)), DMA((NU + 2,)), DMA((NU + 2,)), DMA((NU + 2,)), DMA((NU + 2,)), DMA((NU + 2,)),
-            DMA((2, 2)), DMA((4,)), DMA(()), DMA((3, 4)), DMA((2, 4)), DMA((2,)), DMA((2,)), DMA(()), DMA(()),
-            DMA((3,)), DMA((3,)), DMA((3,)), DMA((3,)),
-            DMA(()), DMA(()), DMA(()), DMA(()), DMA(()), DMA((3,)), DMA((3,)), DMA((3,)), DMA((3,)), DMA((3,)), DMA(()),
+            pltpu.VMEM((2, 4, SEG, SEG), F32),
+            DMA((4,)), pltpu.SemaphoreType.REGULAR, DMA(()), DMA(()), DMA(()), DMA(()),
         ],
-        compiler_params=params(7, 63.9), cost_estimate=COST, name='backward_pass',
-    )(q0, k0, v0, q_rot, k_rot, grad_o, stats, gains, cos_tab, sin_tab, gy, post, y_cols, a_seg, p_rest, x_t, w_q, w_k, w_v)
+        compiler_params=params(5, 63.9), cost_estimate=COST, name='layer',
+    )(w_q, w_k, w_v, w_o, x_tok, gy_tok, gq, gk, gp, cos_tab, sin_tab)
 
 
 def copy_kernel(*refs):
@@ -1368,10 +1370,8 @@
     def local_step(x, grad_y, wq_rows, wk_rows, wv_rows, wo_rows, gq_rows, gk_rows, gpost_rows):
         x_tok, gy_tok = x[0], grad_y[0]
         cos_tab, sin_tab = rope_tables(4 * x_tok.shape[0])
-        w_q, w_k, w_v, x_t, q0, k0, v0, q_rot, k_rot, y_cols, a_seg, p_rest, grad_o, gains, stats, post = forward_pass(
+        dwv, dwk, dwq, dwo, y, grad_x, *_, gn = layer(
             wq_rows, wk_rows, wv_rows, wo_rows, x_tok, gy_tok, gq_rows[None], gk_rows[None], gpost_rows[None], cos_tab, sin_tab)
-        dwv, dwk, dwq, dwo, y, _, grad_x, gn = backward_pass(
-            q0, k0, v0, q_rot, k_rot, grad_o, stats, gains, cos_tab, sin_tab, gy_tok, post, y_cols, a_seg, p_rest, x_t, w_q, w_k, w_v)
         dwv, dwk, dwq, dwo, y, grad_x, *gn = copy_out(gn, dwv, dwk, dwq, dwo, y, grad_x)
         return y[None], grad_x[None], dwq, dwk, dwv, dwo, gn[0][0], gn[1][0], gn[2][0]
 

time: 382 us -> 363 us (0.950)
  Pallas kernels: 381 us -> 361 us
    pallas_call x2 -> x1, Pallas kernels: 373 us -> 354 us  [layer(): pl.pallas_call(layer_kernel, out_shape=[grad] * 4 + [tok] * 2 + [mat] * 4...]
where the time goes in v4:
time: 363 us; the launch traced here: 362 us
  Pallas kernels  361 us (99%)
    pallas_call x1, Pallas kernels, layer(): pl.pallas_call(layer_kernel, out_shape=[grad] * 4 + [tok] * 2 + [mat] * 4...  354 us
    pallas_call x1, Pallas kernels, copy_out(): pl.pallas_call(copy_kernel, out_shape=[SDS(a.shape, a.dtype) for a in arr...  7.37 us

profile of v4, /device:TPU:1, one launch (start us, length us, event | category | flops | bytes accessed | tf_op | source)
XLA Modules:
  0.0 362.2 jit_solution(10593950630776537306)
XLA Ops:
  0.6 354.0 %layer.1 = (f32[128,4096]{1,0:T(8,128)}, f32[128,4096]{1,0:T(8,128)}, f32[128,4096]{1,0:T(8,128)}, f32[128,4096]{1,0:T(8,128)}, bf16[128,4096]{1,0:T(8,128)(2,1)...) custom-call(bf16[128,4096]{1,0:T(8,128)(2,1)} %wq_in.1, ...), custom_call_target="tpu_custom_call" | custom-call | flops 99999997952 | bytes 100000000 | tf_op jit(solution)/shard_map/layer/pallas_call | solution.py:1299
  354.7 7.4 %copy_out.1 = (f32[128,4096]{1,0:T(8,128)}, f32[128,4096]{1,0:T(8,128)}, f32[128,4096]{1,0:T(8,128)}, f32[128,4096]{1,0:T(8,128)}, bf16[128,4096]{1,0:T(8,128)(2...) custom-call(f32[128,4096]{1,0:T(8,128)} %get-tuple-element.25.refs_0_, ...), custom_call_target="tpu_custom_call" | custom-call | flops 99999997952 | bytes 100000000 | tf_op jit(solution)/shard_map/copy_out/pallas_call | solution.py:1354

commit v5 on v4

--- a/solution.py
+++ b/solution.py
@@ -244,7 +244,7 @@
             g1s, g1r, g2s, g2r, g3s, g3r, free,
             scl, sc1s, sc1r, sc2s, sc2r, osd, orv, ofs, ofr, ops, opr, gsd, grv, gfs, gfr, gps, gpr, s1s, s1r, *ring):
     (wq_in, wk_in, wv_in, wo_in, x_in, gy_in, gq_in, gk_in, gp_in, cos_tab, sin_tab, wq_out, wk_out, wv_out, x_t, y_cols) = io
-    acts, gains, stats, post, wo_seg, wo_add, wor = keep
+    acts, gains, stats, post, wo_seg, wo_add, wo_mid, wor, wo_sent = keep
     s0 = wo_add
     w_in, w_out = (wq_in, wk_in, wv_in, wo_in), (wq_out, wk_out, wv_out)
     nw = 3
@@ -368,8 +368,8 @@
         for d in (1, 2, 3):
             gain1(d).start()
 
-    def chunk(m, theirs, i):
-        cols = at256((2 * ((1 - c) if theirs else c) + i) * SEG)
+    def chunk(m, half, i):
+        cols = at256((2 * (c + half * (1 - 2 * c)) + i) * SEG)
         acc_ref = a_acc.at[:, pl.ds(0, SEG)]
 
         def accumulate(kc):
@@ -384,27 +384,39 @@
             sqv = sqv * sqv
             sq[m] = sq[m] + (sqv[:, :128] + sqv[:, 128:])
 
-    def chunk_beside(m, theirs):
-        return lambda jj: pl.when(lax.rem(jj, 2) == 1)(lambda: chunk(m, theirs, jj // 2))
+    def chunk_beside(m, half):
+        return lambda jj: pl.when(lax.rem(jj, 2) == 1)(lambda: chunk(m, half, jj // 2))
 
     rings.first(0, True)
     rings.first(1)
     for u in range(3):
         rings.second(0, u, True)
 
+    def prep_pair(jj):
+        def step(i):
+            cols = at128((2 * jj + i) * 128)
+            for j in range(2):
+                u = acts[j, :, cols].astype(F32) * sq[j] * gains[j:j + 1, cols]
+                acts[3 + j, :, cols] = rope_turn(u, cos_tab[...], sin_tab[...]).astype(BF16)
+        loop(0, 2, step)
+
+    def tell(slot):
+        for peer in everyone:
+            pl.semaphore_signal(free.at[slot], inc=1, device_id=peer, device_id_type=MESH_ID)
+
     def beside(m, t):
         if (m, t) == (1, 1):
-            own = chunk_beside(0, False)
+            own = chunk_beside(0, 0)
 
             def both(jj):
                 turn(jj)
                 own(jj)
             return both
-        return {(1, 2): chunk_beside(0, True), (2, 0): chunk_beside(1, False), (2, 1): chunk_beside(1, True)}.get((m, t))
+        return {(1, 2): chunk_beside(0, 1), (2, 0): lambda jj: chunk(1, jj // 2, lax.rem(jj, 2)), (2, 2): prep_pair}.get((m, t))
 
     for m in range(nw):
         for t in range(3):
-            if (m, t) == (2, 1):
+            if (m, t) == (2, 0):
                 rings.pair_done(1)
                 w_store(1, True).start()
             rings.round(m, t, beside(m, t))
@@ -443,12 +455,17 @@
                 rings.drain(0)
                 w_store(0, False).wait()
                 w_store(0, True).wait()
+                tell(0)
                 for k in range(4):
                     load(cols_m, k).start()
-            if (m, t) == (2, 1):
+            if (m, t) == (2, 0):
                 for i in range(2):
                     stat.put(i, sq[i])
                 stat.start()
+                load_wait(cols_m)
+                pl.semaphore_wait(free.at[0], len(everyone))
+                rings.pair_send(cols_m).start()
+            if (m, t) == (2, 1):
                 rings.drain(1)
                 w_store(1, False).wait()
                 w_store(1, True).wait()
@@ -458,35 +475,22 @@
                 tmp_own.start()
                 for d in (1, 2, 3):
                     rows_y(d).start()
-                for peer in everyone:
-                    pl.semaphore_signal(free, inc=1, device_id=peer, device_id_type=MESH_ID)
-
-    load_wait(cols_m)
-    pl.semaphore_wait(free, len(everyone))
-    rings.pair_send(cols_m).start()
-
+                tell(1)
+                gain_half = gains.at[:, pl.ds(0, 512)]
+                remote(gain_half, gain_half, g3s, g3r, g.partner).wait()
+                total = stat.total()
+                stats[...] = total
+                for i in range(2):
+                    sq[i] = jnp.broadcast_to(inv_column(total, i), (512, 128))
+
+    rings.first(cols_m, True)
     remote(tmp3, tmp3, sc1s, sc1r, g.partner).wait_recv()
     tmp_own.wait()
+    pl.semaphore_wait(free.at[1], len(everyone))
     for d in (1, -1, 2):
         rows_x(d).start()
     w[1, rings.my_rows, at256(x * SEG)] = tmp[x]
     w_store(2, False).start()
-    total = stat.total()
-    stats[...] = total
-    inv_q, inv_k = inv_column(total, 0), inv_column(total, 1)
-    loop(0, 2, lambda i: chunk(2, False, i))
-    rings.first(cols_m, True)
-    gain_half = gains.at[:, pl.ds(0, 512)]
-    remote(gain_half, gain_half, g3s, g3r, g.partner).wait()
-
-    def heads_prep(base):
-        def step(i):
-            cols = at128((base + i) * 128)
-            for j, inv in ((0, inv_q), (1, inv_k)):
-                u = acts[j, :, cols].astype(F32) * inv * gains[j:j + 1, cols]
-                acts[3 + j, :, cols] = rope_turn(u, cos_tab[...], sin_tab[...]).astype(BF16)
-        loop(0, 4, step)
-
     def oblk(k, s):
         return o_full.at[:, at256(k * 1024 + s * SEG)]
 
@@ -537,13 +541,12 @@
             rings.pair_send(rows_m).start()
             rings.pair_done(2)
             w_store(2, True).start()
-            loop(0, 2, lambda i: chunk(2, True, i))
-            rings.first(rows_m, True)
         base = own_k + half * (pair_k - own_k)
-        heads_prep(2 * base)
 
         def one(i):
+            chunk(2, half, i)
             attend(base + i)
+            pl.when(jnp.logical_and(half == 1, i == 0))(lambda: rings.first(rows_m, True))
 
             @pl.when(half == 0)
             def _():
@@ -606,7 +609,6 @@
     for i in range(2):
         stat2.put(i, sq[i])
     stat2.start()
-    rings.round(rows_m, 1)
     total2 = stat2.total()
     inv_a = inv_column(total2, 0)
     sq[0] = jnp.broadcast_to(inv_a, (512, 128))
@@ -653,17 +655,16 @@
         post[0:1, cols] = jnp.sum(gyc[:, cols].astype(F32) * a_hat, axis=0, keepdims=True)
     loop(0, 8, finish_y)
     y_store.start()
-    rings.round(rows_m, 2)
     remote(o_full, o_oth, ops, opr, g.partner).wait_recv()
     ga_pair.wait_recv()
 
     def slot(kk, t, jj):
-        return wo_seg.at[kk, jj] if t == 2 else r1.at[kk, t, jj]
+        return (r1, wo_mid, wo_seg)[t].at[kk, jj]
 
     def send1(t, kk, jj):
-        src = s0.at[kk, jj] if t == 0 else r1.at[kk, t - 1, jj]
-        rs = wor.at[jj] if t == 2 else s1r.at[t, jj]
-        return remote(src, slot(kk, t, jj), s1s.at[t], rs, g.axis1(1 - 2 * kk))
+        src = s0.at[kk, jj] if t == 0 else slot(kk, t - 1, jj)
+        ss, rs = (wo_sent, wor.at[jj]) if t == 2 else (s1s.at[t], s1r.at[t, jj])
+        return remote(src, slot(kk, t, jj), ss, rs, g.axis1(1 - 2 * kk))
 
     def tile(kk, tt, jj):
         d = 1 - 2 * kk
@@ -683,7 +684,7 @@
         remote(ref, ref, s1s.at[t], s1r.at[t, jj], g.partner).wait_recv()
 
         def color(kk):
-            dst = r1.at[kk, t, jj]
+            dst = slot(kk, t, jj)
             dst[...] = dst[...] + tile(kk, t + 1, jj)
             send1(t + 1, kk, jj).start()
         loop(0, 2, color)
@@ -699,6 +700,8 @@
             gfwd(k).start()
 
     loop(0, 4, start_item)
+    rings.round(rows_m, 1)
+    rings.round(rows_m, 2)
     g_forward(0)
     loop(0, 2, lambda jj: ring_item(0, jj))
     g_forward(2)
@@ -717,12 +720,13 @@
         loop(0, 4, step)
 
     go_part(x, True)
-    loop(0, 4, lambda jj: ring_item(1, jj))
     for k in range(4):
         gsend(1 - k % 2, k).wait_recv()
     loop(0, 2, lambda i: go_part(mod4(x + 2 * i - 1)))
     remote(s0, s0, s1s.at[0], opr, g.partner).wait_send()
     loop(0, 4, last_tiles)
+    loop(0, 4, lambda jj: ring_item(1, jj))
+
     @pl.when(y == x)
     def _():
         remote(gain_rest, gain_rest, g1s, g1r, g.partner).wait_send()
@@ -755,8 +759,7 @@
     loop(0, 8, keep_grad_o)
 
     remote(one, one, gfs, opr, g.partner).wait_send()
-    for t in (1, 2):
-        remote(s0, s0, s1s.at[t], opr, g.partner).wait_send()
+    remote(s0, s0, s1s.at[1], opr, g.partner).wait_send()
 
 
 FORWARD_SCRATCH = [
@@ -773,16 +776,16 @@
     pltpu.VMEM((2, 512, 128), F32),
     pltpu.VMEM((4, 8, 512), F32),
     pltpu.VMEM((4, 8, 512), F32),
-    pltpu.VMEM((2, 2, 4, SEG, SEG), F32),
+    pltpu.VMEM((2, 4, SEG, SEG), F32),
     pltpu.VMEM((512, 512), BF16),
     pltpu.VMEM((4, 128, SEG), BF16),
     DMA((4,)), DMA(()), DMA(()), DMA((2, 4)), DMA(()), DMA((4,)),
     DMA(()), DMA(()), DMA(()), DMA((3,)), DMA((3,)), DMA((3,)), DMA((3,)),
     DMA((3, 2)), DMA((4,)), DMA((4,)), DMA((4,)), DMA(()),
-    DMA(()), DMA(()), DMA(()), DMA(()), DMA(()), DMA(()), pltpu.SemaphoreType.REGULAR(()),
+    DMA(()), DMA(()), DMA(()), DMA(()), DMA(()), DMA(()), pltpu.SemaphoreType.REGULAR((2,)),
     DMA(()), DMA(()), DMA(()), DMA(()), DMA(()), DMA(()), DMA((2, 4)), DMA(()), DMA((4,)), DMA(()), DMA(()),
     DMA(()), DMA((2, 4)), DMA(()), DMA((4,)), DMA(()), DMA(()),
-    DMA((3,)), DMA((2, 4)),
+    DMA((2,)), DMA((2, 4)),
 ] + ring_sems(3)
 
 
@@ -794,7 +797,7 @@
             s1s, s1t, s1r, s2s, s2r, ags, agr, agx, d2s, d2r, fws, fwr, lws, lts, gs, gr, gls, wls, gxs, gyl, dps, dpr, sts, strv,
             e1s, e1r, e2s, e2r, e3s, e3r, e4s):
     gy_in, cos_tab, sin_tab, wq, wk, wv, x_t, y_cols, dwv, dwk, dwq, dwo, y_out, gx_part, gx_out, gain_out = io
-    acts, gains, stats, post, wo_seg, wo_add, wor, inside, ysd, yrv, yst, e4r = keep
+    acts, gains, stats, post, wo_seg, wo_add, wo_mid, wor, wo_sent, inside, ysd, yrv, yst, e4r = keep
     s0 = wo_add
     outs = (dwv, dwk, dwq, dwq, dwo)
     widths = (SEG, SEG, 128, 128, SEG)
@@ -1132,18 +1135,18 @@
     def head_step(i):
         head(i)
 
-        @pl.when(i == 1)
+        @pl.when(i == 2)
         def _():
             pl.semaphore_wait(inside, len(peers))
             wo_item(0)
             phase2(WO, 0)
 
-        @pl.when(i == 3)
+        @pl.when(i == 4)
         def _():
             wo_item(1)
             phase2(WO, 1)
 
-        @pl.when(i == 5)
+        @pl.when(i == 7)
         def _():
             wo_item(2)
             phase2(WO, 2)
@@ -1157,7 +1160,6 @@
     swap(0).wait_recv()
     loop(0, 4, lambda jj: start_item(0, jj))
     total = stat.total().T / 4096.0
-    phase2(WO, 3)
     finish(1, 1, total[:, 1:2])
     share(1)
     finish(0, 2, total[:, 0:1])
@@ -1165,6 +1167,7 @@
     for e in range(2):
         for i in range(3):
             wload(e, i).start()
+    phase2(WO, 3)
     gy_load.wait()
 
     for m in range(NU):
@@ -1234,6 +1237,7 @@
     last_phase2(NU - 1)
     do_forward(NU - 1)
 
+    remote(wo_mid, wo_mid, wo_sent, yrv, g.partner).wait_send()
     @pl.when(y == x)
     def _():
         for d in (1, 2, 3):
@@ -1286,8 +1290,8 @@
 
 def layer_kernel(wq_in, wk_in, wv_in, wo_in, x_in, gy_in, gq_in, gk_in, gp_in, cos_tab, sin_tab,
                  dwv, dwk, dwq, dwo, y_out, gx_out, wq_out, wk_out, wv_out, x_t, y_cols, gx_part, gain_out,
-                 acts, gains, stats, post, wo_seg, wo_add, wor, inside, ysd, yrv, yst, e4r):
-    keep = (acts, gains, stats, post, wo_seg, wo_add, wor)
+                 acts, gains, stats, post, wo_seg, wo_add, wo_mid, wor, wo_sent, inside, ysd, yrv, yst, e4r):
+    keep = (acts, gains, stats, post, wo_seg, wo_add, wo_mid, wor, wo_sent)
     first = (wq_in, wk_in, wv_in, wo_in, x_in, gy_in, gq_in, gk_in, gp_in, cos_tab, sin_tab, wq_out, wk_out, wv_out, x_t, y_cols)
     second = (gy_in, cos_tab, sin_tab, wq_out, wk_out, wv_out, x_t, y_cols, dwv, dwk, dwq, dwo, y_out, gx_part, gx_out, gain_out)
     pl.run_scoped(lambda *refs: forward_phase(first, keep, *refs), *FORWARD_SCRATCH)
@@ -1308,7 +1312,8 @@
             pltpu.VMEM((1, 1024), F32),
             pltpu.VMEM((2, 4, SEG, SEG), F32),
             pltpu.VMEM((2, 4, SEG, SEG), F32),
-            DMA((4,)), pltpu.SemaphoreType.REGULAR, DMA(()), DMA(()), DMA(()), DMA(()),
+            pltpu.VMEM((2, 4, SEG, SEG), F32),
+            DMA((4,)), DMA(()), pltpu.SemaphoreType.REGULAR, DMA(()), DMA(()), DMA(()), DMA(()),
         ],
         compiler_params=params(5, 63.9), cost_estimate=COST, name='layer',
     )(w_q, w_k, w_v, w_o, x_tok, gy_tok, gq, gk, gp, cos_tab, sin_tab)

time: 363 us -> 357 us (0.983)
  Pallas kernels: 361 us -> 356 us
    pallas_call x1, Pallas kernels: 354 us -> 348 us  [layer(): pl.pallas_call(layer_kernel, out_shape=[grad] * 4 + [tok] * 2 + [mat] * 4...]
where the time goes in v5:
time: 357 us
  Pallas kernels  356 us (100%)
    pallas_call x1, Pallas kernels, layer(): pl.pallas_call(layer_kernel, out_shape=[grad] * 4 + [tok] * 2 + [mat] * 4...  348 us
    pallas_call x1, Pallas kernels, copy_out(): pl.pallas_call(copy_kernel, out_shape=[SDS(a.shape, a.dtype) for a in arr...  7.37 us

profile of v5, /device:TPU:1, one launch (start us, length us, event | category | flops | bytes accessed | tf_op | source)
XLA Modules:
  0.0 356.6 jit_solution(15140015131958942642)
XLA Ops:
  0.6 348.4 %layer.1 = (f32[128,4096]{1,0:T(8,128)}, f32[128,4096]{1,0:T(8,128)}, f32[128,4096]{1,0:T(8,128)}, f32[128,4096]{1,0:T(8,128)}, bf16[128,4096]{1,0:T(8,128)(2,1)...) custom-call(bf16[128,4096]{1,0:T(8,128)(2,1)} %wq_in.1, ...), custom_call_target="tpu_custom_call" | custom-call | flops 99999997952 | bytes 100000000 | tf_op jit(solution)/shard_map/layer/pallas_call | solution.py:1303
  349.0 7.4 %copy_out.1 = (f32[128,4096]{1,0:T(8,128)}, f32[128,4096]{1,0:T(8,128)}, f32[128,4096]{1,0:T(8,128)}, f32[128,4096]{1,0:T(8,128)}, bf16[128,4096]{1,0:T(8,128)(2...) custom-call(f32[128,4096]{1,0:T(8,128)} %get-tuple-element.25.refs_0_, ...), custom_call_target="tpu_custom_call" | custom-call | flops 99999997952 | bytes 100000000 | tf_op jit(solution)/shard_map/copy_out/pallas_call | solution.py:1359

commit v6 on v5

--- a/solution.py
+++ b/solution.py
@@ -574,13 +574,13 @@
 
     def a_part(s, init=False):
         def step(i):
-            cols = at256(i * SEG)
+            cols = pl.ds(pl.multiple_of(i * 512, 512), 512)
             acc = None
             for k in range(4):
                 dot = jnp.dot(o_full[:, at256(k * 1024 + s * SEG)], w[0, at256(k * 1024 + s * SEG), cols], preferred_element_type=F32)
                 acc = dot if acc is None else acc + dot
             a_acc[:, cols] = acc if init else a_acc[:, cols] + acc
-        loop(0, 4, step)
+        loop(0, 2, step)
 
     a_part(x, True)
     for k in range(4):
@@ -995,7 +995,7 @@
         return pl.ds(pl.multiple_of((lax.rem(e, 2) * 4 + e // 2) * 512, 512), 512)
 
     def wload(e, i):
-        par = lax.rem(e, 2)
+        par = lax.rem(e + 1, 2)
         return pltpu.make_async_copy(weights[i].at[chunk_rows(e)], acts.at[3 * par + i], wls.at[par])
 
     def gx_store(e):
@@ -1007,15 +1007,15 @@
         gsend(0, kk, e // 2).start()
 
     def gx_chunk(e):
-        par = lax.rem(e, 2)
+        par, wpar = lax.rem(e, 2), lax.rem(e + 1, 2)
         ref = acts.at[pl.ds(0, 3)]
-        pltpu.make_async_copy(ref, ref, wls.at[par]).wait()
+        pltpu.make_async_copy(ref, ref, wls.at[wpar]).wait()
 
         def rows_half(r):
             rows = at256(r * SEG)
             acc = None
             for i in range(3):
-                dot = lax.dot_general(dall[i, rows, :], acts[3 * par + i], NT, preferred_element_type=F32)
+                dot = lax.dot_general(dall[i, rows, :], acts[3 * wpar + i], NT, preferred_element_type=F32)
                 acc = dot if acc is None else acc + dot
             gxc[par, rows, :] = acc
         loop(0, 2, rows_half)
@@ -1156,6 +1156,8 @@
         stat.put(i, lanes[i])
     stat.start()
     gain1.start()
+    for i in range(3):
+        wload(0, i).start()
     wo_item(3)
     swap(0).wait_recv()
     loop(0, 4, lambda jj: start_item(0, jj))
@@ -1164,9 +1166,8 @@
     share(1)
     finish(0, 2, total[:, 0:1])
     share(2)
-    for e in range(2):
-        for i in range(3):
-            wload(e, i).start()
+    for i in range(3):
+        wload(1, i).start()
     phase2(WO, 3)
     gy_load.wait()
 

time: 357 us -> 356 us (level)
  no operation moved by 1% of the time
where the time goes in v6:
time: 356 us
  Pallas kernels  355 us (100%)
    pallas_call x1, Pallas kernels, layer(): pl.pallas_call(layer_kernel, out_shape=[grad] * 4 + [tok] * 2 + [mat] * 4...  347 us
    pallas_call x1, Pallas kernels, copy_out(): pl.pallas_call(copy_kernel, out_shape=[SDS(a.shape, a.dtype) for a in arr...  7.37 us

profile of v6, /device:TPU:1, one launch (start us, length us, event | category | flops | bytes accessed | tf_op | source)
XLA Modules:
  0.0 355.6 jit_solution(513792556072832205)
XLA Ops:
  0.6 347.5 %layer.1 = (f32[128,4096]{1,0:T(8,128)}, f32[128,4096]{1,0:T(8,128)}, f32[128,4096]{1,0:T(8,128)}, f32[128,4096]{1,0:T(8,128)}, bf16[128,4096]{1,0:T(8,128)(2,1)...) custom-call(bf16[128,4096]{1,0:T(8,128)(2,1)} %wq_in.1, ...), custom_call_target="tpu_custom_call" | custom-call | flops 99999997952 | bytes 100000000 | tf_op jit(solution)/shard_map/layer/pallas_call | solution.py:1304
  348.1 7.4 %copy_out.1 = (f32[128,4096]{1,0:T(8,128)}, f32[128,4096]{1,0:T(8,128)}, f32[128,4096]{1,0:T(8,128)}, f32[128,4096]{1,0:T(8,128)}, bf16[128,4096]{1,0:T(8,128)(2...) custom-call(f32[128,4096]{1,0:T(8,128)} %get-tuple-element.25.refs_0_, ...), custom_call_target="tpu_custom_call" | custom-call | flops 99999997952 | bytes 100000000 | tf_op jit(solution)/shard_map/copy_out/pallas_call | solution.py:1360
